TPU v7x, 32 devices: a whole 2x2x4 slice. The times are simulated.
32 devices in a mesh: rate: 4 (over y, core), seq: 8 (over z, x).
Axes of the slice: x: 2, y: 2, z: 4, core: 2. Of those that a mesh axis runs over, the one named last changes fastest.
Arguments:
- queries: bfloat16 [8192, 16, 128], P('seq'), may hold values from -6 to 6
- key_rows: bfloat16 [8192, 16, 128], P('seq'), may hold values from -6 to 6
- values: bfloat16 [8192, 16, 128], P('seq'), may hold values from -6 to 6
- attn_out: bfloat16 [8192, 16, 128], P('seq'), may hold values from -6 to 6
- out_grad: bfloat16 [8192, 16, 128], P('seq'), may hold values from -6 to 6
- log_totals: float32 [8192, 16], P('seq'), as said below
- assignment: int32 [16], replicated, may hold values from 0 to 15, as said below
Outputs:
- query_grad: bfloat16 [8192, 16, 128], P('seq', 'rate')
- key_grad: bfloat16 [8192, 16, 128], P('seq', 'rate')
- value_grad: bfloat16 [8192, 16, 128], P('seq', 'rate')
Inputs may be any that keep to these rules, and one draw needn't show every extreme that they name: `assignment`: each of the 16 heads appears once. `log_totals`: at each head's selected positions the natural logarithm of the sum of exp(scores) over the keys b <= a of its segment, computed from queries and key_rows; 0 at other positions.
All inputs are finite; a program needn't handle non-finite values.
Results may differ from a plain program's by a relative error of at most 0.0049.
Values may be sent and summed in bfloat16 or wider, within the bound.
No kernel may reach another device: no remote copies, remote signals or barrier semaphores. Data moves between devices by JAX's collectives and lax.ppermute only.
A program may use at most 128 MiB of HBM per device.

v0:
```python
import jax
import jax.numpy as jnp
from jax import lax
from jax.sharding import PartitionSpec as P

HEADS = 16
SEG = 2048


def passed_along(array, axis, by):
    devices = lax.axis_size(axis)
    return lax.ppermute(array, axis, [(i, (i + by) % devices) for i in range(devices)])


def shortened(array):
    return jax.tree.map(lambda a: a.astype(jnp.bfloat16) if a.dtype == jnp.float32 else a, array)


def pick_rows(source_array, head_index, offset, dilation):
    column = lax.dynamic_index_in_dim(source_array, head_index, 1, keepdims=False)
    split_rows = column.reshape((column.shape[0] // dilation, dilation) + column.shape[1:])
    return lax.dynamic_index_in_dim(split_rows, offset, 1, keepdims=False)


def place_rows(block_grad, offset, dilation):
    lanes = jnp.arange(dilation, dtype=jnp.int32)
    spread = jnp.where((lanes == offset)[None, :, None], block_grad[:, None, :], 0.0)
    return spread.reshape(block_grad.shape[0] * dilation, block_grad.shape[1])


def causal_mask(query_block, key_block, block_rows):
    within = jnp.arange(block_rows, dtype=jnp.int32)
    query_pos = query_block * block_rows + within
    key_pos = key_block * block_rows + within
    return (key_pos[None, :] <= query_pos[:, None])[None]


def block_terms(query_blk, key_blk, value_blk, grad_blk, total_blk, delta_blk, allowed, scaling):
    scores = (
        jnp.einsum("hqd,hkd->hqk", query_blk, key_blk, preferred_element_type=jnp.float32) * scaling
    )
    probs = jnp.where(allowed, jnp.exp(scores - total_blk[:, :, None]), 0.0)
    value_part = jnp.einsum(
        "hqk,hqd->hkd", probs.astype(jnp.bfloat16), grad_blk, preferred_element_type=jnp.float32
    )
    dprobs = jnp.einsum("hqd,hkd->hqk", grad_blk, value_blk, preferred_element_type=jnp.float32)
    dscores = (probs * (dprobs - delta_blk[:, :, None])).astype(jnp.bfloat16)
    query_part = (
        jnp.einsum("hqk,hkd->hqd", dscores, key_blk, preferred_element_type=jnp.float32) * scaling
    )
    key_part = (
        jnp.einsum("hqk,hqd->hkd", dscores, query_blk, preferred_element_type=jnp.float32) * scaling
    )
    return (query_part, key_part, value_part)


def travel_keys(selected, position, span_devices, scaling):
    query_sel, key_sel, value_sel, grad_sel, total_sel, delta_sel = selected
    block_rows = query_sel.shape[1]
    own = block_terms(
        query_sel,
        key_sel,
        value_sel,
        grad_sel,
        total_sel,
        delta_sel,
        causal_mask(position, position, block_rows),
        scaling,
    )

    def turn(step_index, state):
        query_acc, key_blk, value_blk, key_acc, value_acc = state
        key_wide, value_wide, key_acc, value_acc = passed_along(
            (key_blk.astype(jnp.float32), value_blk.astype(jnp.float32), key_acc, value_acc),
            "seq",
            1,
        )
        key_blk = key_wide.astype(jnp.bfloat16)
        value_blk = value_wide.astype(jnp.bfloat16)
        source_block = position - step_index

        def active():
            return block_terms(
                query_sel,
                key_blk,
                value_blk,
                grad_sel,
                total_sel,
                delta_sel,
                causal_mask(position, source_block, block_rows),
                scaling,
            )

        def quiet():
            nothing = jnp.zeros_like(query_acc)
            return (nothing, nothing, nothing)

        parts_now = lax.cond(source_block >= 0, active, quiet)
        return (
            query_acc + parts_now[0],
            key_blk,
            value_blk,
            key_acc + parts_now[1],
            value_acc + parts_now[2],
        )

    state = lax.fori_loop(1, span_devices, turn, (own[0], key_sel, value_sel, own[1], own[2]))
    key_acc, value_acc = (state[3], state[4])
    key_acc, value_acc = passed_along((key_acc, value_acc), "seq", 1 - span_devices)
    return (state[0], key_acc, value_acc)


def run_group(
    sources, head_list, offset_list, dilation, all_tokens, local_tokens, seq_index, scaling
):
    seg_rows = min(SEG, all_tokens // dilation)
    span_devices = seg_rows * dilation // local_tokens
    position = seq_index % span_devices
    selected = tuple(
        (
            jnp.stack(
                [
                    pick_rows(source_array, head_index, offset, dilation)
                    for head_index, offset in zip(head_list, offset_list)
                ]
            )
            for source_array in sources
        )
    )
    results = travel_keys(selected, position, span_devices, scaling)
    return tuple(
        (
            jnp.stack([place_rows(results[which_grad][0], offset_list[0], dilation)])
            for which_grad in range(3)
        )
    )


def body(queries, key_rows, values, attn_out, out_grad, log_totals, assignment):
    local_tokens = queries.shape[0]
    scaling = queries.shape[2] ** (-0.5)
    rate_count = lax.axis_size("rate")
    seq_count = lax.axis_size("seq")
    rate_index = lax.axis_index("rate")
    seq_index = lax.axis_index("seq")
    group_size = HEADS // 4
    all_tokens = local_tokens * seq_count
    delta_rows = jnp.einsum("thd,thd->th", out_grad, attn_out, preferred_element_type=jnp.float32)
    sources = (queries, key_rows, values, out_grad, log_totals, delta_rows)
    per_device = group_size // rate_count
    grads = [jnp.zeros(queries.shape, jnp.float32) for which_grad in range(3)]
    for rate_level in range(4):
        dilation = 2**rate_level
        member = 0
        lane_index = rate_index * per_device + member
        head_list = [assignment[rate_level * group_size + lane_index]]
        offset_list = [lane_index % dilation]
        placed = run_group(
            sources, head_list, offset_list, dilation, all_tokens, local_tokens, seq_index, scaling
        )
        for which_grad in range(3):
            member = 0
            grads[which_grad] = lax.dynamic_update_index_in_dim(
                grads[which_grad], placed[which_grad][member], head_list[member], 1
            )
    lowered = tuple((grads[which_grad].astype(jnp.bfloat16) for which_grad in range(3)))
    summed = jax.tree.map(
        lambda part: part.astype(jnp.float32),
        lax.psum_scatter(shortened(lowered), "rate", scatter_dimension=1, tiled=True),
    )
    return (
        summed[0].astype(jnp.bfloat16),
        summed[1].astype(jnp.bfloat16),
        summed[2].astype(jnp.bfloat16),
    )


def solution(mesh):
    placed = (
        P("seq", None, None),
        P("seq", None, None),
        P("seq", None, None),
        P("seq", None, None),
        P("seq", None, None),
        P("seq", None),
        P(),
    )
    return jax.shard_map(
        body,
        mesh=mesh,
        in_specs=placed,
        out_specs=(P("seq", "rate", None), P("seq", "rate", None), P("seq", "rate", None)),
        check_vma=False,
    )
```

profile of v0, /device:TPU:0, one launch (start us, length us, event | category | flops | bytes accessed | tf_op | source)
XLA Modules:
  0.0 536.7 jit_solution(12810043978344858049)
XLA Ops:
  16.5 8.9 %constant_dynamic-slice_fusion.6 = (bf16[1024,1,128]{2,1,0:T(2,128)(2,1)}, bf16[1024,1,128]{2,1,0:T(2,128)(2,1)}, bf16[1024,1,128]{2,1,0:T(2,128)(2,1)S(1)}, bf1...) fusion(bf16[1024,16,128]{2,1,0:T(8,128)(2,1)} %param.22, ...), kind=kLoop, calls=%fused_computation.207 | loop fusion | bytes 4194320 | tf_op jit(solution)/shard_map/jit(dynamic_index_in_dim)/dynamic_slice | solution.py:20
  26.1 3.0 collective-permute-start.12
  30.4 5.7 %fusion.63 = f32[1024,16]{1,0:T(8,128)S(1)} fusion(bf16[1024,16,128]{2,1,0:T(8,128)(2,1)} %param.25, bf16[1024,16,128]{2,1,0:T(8,128)(2,1)} %param.24), kind=kLoop, calls=%fused_computation.88 | loop fusion | flops 8372224 | bytes 8454144
  37.6 2.0 fusion.134
  39.8 9.2 %constant_dynamic-slice_fusion.1 = (bf16[1024,1,128]{2,1,0:T(2,128)(2,1)S(1)}, bf16[1024,1,128]{2,1,0:T(2,128)(2,1)}, bf16[1024,1,128]{2,1,0:T(2,128)(2,1)}, bf1...) fusion(bf16[1024,16,128]{2,1,0:T(8,128)(2,1)} %param.23, ...), kind=kLoop, calls=%fused_computation.202 | loop fusion | bytes 4194320 | tf_op jit(solution)/shard_map/jit(dynamic_index_in_dim)/dynamic_slice | solution.py:20
  80.3 81.5 %while.74 = (s32[]{:T(128)}, f32[1,128,128]{2,1,0:T(8,128)S(1)}, bf16[1,128,128]{2,1,0:T(8,128)(2,1)}, bf16[1,128,128]{2,1,0:T(8,128)(2,1)}, f32[1,128,128]{2,1,...) while((s32[]{:T(128)}, f32[1,128,128]{2,1,0:T(8,128)S(1)}, ...), condition=%wide.region_13.14_spmd, body=%wide.region_10.13_spmd.sunk | while | flops 21184776 | bytes 2231727 | solution.py:107
  86.4 3.8 collective-permute-done.8
  93.4 2.4 collective-permute-start.11
  97.7 5.0 collective-permute-done.8
  109.1 3.8 collective-permute-done.8
  119.2 2.4 collective-permute-start.9
  121.6 2.6 collective-permute-done.8
  129.3 2.7 collective-permute-start.9
  132.0 4.4 collective-permute-done.8
  142.1 6.2 %collective-permute-done.8 = bf16[1,128,128]{2,1,0:T(8,128)(2,1)S(1)} collective-permute-done((bf16[1,128,128]{2,1,0:T(8,128)(2,1)}, bf16[1,128,128]{2,1,0:T(8,128)(2,1)S(1)}, u32[]{:S(2)}, u32[]{:S(2)}) %collective-permute-start.8) | collective-permute-done | bytes 32800 | tf_op jit(solution)/shard_map/while/body/eval_jaxpr/ppermute | solution.py:12
  154.0 5.8 %collective-permute-done.8 = bf16[1,128,128]{2,1,0:T(8,128)(2,1)S(1)} collective-permute-done((bf16[1,128,128]{2,1,0:T(8,128)(2,1)}, bf16[1,128,128]{2,1,0:T(8,128)(2,1)S(1)}, u32[]{:S(2)}, u32[]{:S(2)}) %collective-permute-start.8) | collective-permute-done | bytes 32800 | tf_op jit(solution)/shard_map/while/body/eval_jaxpr/ppermute | solution.py:12
  162.5 83.7 %while.73 = (s32[]{:T(128)}, f32[1,256,128]{2,1,0:T(8,128)S(1)}, bf16[1,256,128]{2,1,0:T(8,128)(2,1)S(1)}, bf16[1,256,128]{2,1,0:T(8,128)(2,1)S(1)}, f32[1,256,1...) while((s32[]{:T(128)}, f32[1,256,128]{2,1,0:T(8,128)S(1)}, ...), condition=%wide.region_9.10_spmd, body=%wide.region_6.9_spmd.sunk | while | flops 84574720 | bytes 5052847 | solution.py:107
  165.5 9.6 %collective-permute-done.4 = bf16[1,256,128]{2,1,0:T(8,128)(2,1)S(1)} collective-permute-done((bf16[1,256,128]{2,1,0:T(8,128)(2,1)S(1)}, bf16[1,256,128]{2,1,0:T(8,128)(2,1)S(1)}, u32[]{:S(2)}, u32[]{:S(2)}) %collective-permute-start.4) | collective-permute-done | bytes 65568 | tf_op jit(solution)/shard_map/while/body/eval_jaxpr/ppermute | solution.py:12
  177.1 10.7 %collective-permute-done.4 = bf16[1,256,128]{2,1,0:T(8,128)(2,1)S(1)} collective-permute-done((bf16[1,256,128]{2,1,0:T(8,128)(2,1)S(1)}, bf16[1,256,128]{2,1,0:T(8,128)(2,1)S(1)}, u32[]{:S(2)}, u32[]{:S(2)}) %collective-permute-start.4) | collective-permute-done | bytes 65568 | tf_op jit(solution)/shard_map/while/body/eval_jaxpr/ppermute | solution.py:12
  190.1 9.7 %collective-permute-done.4 = bf16[1,256,128]{2,1,0:T(8,128)(2,1)S(1)} collective-permute-done((bf16[1,256,128]{2,1,0:T(8,128)(2,1)S(1)}, bf16[1,256,128]{2,1,0:T(8,128)(2,1)S(1)}, u32[]{:S(2)}, u32[]{:S(2)}) %collective-permute-start.4) | collective-permute-done | bytes 65568 | tf_op jit(solution)/shard_map/while/body/eval_jaxpr/ppermute | solution.py:12
  202.8 8.0 %collective-permute-done.4 = bf16[1,256,128]{2,1,0:T(8,128)(2,1)S(1)} collective-permute-done((bf16[1,256,128]{2,1,0:T(8,128)(2,1)S(1)}, bf16[1,256,128]{2,1,0:T(8,128)(2,1)S(1)}, u32[]{:S(2)}, u32[]{:S(2)}) %collective-permute-start.4) | collective-permute-done | bytes 65568 | tf_op jit(solution)/shard_map/while/body/eval_jaxpr/ppermute | solution.py:12
  211.9 2.8 collective-permute-start.5
  214.7 6.8 %collective-permute-done.4 = bf16[1,256,128]{2,1,0:T(8,128)(2,1)S(1)} collective-permute-done((bf16[1,256,128]{2,1,0:T(8,128)(2,1)S(1)}, bf16[1,256,128]{2,1,0:T(8,128)(2,1)S(1)}, u32[]{:S(2)}, u32[]{:S(2)}) %collective-permute-start.4) | collective-permute-done | bytes 65568 | tf_op jit(solution)/shard_map/while/body/eval_jaxpr/ppermute | solution.py:12
  224.9 7.5 %collective-permute-done.4 = bf16[1,256,128]{2,1,0:T(8,128)(2,1)S(1)} collective-permute-done((bf16[1,256,128]{2,1,0:T(8,128)(2,1)S(1)}, bf16[1,256,128]{2,1,0:T(8,128)(2,1)S(1)}, u32[]{:S(2)}, u32[]{:S(2)}) %collective-permute-start.4) | collective-permute-done | bytes 65568 | tf_op jit(solution)/shard_map/while/body/eval_jaxpr/ppermute | solution.py:12
  236.5 8.7 %collective-permute-done.4 = bf16[1,256,128]{2,1,0:T(8,128)(2,1)S(1)} collective-permute-done((bf16[1,256,128]{2,1,0:T(8,128)(2,1)S(1)}, bf16[1,256,128]{2,1,0:T(8,128)(2,1)S(1)}, u32[]{:S(2)}, u32[]{:S(2)}) %collective-permute-start.4) | collective-permute-done | bytes 65568 | tf_op jit(solution)/shard_map/while/body/eval_jaxpr/ppermute | solution.py:12
  246.8 72.0 %while.72 = (s32[]{:T(128)}, f32[1,512,128]{2,1,0:T(8,128)S(1)}, bf16[1,512,128]{2,1,0:T(8,128)(2,1)}, bf16[1,512,128]{2,1,0:T(8,128)(2,1)}, f32[1,512,128]{2,1,...) while((s32[]{:T(128)}, f32[1,512,128]{2,1,0:T(8,128)S(1)}, ...), condition=%wide.region_5.6_spmd, body=%wide.region_2.5_spmd.sunk | while | flops 337970176 | bytes 12464559 | solution.py:107
  247.1 2.1 collective-permute-start.1
  249.1 18.2 %collective-permute-done = bf16[1,512,128]{2,1,0:T(8,128)(2,1)S(1)} collective-permute-done((bf16[1,512,128]{2,1,0:T(8,128)(2,1)}, bf16[1,512,128]{2,1,0:T(8,128)(2,1)S(1)}, u32[]{:S(2)}, u32[]{:S(2)}) %collective-permute-start) | collective-permute-done | bytes 131104 | tf_op jit(solution)/shard_map/while/body/eval_jaxpr/ppermute | solution.py:12
  267.3 2.0 collective-permute-done.1
  273.6 19.1 %collective-permute-done = bf16[1,512,128]{2,1,0:T(8,128)(2,1)S(1)} collective-permute-done((bf16[1,512,128]{2,1,0:T(8,128)(2,1)}, bf16[1,512,128]{2,1,0:T(8,128)(2,1)S(1)}, u32[]{:S(2)}, u32[]{:S(2)}) %collective-permute-start) | collective-permute-done | bytes 131104 | tf_op jit(solution)/shard_map/while/body/eval_jaxpr/ppermute | solution.py:12
  297.2 15.7 %collective-permute-done = bf16[1,512,128]{2,1,0:T(8,128)(2,1)S(1)} collective-permute-done((bf16[1,512,128]{2,1,0:T(8,128)(2,1)}, bf16[1,512,128]{2,1,0:T(8,128)(2,1)S(1)}, u32[]{:S(2)}, u32[]{:S(2)}) %collective-permute-start) | collective-permute-done | bytes 131104 | tf_op jit(solution)/shard_map/while/body/eval_jaxpr/ppermute | solution.py:12
  313.0 2.8 collective-permute-done.1
  318.9 2.7 fusion.101
  321.9 3.2 multiply_convert_fusion.1
  328.2 2.2 fusion.72
  336.0 2.3 fusion.76
  340.4 15.2 %collective-permute-start.15 = (bf16[1,1024,128]{2,1,0:T(8,128)(2,1)S(1)}, bf16[1,1024,128]{2,1,0:T(8,128)(2,1)S(1)}, u32[]{:S(2)}, u32[]{:S(2)}) collective-permute-start(bf16[1,1024,128]{2,1,0:T(8,128)(2,1)S(1)} %add.436), channel_id=1, source_target_pairs={{0,7},{1,0},{2,1},{3,2},{4,3},{5,4},{6,5},{7,6},{8,15},{9,8},{10,9... | collective-permute-start | bytes 786440 | tf_op jit(solution)/shard_map/ppermute | solution.py:12
  356.0 2.8 broadcast.444.clone.2
  361.5 4.8 collective-permute-start.16
  366.4 2.8 broadcast.444.clone.1
  370.4 2.8 broadcast.444.clone
  373.9 3.8 collective-permute-start.22
  386.6 46.4 %reduce-scatter.4.cloned.1.call-done = bf16[1024,4,128]{2,0,1:T(8,128)(2,1)} async-done(((bf16[1024,16,128]{2,0,1:T(8,128)(2,1)}), bf16[1024,4,128]{2,0,1:T(8,128)(2,1)}) %reduce-scatter.4.cloned.1.call-update) | async-done | bytes 1048592 | tf_op jit(solution)/shard_map/reduce_scatter | solution.py:169
  432.9 3.0 copy.69
  435.9 44.1 %reduce-scatter.6.cloned.1.call-done = bf16[1024,4,128]{2,0,1:T(8,128)(2,1)} async-done(((bf16[1024,16,128]{2,0,1:T(8,128)(2,1)}), bf16[1024,4,128]{2,0,1:T(8,128)(2,1)}) %reduce-scatter.6.cloned.1.call-update) | async-done | bytes 1048592 | tf_op jit(solution)/shard_map/reduce_scatter | solution.py:169
  480.1 3.0 copy.70
  483.1 44.1 %reduce-scatter.8.cloned.1.call-done = bf16[1024,4,128]{2,0,1:T(8,128)(2,1)} async-done(((bf16[1024,16,128]{2,0,1:T(8,128)(2,1)}), bf16[1024,4,128]{2,0,1:T(8,128)(2,1)}) %reduce-scatter.8.cloned.1.call-update) | async-done | bytes 1048592 | tf_op jit(solution)/shard_map/reduce_scatter | solution.py:169
  527.2 3.0 copy.71
  (442 shorter events, 135.9 us)
Async XLA Ops:
  7.2 425.8 %reduce-scatter.4.cloned.1.call-start = ((), (), s32[]{:S(2)}) async-start(), calls=%async_computation.3 | async-start | bytes 5242880 | tf_op jit(solution)/shard_map/reduce_scatter | solution.py:169
  26.1 312.2 %collective-permute-start.12 = (bf16[1,1024,128]{2,1,0:T(8,128)(2,1)}, bf16[1,1024,128]{2,1,0:T(8,128)(2,1)}, u32[]{:S(2)}, u32[]{:S(2)}) collective-permute-start(bf16[1,1024,128]{2,1,0:T(8,128)(2,1)} %bitcast.298), channel_id=1, source_target_pairs={{0,1},{1,2},{2,3},{3,4},{4,5},{5,6},{6,7},{7,0},{8,9},{9,10},{10,1... | collective-permute-start | bytes 786440 | tf_op jit(solution)/shard_map/while/body/eval_jaxpr/ppermute | solution.py:12
  80.3 12.7 %collective-permute-start.10 = (f32[1,128,128]{2,1,0:T(8,128)S(1)}, f32[1,128,128]{2,1,0:T(8,128)S(1)}, u32[]{:S(2)}, u32[]{:S(2)}) collective-permute-start(f32[1,128,128]{2,1,0:T(8,128)S(1)} %get-tuple-element.1185), channel_id=1, source_target_pairs={{0,1},{1,2},{2,3},{3,4},{4,5},{5,6},{6,7},{7,0},{8,9},{9,10},{10,1... | collective-permute-start | bytes 196616 | tf_op jit(solution)/shard_map/while/body/eval_jaxpr/ppermute | solution.py:12
  81.9 11.2 %collective-permute-start.11 = (f32[1,128,128]{2,1,0:T(8,128)S(1)}, f32[1,128,128]{2,1,0:T(8,128)S(1)}, u32[]{:S(2)}, u32[]{:S(2)}) collective-permute-start(f32[1,128,128]{2,1,0:T(8,128)S(1)} %get-tuple-element.1186), channel_id=1, source_target_pairs={{0,1},{1,2},{2,3},{3,4},{4,5},{5,6},{6,7},{7,0},{8,9},{9,10},{10,1... | collective-permute-start | bytes 196616 | tf_op jit(solution)/shard_map/while/body/eval_jaxpr/ppermute | solution.py:12
  93.1 11.5 %collective-permute-start.10 = (f32[1,128,128]{2,1,0:T(8,128)S(1)}, f32[1,128,128]{2,1,0:T(8,128)S(1)}, u32[]{:S(2)}, u32[]{:S(2)}) collective-permute-start(f32[1,128,128]{2,1,0:T(8,128)S(1)} %get-tuple-element.1185), channel_id=1, source_target_pairs={{0,1},{1,2},{2,3},{3,4},{4,5},{5,6},{6,7},{7,0},{8,9},{9,10},{10,1... | collective-permute-start | bytes 196616 | tf_op jit(solution)/shard_map/while/body/eval_jaxpr/ppermute | solution.py:12
  93.4 11.2 %collective-permute-start.11 = (f32[1,128,128]{2,1,0:T(8,128)S(1)}, f32[1,128,128]{2,1,0:T(8,128)S(1)}, u32[]{:S(2)}, u32[]{:S(2)}) collective-permute-start(f32[1,128,128]{2,1,0:T(8,128)S(1)} %get-tuple-element.1186), channel_id=1, source_target_pairs={{0,1},{1,2},{2,3},{3,4},{4,5},{5,6},{6,7},{7,0},{8,9},{9,10},{10,1... | collective-permute-start | bytes 196616 | tf_op jit(solution)/shard_map/while/body/eval_jaxpr/ppermute | solution.py:12
  115.8 11.5 %collective-permute-start.10 = (f32[1,128,128]{2,1,0:T(8,128)S(1)}, f32[1,128,128]{2,1,0:T(8,128)S(1)}, u32[]{:S(2)}, u32[]{:S(2)}) collective-permute-start(f32[1,128,128]{2,1,0:T(8,128)S(1)} %get-tuple-element.1185), channel_id=1, source_target_pairs={{0,1},{1,2},{2,3},{3,4},{4,5},{5,6},{6,7},{7,0},{8,9},{9,10},{10,1... | collective-permute-start | bytes 196616 | tf_op jit(solution)/shard_map/while/body/eval_jaxpr/ppermute | solution.py:12
  115.8 11.5 %collective-permute-start.11 = (f32[1,128,128]{2,1,0:T(8,128)S(1)}, f32[1,128,128]{2,1,0:T(8,128)S(1)}, u32[]{:S(2)}, u32[]{:S(2)}) collective-permute-start(f32[1,128,128]{2,1,0:T(8,128)S(1)} %get-tuple-element.1186), channel_id=1, source_target_pairs={{0,1},{1,2},{2,3},{3,4},{4,5},{5,6},{6,7},{7,0},{8,9},{9,10},{10,1... | collective-permute-start | bytes 196616 | tf_op jit(solution)/shard_map/while/body/eval_jaxpr/ppermute | solution.py:12
  138.5 11.5 %collective-permute-start.10 = (f32[1,128,128]{2,1,0:T(8,128)S(1)}, f32[1,128,128]{2,1,0:T(8,128)S(1)}, u32[]{:S(2)}, u32[]{:S(2)}) collective-permute-start(f32[1,128,128]{2,1,0:T(8,128)S(1)} %get-tuple-element.1185), channel_id=1, source_target_pairs={{0,1},{1,2},{2,3},{3,4},{4,5},{5,6},{6,7},{7,0},{8,9},{9,10},{10,1... | collective-permute-start | bytes 196616 | tf_op jit(solution)/shard_map/while/body/eval_jaxpr/ppermute | solution.py:12
  138.5 11.4 %collective-permute-start.11 = (f32[1,128,128]{2,1,0:T(8,128)S(1)}, f32[1,128,128]{2,1,0:T(8,128)S(1)}, u32[]{:S(2)}, u32[]{:S(2)}) collective-permute-start(f32[1,128,128]{2,1,0:T(8,128)S(1)} %get-tuple-element.1186), channel_id=1, source_target_pairs={{0,1},{1,2},{2,3},{3,4},{4,5},{5,6},{6,7},{7,0},{8,9},{9,10},{10,1... | collective-permute-start | bytes 196616 | tf_op jit(solution)/shard_map/while/body/eval_jaxpr/ppermute | solution.py:12
  150.0 11.8 %collective-permute-start.10 = (f32[1,128,128]{2,1,0:T(8,128)S(1)}, f32[1,128,128]{2,1,0:T(8,128)S(1)}, u32[]{:S(2)}, u32[]{:S(2)}) collective-permute-start(f32[1,128,128]{2,1,0:T(8,128)S(1)} %get-tuple-element.1185), channel_id=1, source_target_pairs={{0,1},{1,2},{2,3},{3,4},{4,5},{5,6},{6,7},{7,0},{8,9},{9,10},{10,1... | collective-permute-start | bytes 196616 | tf_op jit(solution)/shard_map/while/body/eval_jaxpr/ppermute | solution.py:12
  150.0 11.8 %collective-permute-start.11 = (f32[1,128,128]{2,1,0:T(8,128)S(1)}, f32[1,128,128]{2,1,0:T(8,128)S(1)}, u32[]{:S(2)}, u32[]{:S(2)}) collective-permute-start(f32[1,128,128]{2,1,0:T(8,128)S(1)} %get-tuple-element.1186), channel_id=1, source_target_pairs={{0,1},{1,2},{2,3},{3,4},{4,5},{5,6},{6,7},{7,0},{8,9},{9,10},{10,1... | collective-permute-start | bytes 196616 | tf_op jit(solution)/shard_map/while/body/eval_jaxpr/ppermute | solution.py:12
  162.5 13.5 %collective-permute-start.6 = (f32[1,256,128]{2,1,0:T(8,128)S(1)}, f32[1,256,128]{2,1,0:T(8,128)S(1)}, u32[]{:S(2)}, u32[]{:S(2)}) collective-permute-start(f32[1,256,128]{2,1,0:T(8,128)S(1)} %get-tuple-element.1146), channel_id=1, source_target_pairs={{0,1},{1,2},{2,3},{3,4},{4,5},{5,6},{6,7},{7,0},{8,9},{9,10},{10,1... | collective-permute-start | bytes 393224 | tf_op jit(solution)/shard_map/while/body/eval_jaxpr/ppermute | solution.py:12
  162.5 13.5 %collective-permute-start.7 = (f32[1,256,128]{2,1,0:T(8,128)S(1)}, f32[1,256,128]{2,1,0:T(8,128)S(1)}, u32[]{:S(2)}, u32[]{:S(2)}) collective-permute-start(f32[1,256,128]{2,1,0:T(8,128)S(1)} %get-tuple-element.1147), channel_id=1, source_target_pairs={{0,1},{1,2},{2,3},{3,4},{4,5},{5,6},{6,7},{7,0},{8,9},{9,10},{10,1... | collective-permute-start | bytes 393224 | tf_op jit(solution)/shard_map/while/body/eval_jaxpr/ppermute | solution.py:12
  162.5 12.6 %collective-permute-start.4 = (bf16[1,256,128]{2,1,0:T(8,128)(2,1)S(1)}, bf16[1,256,128]{2,1,0:T(8,128)(2,1)S(1)}, u32[]{:S(2)}, u32[]{:S(2)}) collective-permute-start(bf16[1,256,128]{2,1,0:T(8,128)(2,1)S(1)} %get-tuple-element.1144), channel_id=1, source_target_pairs={{0,1},{1,2},{2,3},{3,4},{4,5},{5,6},{6,7},{7,0},{8,9},{9,10},{10,1... | collective-permute-start | bytes 196616 | tf_op jit(solution)/shard_map/while/body/eval_jaxpr/ppermute | solution.py:12
  164.3 11.5 %collective-permute-start.5 = (bf16[1,256,128]{2,1,0:T(8,128)(2,1)S(1)}, bf16[1,256,128]{2,1,0:T(8,128)(2,1)S(1)}, u32[]{:S(2)}, u32[]{:S(2)}) collective-permute-start(bf16[1,256,128]{2,1,0:T(8,128)(2,1)S(1)} %get-tuple-element.1145), channel_id=1, source_target_pairs={{0,1},{1,2},{2,3},{3,4},{4,5},{5,6},{6,7},{7,0},{8,9},{9,10},{10,1... | collective-permute-start | bytes 196616 | tf_op jit(solution)/shard_map/while/body/eval_jaxpr/ppermute | solution.py:12
  176.0 12.7 %collective-permute-start.6 = (f32[1,256,128]{2,1,0:T(8,128)S(1)}, f32[1,256,128]{2,1,0:T(8,128)S(1)}, u32[]{:S(2)}, u32[]{:S(2)}) collective-permute-start(f32[1,256,128]{2,1,0:T(8,128)S(1)} %get-tuple-element.1146), channel_id=1, source_target_pairs={{0,1},{1,2},{2,3},{3,4},{4,5},{5,6},{6,7},{7,0},{8,9},{9,10},{10,1... | collective-permute-start | bytes 393224 | tf_op jit(solution)/shard_map/while/body/eval_jaxpr/ppermute | solution.py:12
  176.1 12.6 %collective-permute-start.7 = (f32[1,256,128]{2,1,0:T(8,128)S(1)}, f32[1,256,128]{2,1,0:T(8,128)S(1)}, u32[]{:S(2)}, u32[]{:S(2)}) collective-permute-start(f32[1,256,128]{2,1,0:T(8,128)S(1)} %get-tuple-element.1147), channel_id=1, source_target_pairs={{0,1},{1,2},{2,3},{3,4},{4,5},{5,6},{6,7},{7,0},{8,9},{9,10},{10,1... | collective-permute-start | bytes 393224 | tf_op jit(solution)/shard_map/while/body/eval_jaxpr/ppermute | solution.py:12
  176.2 11.7 %collective-permute-start.4 = (bf16[1,256,128]{2,1,0:T(8,128)(2,1)S(1)}, bf16[1,256,128]{2,1,0:T(8,128)(2,1)S(1)}, u32[]{:S(2)}, u32[]{:S(2)}) collective-permute-start(bf16[1,256,128]{2,1,0:T(8,128)(2,1)S(1)} %get-tuple-element.1144), channel_id=1, source_target_pairs={{0,1},{1,2},{2,3},{3,4},{4,5},{5,6},{6,7},{7,0},{8,9},{9,10},{10,1... | collective-permute-start | bytes 196616 | tf_op jit(solution)/shard_map/while/body/eval_jaxpr/ppermute | solution.py:12
  176.2 12.3 %collective-permute-start.5 = (bf16[1,256,128]{2,1,0:T(8,128)(2,1)S(1)}, bf16[1,256,128]{2,1,0:T(8,128)(2,1)S(1)}, u32[]{:S(2)}, u32[]{:S(2)}) collective-permute-start(bf16[1,256,128]{2,1,0:T(8,128)(2,1)S(1)} %get-tuple-element.1145), channel_id=1, source_target_pairs={{0,1},{1,2},{2,3},{3,4},{4,5},{5,6},{6,7},{7,0},{8,9},{9,10},{10,1... | collective-permute-start | bytes 196616 | tf_op jit(solution)/shard_map/while/body/eval_jaxpr/ppermute | solution.py:12
  188.8 11.8 %collective-permute-start.6 = (f32[1,256,128]{2,1,0:T(8,128)S(1)}, f32[1,256,128]{2,1,0:T(8,128)S(1)}, u32[]{:S(2)}, u32[]{:S(2)}) collective-permute-start(f32[1,256,128]{2,1,0:T(8,128)S(1)} %get-tuple-element.1146), channel_id=1, source_target_pairs={{0,1},{1,2},{2,3},{3,4},{4,5},{5,6},{6,7},{7,0},{8,9},{9,10},{10,1... | collective-permute-start | bytes 393224 | tf_op jit(solution)/shard_map/while/body/eval_jaxpr/ppermute | solution.py:12
  188.8 11.8 %collective-permute-start.7 = (f32[1,256,128]{2,1,0:T(8,128)S(1)}, f32[1,256,128]{2,1,0:T(8,128)S(1)}, u32[]{:S(2)}, u32[]{:S(2)}) collective-permute-start(f32[1,256,128]{2,1,0:T(8,128)S(1)} %get-tuple-element.1147), channel_id=1, source_target_pairs={{0,1},{1,2},{2,3},{3,4},{4,5},{5,6},{6,7},{7,0},{8,9},{9,10},{10,1... | collective-permute-start | bytes 393224 | tf_op jit(solution)/shard_map/while/body/eval_jaxpr/ppermute | solution.py:12
  189.0 11.5 %collective-permute-start.5 = (bf16[1,256,128]{2,1,0:T(8,128)(2,1)S(1)}, bf16[1,256,128]{2,1,0:T(8,128)(2,1)S(1)}, u32[]{:S(2)}, u32[]{:S(2)}) collective-permute-start(bf16[1,256,128]{2,1,0:T(8,128)(2,1)S(1)} %get-tuple-element.1145), channel_id=1, source_target_pairs={{0,1},{1,2},{2,3},{3,4},{4,5},{5,6},{6,7},{7,0},{8,9},{9,10},{10,1... | collective-permute-start | bytes 196616 | tf_op jit(solution)/shard_map/while/body/eval_jaxpr/ppermute | solution.py:12
  233.2 12.8 %collective-permute-start.6 = (f32[1,256,128]{2,1,0:T(8,128)S(1)}, f32[1,256,128]{2,1,0:T(8,128)S(1)}, u32[]{:S(2)}, u32[]{:S(2)}) collective-permute-start(f32[1,256,128]{2,1,0:T(8,128)S(1)} %get-tuple-element.1146), channel_id=1, source_target_pairs={{0,1},{1,2},{2,3},{3,4},{4,5},{5,6},{6,7},{7,0},{8,9},{9,10},{10,1... | collective-permute-start | bytes 393224 | tf_op jit(solution)/shard_map/while/body/eval_jaxpr/ppermute | solution.py:12
  233.3 12.8 %collective-permute-start.7 = (f32[1,256,128]{2,1,0:T(8,128)S(1)}, f32[1,256,128]{2,1,0:T(8,128)S(1)}, u32[]{:S(2)}, u32[]{:S(2)}) collective-permute-start(f32[1,256,128]{2,1,0:T(8,128)S(1)} %get-tuple-element.1147), channel_id=1, source_target_pairs={{0,1},{1,2},{2,3},{3,4},{4,5},{5,6},{6,7},{7,0},{8,9},{9,10},{10,1... | collective-permute-start | bytes 393224 | tf_op jit(solution)/shard_map/while/body/eval_jaxpr/ppermute | solution.py:12
  246.8 24.0 %collective-permute-start.2 = (f32[1,512,128]{2,1,0:T(8,128)}, f32[1,512,128]{2,1,0:T(8,128)S(1)}, u32[]{:S(2)}, u32[]{:S(2)}) collective-permute-start(f32[1,512,128]{2,1,0:T(8,128)} %get-tuple-element.1107), channel_id=1, source_target_pairs={{0,1},{1,2},{2,3},{3,4},{4,5},{5,6},{6,7},{7,0},{8,9},{9,10},{10,1... | collective-permute-start | bytes 786440 | tf_op jit(solution)/shard_map/while/body/eval_jaxpr/ppermute | solution.py:12
  246.8 24.8 %collective-permute-start.3 = (f32[1,512,128]{2,1,0:T(8,128)}, f32[1,512,128]{2,1,0:T(8,128)S(1)}, u32[]{:S(2)}, u32[]{:S(2)}) collective-permute-start(f32[1,512,128]{2,1,0:T(8,128)} %get-tuple-element.1108), channel_id=1, source_target_pairs={{0,1},{1,2},{2,3},{3,4},{4,5},{5,6},{6,7},{7,0},{8,9},{9,10},{10,1... | collective-permute-start | bytes 786440 | tf_op jit(solution)/shard_map/while/body/eval_jaxpr/ppermute | solution.py:12
  246.8 20.5 %collective-permute-start = (bf16[1,512,128]{2,1,0:T(8,128)(2,1)}, bf16[1,512,128]{2,1,0:T(8,128)(2,1)S(1)}, u32[]{:S(2)}, u32[]{:S(2)}) collective-permute-start(bf16[1,512,128]{2,1,0:T(8,128)(2,1)} %get-tuple-element.1105), channel_id=1, source_target_pairs={{0,1},{1,2},{2,3},{3,4},{4,5},{5,6},{6,7},{7,0},{8,9},{9,10},{10,1... | collective-permute-start | bytes 393224 | tf_op jit(solution)/shard_map/while/body/eval_jaxpr/ppermute | solution.py:12
  247.1 22.3 %collective-permute-start.1 = (bf16[1,512,128]{2,1,0:T(8,128)(2,1)}, bf16[1,512,128]{2,1,0:T(8,128)(2,1)S(1)}, u32[]{:S(2)}, u32[]{:S(2)}) collective-permute-start(bf16[1,512,128]{2,1,0:T(8,128)(2,1)} %get-tuple-element.1106), channel_id=1, source_target_pairs={{0,1},{1,2},{2,3},{3,4},{4,5},{5,6},{6,7},{7,0},{8,9},{9,10},{10,1... | collective-permute-start | bytes 393224 | tf_op jit(solution)/shard_map/while/body/eval_jaxpr/ppermute | solution.py:12
  272.4 23.2 %collective-permute-start.2 = (f32[1,512,128]{2,1,0:T(8,128)}, f32[1,512,128]{2,1,0:T(8,128)S(1)}, u32[]{:S(2)}, u32[]{:S(2)}) collective-permute-start(f32[1,512,128]{2,1,0:T(8,128)} %get-tuple-element.1107), channel_id=1, source_target_pairs={{0,1},{1,2},{2,3},{3,4},{4,5},{5,6},{6,7},{7,0},{8,9},{9,10},{10,1... | collective-permute-start | bytes 786440 | tf_op jit(solution)/shard_map/while/body/eval_jaxpr/ppermute | solution.py:12
  272.4 23.9 %collective-permute-start.3 = (f32[1,512,128]{2,1,0:T(8,128)}, f32[1,512,128]{2,1,0:T(8,128)S(1)}, u32[]{:S(2)}, u32[]{:S(2)}) collective-permute-start(f32[1,512,128]{2,1,0:T(8,128)} %get-tuple-element.1108), channel_id=1, source_target_pairs={{0,1},{1,2},{2,3},{3,4},{4,5},{5,6},{6,7},{7,0},{8,9},{9,10},{10,1... | collective-permute-start | bytes 786440 | tf_op jit(solution)/shard_map/while/body/eval_jaxpr/ppermute | solution.py:12
  272.4 20.3 %collective-permute-start = (bf16[1,512,128]{2,1,0:T(8,128)(2,1)}, bf16[1,512,128]{2,1,0:T(8,128)(2,1)S(1)}, u32[]{:S(2)}, u32[]{:S(2)}) collective-permute-start(bf16[1,512,128]{2,1,0:T(8,128)(2,1)} %get-tuple-element.1105), channel_id=1, source_target_pairs={{0,1},{1,2},{2,3},{3,4},{4,5},{5,6},{6,7},{7,0},{8,9},{9,10},{10,1... | collective-permute-start | bytes 393224 | tf_op jit(solution)/shard_map/while/body/eval_jaxpr/ppermute | solution.py:12
  272.4 21.7 %collective-permute-start.1 = (bf16[1,512,128]{2,1,0:T(8,128)(2,1)}, bf16[1,512,128]{2,1,0:T(8,128)(2,1)S(1)}, u32[]{:S(2)}, u32[]{:S(2)}) collective-permute-start(bf16[1,512,128]{2,1,0:T(8,128)(2,1)} %get-tuple-element.1106), channel_id=1, source_target_pairs={{0,1},{1,2},{2,3},{3,4},{4,5},{5,6},{6,7},{7,0},{8,9},{9,10},{10,1... | collective-permute-start | bytes 393224 | tf_op jit(solution)/shard_map/while/body/eval_jaxpr/ppermute | solution.py:12
  297.1 20.2 %collective-permute-start.2 = (f32[1,512,128]{2,1,0:T(8,128)}, f32[1,512,128]{2,1,0:T(8,128)S(1)}, u32[]{:S(2)}, u32[]{:S(2)}) collective-permute-start(f32[1,512,128]{2,1,0:T(8,128)} %get-tuple-element.1107), channel_id=1, source_target_pairs={{0,1},{1,2},{2,3},{3,4},{4,5},{5,6},{6,7},{7,0},{8,9},{9,10},{10,1... | collective-permute-start | bytes 786440 | tf_op jit(solution)/shard_map/while/body/eval_jaxpr/ppermute | solution.py:12
  297.1 21.0 %collective-permute-start.3 = (f32[1,512,128]{2,1,0:T(8,128)}, f32[1,512,128]{2,1,0:T(8,128)S(1)}, u32[]{:S(2)}, u32[]{:S(2)}) collective-permute-start(f32[1,512,128]{2,1,0:T(8,128)} %get-tuple-element.1108), channel_id=1, source_target_pairs={{0,1},{1,2},{2,3},{3,4},{4,5},{5,6},{6,7},{7,0},{8,9},{9,10},{10,1... | collective-permute-start | bytes 786440 | tf_op jit(solution)/shard_map/while/body/eval_jaxpr/ppermute | solution.py:12
  297.1 15.9 %collective-permute-start = (bf16[1,512,128]{2,1,0:T(8,128)(2,1)}, bf16[1,512,128]{2,1,0:T(8,128)(2,1)S(1)}, u32[]{:S(2)}, u32[]{:S(2)}) collective-permute-start(bf16[1,512,128]{2,1,0:T(8,128)(2,1)} %get-tuple-element.1105), channel_id=1, source_target_pairs={{0,1},{1,2},{2,3},{3,4},{4,5},{5,6},{6,7},{7,0},{8,9},{9,10},{10,1... | collective-permute-start | bytes 393224 | tf_op jit(solution)/shard_map/while/body/eval_jaxpr/ppermute | solution.py:12
  297.1 18.7 %collective-permute-start.1 = (bf16[1,512,128]{2,1,0:T(8,128)(2,1)}, bf16[1,512,128]{2,1,0:T(8,128)(2,1)S(1)}, u32[]{:S(2)}, u32[]{:S(2)}) collective-permute-start(bf16[1,512,128]{2,1,0:T(8,128)(2,1)} %get-tuple-element.1106), channel_id=1, source_target_pairs={{0,1},{1,2},{2,3},{3,4},{4,5},{5,6},{6,7},{7,0},{8,9},{9,10},{10,1... | collective-permute-start | bytes 393224 | tf_op jit(solution)/shard_map/while/body/eval_jaxpr/ppermute | solution.py:12
  318.8 19.6 %collective-permute-start.13 = (bf16[1,1024,128]{2,1,0:T(8,128)(2,1)}, bf16[1,1024,128]{2,1,0:T(8,128)(2,1)}, u32[]{:S(2)}, u32[]{:S(2)}) collective-permute-start(bf16[1,1024,128]{2,1,0:T(8,128)(2,1)} %bitcast.338), channel_id=1, source_target_pairs={{0,1},{1,2},{2,3},{3,4},{4,5},{5,6},{6,7},{7,0},{8,9},{9,10},{10,1... | collective-permute-start | bytes 786440 | tf_op jit(solution)/shard_map/while/body/eval_jaxpr/ppermute | solution.py:12
  326.7 12.6 %collective-permute-start.14 = (f32[1,1024,128]{2,1,0:T(8,128)}, f32[1,1024,128]{2,1,0:T(8,128)}, u32[]{:S(2)}, u32[]{:S(2)}) collective-permute-start(f32[1,1024,128]{2,1,0:T(8,128)} %fusion.75), channel_id=1, source_target_pairs={{0,1},{1,2},{2,3},{3,4},{4,5},{5,6},{6,7},{7,0},{8,9},{9,10},{10,1... | collective-permute-start | bytes 1572872 | tf_op jit(solution)/shard_map/while/body/eval_jaxpr/ppermute | solution.py:12
  330.5 25.1 %collective-permute-start.19 = (f32[1,1024,128]{2,1,0:T(8,128)}, f32[1,1024,128]{2,1,0:T(8,128)S(1)}, u32[]{:S(2)}, u32[]{:S(2)}) collective-permute-start(f32[1,1024,128]{2,1,0:T(8,128)} %fusion.72), channel_id=1, source_target_pairs={{0,1},{1,2},{2,3},{3,4},{4,5},{5,6},{6,7},{7,0},{8,9},{9,10},{10,1... | collective-permute-start | bytes 1572872 | tf_op jit(solution)/shard_map/while/body/eval_jaxpr/ppermute | solution.py:12
  332.4 50.7 %collective-permute-start.18 = (bf16[1,128,128]{2,1,0:T(8,128)(2,1)}, bf16[1,128,128]{2,1,0:T(8,128)(2,1)}, u32[]{:S(2)}, u32[]{:S(2)}) collective-permute-start(bf16[1,128,128]{2,1,0:T(8,128)(2,1)} %convert.30), channel_id=1, source_target_pairs={{0,1},{1,2},{2,3},{3,4},{4,5},{5,6},{6,7},{7,0},{8,9},{9,10},{10,1... | collective-permute-start | bytes 98312 | tf_op jit(solution)/shard_map/ppermute | solution.py:12
  338.3 44.8 %collective-permute-start.23 = (bf16[1,128,128]{2,1,0:T(8,128)(2,1)}, bf16[1,128,128]{2,1,0:T(8,128)(2,1)}, u32[]{:S(2)}, u32[]{:S(2)}) collective-permute-start(bf16[1,128,128]{2,1,0:T(8,128)(2,1)} %convert.33), channel_id=1, source_target_pairs={{0,1},{1,2},{2,3},{3,4},{4,5},{5,6},{6,7},{7,0},{8,9},{9,10},{10,1... | collective-permute-start | bytes 98312 | tf_op jit(solution)/shard_map/ppermute | solution.py:12
  338.4 40.9 %collective-permute-start.17 = (bf16[1,256,128]{2,1,0:T(8,128)(2,1)}, bf16[1,256,128]{2,1,0:T(8,128)(2,1)}, u32[]{:S(2)}, u32[]{:S(2)}) collective-permute-start(bf16[1,256,128]{2,1,0:T(8,128)(2,1)} %convert.29), channel_id=1, source_target_pairs={{0,1},{1,2},{2,3},{3,4},{4,5},{5,6},{6,7},{7,0},{8,9},{9,10},{10,1... | collective-permute-start | bytes 196616 | tf_op jit(solution)/shard_map/ppermute | solution.py:12
  340.4 21.1 %collective-permute-start.15 = (bf16[1,1024,128]{2,1,0:T(8,128)(2,1)S(1)}, bf16[1,1024,128]{2,1,0:T(8,128)(2,1)S(1)}, u32[]{:S(2)}, u32[]{:S(2)}) collective-permute-start(bf16[1,1024,128]{2,1,0:T(8,128)(2,1)S(1)} %add.436), channel_id=1, source_target_pairs={{0,7},{1,0},{2,1},{3,2},{4,3},{5,4},{6,5},{7,6},{8,15},{9,8},{10,9... | collective-permute-start | bytes 786440 | tf_op jit(solution)/shard_map/ppermute | solution.py:12
  355.7 14.3 %collective-permute-start.20 = (bf16[1,1024,128]{2,1,0:T(8,128)(2,1)S(1)}, bf16[1,1024,128]{2,1,0:T(8,128)(2,1)S(1)}, u32[]{:S(2)}, u32[]{:S(2)}) collective-permute-start(bf16[1,1024,128]{2,1,0:T(8,128)(2,1)S(1)} %add.437), channel_id=1, source_target_pairs={{0,7},{1,0},{2,1},{3,2},{4,3},{5,4},{6,5},{7,6},{8,15},{9,8},{10,9... | collective-permute-start | bytes 786440 | tf_op jit(solution)/shard_map/ppermute | solution.py:12
  361.5 12.4 %collective-permute-start.16 = (bf16[1,512,128]{2,1,0:T(8,128)(2,1)S(1)}, bf16[1,512,128]{2,1,0:T(8,128)(2,1)S(1)}, u32[]{:S(2)}, u32[]{:S(2)}) collective-permute-start(bf16[1,512,128]{2,1,0:T(8,128)(2,1)S(1)} %copy-done.18), channel_id=1, source_target_pairs={{0,5},{1,6},{2,7},{3,0},{4,1},{5,2},{6,3},{7,4},{8,13},{9,14},{10,... | collective-permute-start | bytes 393224 | tf_op jit(solution)/shard_map/ppermute | solution.py:12
  385.1 95.0 %reduce-scatter.6.cloned.1.call-start = ((), (), s32[]{:S(2)}) async-start(), calls=%async_computation.4 | async-start | bytes 5242880 | tf_op jit(solution)/shard_map/reduce_scatter | solution.py:169
  385.8 141.4 %reduce-scatter.8.cloned.1.call-start = ((), (), s32[]{:S(2)}) async-start(), calls=%async_computation.5 | async-start | bytes 5242880 | tf_op jit(solution)/shard_map/reduce_scatter | solution.py:169
  (58 other events, 843.2 us)
Sparse Core Ops, SparseCore 0:
  385.2 47.6 reduce-scatter.3
  435.5 44.5 reduce-scatter.5
  482.6 44.5 reduce-scatter.7
where the time goes:
time: 530 us; the launch traced here: 537 us
  waiting for transfers between devices  304 us (57%)
  local copies, waits for them, and re-layouts  86.8 us (16%)
  starting transfers between devices  80.9 us (15%)
  between operations  22.3 us (4%)
  other arithmetic  22.1 us (4%)
  matrix products  18.9 us (4%)
    ppermute x80, waiting for transfers between devices, passed_along(): lax.ppermute(array, axis, [(i, (i + by) % devices) for i in range(devices)])  168 us
    reduce_scatter x3, waiting for transfers between devices, body(): lax.psum_scatter(shortened(lowered), 'rate', scatter_dimension=1, tiled=T...  135 us
    ppermute x80, starting transfers between devices, passed_along(): lax.ppermute(array, axis, [(i, (i + by) % devices) for i in range(devices)])  80.8 us
    unnamed x79, local copies, waits for them, and re-layouts  30.1 us
    dynamic_slice x3, local copies, waits for them, and re-layouts, pick_rows(): lax.dynamic_index_in_dim(source_array, head_index, 1, keepdims=False)  20.1 us
    while x34, local copies, waits for them, and re-layouts  12.5 us
  transfers between devices with their start and end apart: 83, of which 40 were waited for; matrix products, arithmetic and copies ran while one was open for 20% of the time, Pallas kernels for 0%

commit v1 on v0

v1 whole, which is shorter than its diff:
```python
import math

import jax
import jax.numpy as jnp
from jax import lax
from jax.experimental import pallas as pl
from jax.experimental.pallas import tpu as pltpu
from jax.sharding import PartitionSpec as P


HEADS = 16
SEG = 2048
LEVELS = 4
GROUPS = ((0,), (1,), (2, 3))
LANES = 128
TAG_ROWS = 16
LOG2E = math.log2(math.e)


F32 = jnp.float32
BF16 = jnp.bfloat16


def swapped(array, axis, by):
    devices = lax.axis_size(axis)
    return lax.ppermute(array, axis, [(i, i ^ by) for i in range(devices)])


def rows_dot(a, b):
    return lax.dot_general(a, b, (((1,), (1,)), ((), ())), preferred_element_type=F32)


def plain_dot(a, b):
    return jnp.dot(a, b, preferred_element_type=F32)


class Level:
    def __init__(self, level, local_tokens, all_tokens):
        self.rate = 2**level
        self.rows = local_tokens // self.rate
        self.span = min(SEG, all_tokens // self.rate) * self.rate // local_tokens
        self.bits = self.span.bit_length() - 1
        self.tags = self.rows // LANES * TAG_ROWS
        self.pack_rows = 2 * self.rows + self.tags


def pack_layout(levels, members, bit):
    at, offsets = 0, {}
    for level in members:
        if bit < levels[level].bits:
            offsets[level] = at
            at += levels[level].pack_rows
    return offsets, at


def split3(col):
    hi = col.astype(BF16).astype(F32)
    rest = col - hi
    mid = rest.astype(BF16).astype(F32)
    return hi, mid, rest - mid


def extract_kernel(levels, groups, group_size, sm, keys, values, queries, grads, outs, logs, *refs):
    members = [m for group in groups for m in group]
    n = len(members)
    own_refs, tag_refs, col_refs = refs[:n], refs[n : 2 * n], refs[2 * n : 3 * n]
    at = 3 * n
    send_refs = {}
    for group in groups:
        for bit in range(group_bits(levels, group)):
            send_refs[group, bit] = refs[at]
            at += 1
    bufs = refs[at : at + n]
    turned, sems = refs[at + n :]
    rho, seq = lax.axis_index("rate"), lax.axis_index("seq")
    tokens = keys.shape[0]
    sources = (keys, values, queries, grads, outs)
    copies = []
    for w, level in enumerate(members):
        rate, rows = levels[level].rate, levels[level].rows
        head = sm[level * group_size + rho]
        off = rho & (rate - 1)
        for s, source in enumerate(sources):
            picked = source.reshape(rows, rate, HEADS // 2, 2, LANES).at[:, off, head // 2]
            copy = pltpu.make_async_copy(picked, bufs[w].at[s], sems.at[w, s])
            copy.start()
            copies.append(copy)
    for u in range(tokens // LANES):
        part = logs[:, u * LANES : (u + 1) * LANES]
        square = jnp.concatenate([part, jnp.zeros((LANES - HEADS, LANES), F32)], axis=0)
        turned[u * LANES : (u + 1) * LANES, :] = square.T
    row_id = lax.broadcasted_iota(jnp.int32, (LANES, 2 * LANES), 0)
    col_id = lax.broadcasted_iota(jnp.int32, (LANES, 2 * LANES), 1)
    lane = lax.broadcasted_iota(jnp.int32, (LANES, LANES), 1)
    group_of = {m: group for group in groups for m in group}
    for w, level in enumerate(members):
        lv = levels[level]
        group = group_of[level]
        head = sm[level * group_size + rho]
        off = rho & (lv.rate - 1)
        pick = (col_id == 2 * row_id + head % 2).astype(BF16)
        for s in range(len(sources)):
            copies[w * len(sources) + s].wait()
        flat = [bufs[w].at[s].reshape(2 * lv.rows, LANES) for s in range(len(sources))]
        for u in range(lv.rows // LANES):
            got = [
                plain_dot(pick, flat[s][u * 2 * LANES : (u + 1) * 2 * LANES, :])
                for s in range(len(sources))
            ]
            delta = jnp.sum(got[3] * got[4], axis=1, keepdims=True)
            start = u * LANES * lv.rate + off
            if lv.rate == 1:
                logs_u = turned[u * LANES : (u + 1) * LANES, :]
            else:
                logs_u = turned[pl.ds(start, LANES, stride=lv.rate), :]
            total = jnp.sum(jnp.where(lane == head, logs_u, 0.0), axis=1, keepdims=True) * LOG2E
            square = jnp.zeros((LANES, LANES), F32)
            for at, col in enumerate(split3(total) + split3(delta) + (total, delta)):
                square = jnp.where(lane == at, col, square)
            col_refs[w][u * LANES : (u + 1) * LANES, :] = square
            tags = square.T[:TAG_ROWS].astype(BF16)
            tag_refs[w][u * TAG_ROWS : (u + 1) * TAG_ROWS, :] = tags
            low = [g.astype(BF16) for g in got[:4]]
            for s in range(4):
                own_refs[w][s * lv.rows + u * LANES : s * lv.rows + (u + 1) * LANES, :] = low[s]
            for bit in range(lv.bits):
                base = pack_layout(levels, group, bit)[0][level]
                later = (seq >> bit) % 2 == 1
                send = send_refs[group, bit]
                for s in range(2):
                    first = base + s * lv.rows + u * LANES
                    send[first : first + LANES, :] = jnp.where(later, low[2 + s], low[s])
                first = base + 2 * lv.rows + u * TAG_ROWS
                send[first : first + TAG_ROWS, :] = tags


def group_bits(levels, group):
    return max(levels[m].bits for m in group)


def extract(levels, groups, group_size, sm, sources, logs):
    tokens = sources[0].shape[0]
    members = [m for group in groups for m in group]
    n = len(members)
    shapes = [jax.ShapeDtypeStruct((4 * levels[m].rows, LANES), BF16) for m in members]
    shapes += [jax.ShapeDtypeStruct((levels[m].tags, LANES), BF16) for m in members]
    shapes += [jax.ShapeDtypeStruct((levels[m].rows, LANES), F32) for m in members]
    sent = [(group, bit) for group in groups for bit in range(group_bits(levels, group))]
    shapes += [
        jax.ShapeDtypeStruct((pack_layout(levels, group, bit)[1], LANES), BF16)
        for group, bit in sent
    ]

    def kernel(*refs):
        extract_kernel(levels, groups, group_size, *refs)

    results = pl.pallas_call(
        kernel,
        out_shape=shapes,
        in_specs=[pl.BlockSpec(memory_space=pltpu.SMEM)]
        + [pl.BlockSpec(memory_space=pl.ANY)] * 5
        + [pl.BlockSpec(memory_space=pltpu.VMEM)],
        scratch_shapes=[pltpu.VMEM((5, levels[m].rows, 2, LANES), BF16) for m in members]
        + [pltpu.VMEM((tokens, LANES), F32), pltpu.SemaphoreType.DMA((n, 5))],
    )(sm, *sources, logs)
    kept = {m: (results[w], results[n + w], results[2 * n + w]) for w, m in enumerate(members)}
    return kept, dict(zip(sent, results[3 * n :]))


def tag_row(tags, first_row, count, which):
    parts = []
    for u in range(count // LANES):
        at = pl.multiple_of(first_row // LANES * TAG_ROWS + u * TAG_ROWS, TAG_ROWS)
        tile = tags[pl.ds(at, TAG_ROWS), :].astype(F32)
        parts.append(tile[which : which + 1] + tile[which + 1 : which + 2] + tile[which + 2 : which + 3])
    return parts[0] if len(parts) == 1 else jnp.concatenate(parts, axis=1)


def query_side(q, g, total, delta, k, v, factor, allowed):
    scores = rows_dot(q, k)
    probs = jnp.exp2(scores * factor - total)
    if allowed is not None:
        probs = jnp.where(allowed, probs, 0.0)
    ds = (probs * (rows_dot(g, v) - delta)).astype(BF16)
    return plain_dot(ds, k)


def key_side(k, v, q, g, total, delta, factor, allowed):
    scores = rows_dot(k, q)
    probs = jnp.exp2(scores * factor - total)
    if allowed is not None:
        probs = jnp.where(allowed, probs, 0.0)
    dv = plain_dot(probs.astype(BF16), g)
    ds = (probs * (rows_dot(v, g) - delta)).astype(BF16)
    return plain_dot(ds, q), dv


class Block:
    def __init__(self, ref, first, second, tag_ref, tag_base):
        self.ref, self.first, self.second = ref, first, second
        self.tag_ref, self.tag_base = tag_ref, tag_base

    def pair(self, at, tile):
        def load(base):
            return self.ref[pl.ds(pl.multiple_of(base + at, TAG_ROWS), tile), :]

        return load(self.first), load(self.second)

    def tags(self, at, tile):
        base = self.tag_base // TAG_ROWS * LANES
        return tag_row(self.tag_ref, base + at, tile, 0), tag_row(self.tag_ref, base + at, tile, 3)


def run_tiles(count, tile, step):
    if count == 1:
        step(0)
        return

    def turn(i, carry):
        step(pl.multiple_of(i * tile, tile))
        return carry

    lax.fori_loop(0, count, turn, 0)


class LevelWork:
    def __init__(self, lv, own, tags, col, acc, at, scaling):
        self.rows, self.acc, self.at, self.col = lv.rows, acc, at, col
        self.tile = min(lv.rows, 256)
        self.count = lv.rows // self.tile
        self.factor = scaling * LOG2E
        self.keys = Block(own, 0, lv.rows, None, 0)
        self.queries = Block(own, 2 * lv.rows, 3 * lv.rows, tags, 0)

    def put(self, which, at, value, add):
        first = self.at + which * self.rows + at
        where = pl.ds(pl.multiple_of(first, TAG_ROWS), self.tile)
        if add:
            self.acc[where, :] += value
        else:
            self.acc[where, :] = value

    def query_rows(self, at):
        q, g = self.queries.pair(at, self.tile)
        where = pl.ds(at, self.tile)
        return q, g, self.col[where, 6:7], self.col[where, 7:8]

    def diagonal(self):
        tile = self.tile
        tri_r = lax.broadcasted_iota(jnp.int32, (tile, tile), 0)
        tri_c = lax.broadcasted_iota(jnp.int32, (tile, tile), 1)
        for i in range(self.count):
            mine = self.query_rows(i * tile)
            sum_q = jnp.zeros((tile, LANES), F32)
            for j in range(i + 1):
                allowed = tri_c <= tri_r if i == j else None
                sum_q += query_side(*mine, *self.keys.pair(j * tile, tile), self.factor, allowed)
            self.put(0, i * tile, sum_q, False)
            mine = self.keys.pair(i * tile, tile)
            sum_k = jnp.zeros((tile, LANES), F32)
            sum_v = jnp.zeros((tile, LANES), F32)
            for j in range(i, self.count):
                allowed = tri_r <= tri_c if i == j else None
                there = self.queries.pair(j * tile, tile) + self.queries.tags(j * tile, tile)
                part = key_side(*mine, *there, self.factor, allowed)
                sum_k += part[0]
                sum_v += part[1]
            self.put(1, i * tile, sum_k, False)
            self.put(2, i * tile, sum_v, False)

    def earlier_keys(self, blocks):
        def step(at):
            mine = self.query_rows(at)
            sum_q = jnp.zeros((self.tile, LANES), F32)
            for block in blocks:
                for j in range(self.count):
                    there = block.pair(j * self.tile, self.tile)
                    sum_q += query_side(*mine, *there, self.factor, None)
            self.put(0, at, sum_q, True)

        run_tiles(self.count, self.tile, step)

    def later_queries(self, blocks):
        def step(at):
            mine = self.keys.pair(at, self.tile)
            sum_k = jnp.zeros((self.tile, LANES), F32)
            sum_v = jnp.zeros((self.tile, LANES), F32)
            for block in blocks:
                for j in range(self.count):
                    there = block.pair(j * self.tile, self.tile) + block.tags(j * self.tile, self.tile)
                    part = key_side(*mine, *there, self.factor, None)
                    sum_k += part[0]
                    sum_v += part[1]
            self.put(1, at, sum_k, True)
            self.put(2, at, sum_v, True)

        run_tiles(self.count, self.tile, step)


def compute(levels, members, bits, kept, received, before, after, last, scaling):
    n = len(members)
    steps = [k for k in sorted(received) if k.bit_length() - 1 in bits]
    total_rows = 3 * sum(levels[m].rows for m in members)
    given = [kept[m][part] for part in range(3) for m in members]
    given += [received[k] for k in steps]
    if before is not None:
        given.append(before)
    inputs = len(given)

    def kernel(*refs):
        own_refs, tag_refs, col_refs = refs[:n], refs[n : 2 * n], refs[2 * n : 3 * n]
        got = dict(zip(steps, refs[3 * n :]))
        out = refs[inputs + len(after)]
        acc = refs[inputs + len(after) + 1] if last else out
        seq = lax.axis_index("seq")
        if before is not None:
            acc[...] = refs[inputs - 1][...]
        work, at = [], 0
        for w, level in enumerate(members):
            lv = levels[level]
            work.append(LevelWork(lv, own_refs[w], tag_refs[w], col_refs[w], acc, at, scaling))
            at += 3 * lv.rows
        if before is None:
            for each in work:
                each.diagonal()
        for bit in bits:
            later = (seq >> bit) % 2 == 1
            offsets = pack_layout(levels, members, bit)[0]
            todo = []
            for w, level in enumerate(members):
                if level in offsets:
                    rows, base = levels[level].rows, offsets[level]
                    todo.append(
                        (
                            work[w],
                            [
                                Block(got[k], base, base + rows, got[k], base + 2 * rows)
                                for k in range(2**bit, 2 ** (bit + 1))
                            ],
                        )
                    )

            @pl.when(later)
            def _(todo=todo):
                for each, blocks in todo:
                    each.earlier_keys(blocks)

            @pl.when(jnp.logical_not(later))
            def _(todo=todo):
                for each, blocks in todo:
                    each.later_queries(blocks)

        if last:
            at = 0
            for level in members:
                rows = levels[level].rows
                out[at : at + 2 * rows, :] = (acc[at : at + 2 * rows, :] * scaling).astype(BF16)
                out[at + 2 * rows : at + 3 * rows, :] = acc[at + 2 * rows : at + 3 * rows, :].astype(BF16)
                at += 3 * rows

    return pl.pallas_call(
        kernel,
        out_shape=jax.ShapeDtypeStruct((total_rows, LANES), BF16 if last else F32),
        in_specs=[pl.BlockSpec(memory_space=pltpu.VMEM)] * inputs
        + [pl.BlockSpec(memory_space=pl.ANY)] * len(after),
        scratch_shapes=[pltpu.VMEM((total_rows, LANES), F32)] if last else [],
    )(*given, *after)


def place(levels, group_size, heads_here, local_tokens, sm, gathered):
    rates = len(gathered[0])
    flat = [array for group in gathered for array in group]
    block, half = LANES, LANES // 2
    steps = local_tokens // block
    tall = heads_here * half

    def kernel(sm_ref, *refs):
        sources = refs[: len(flat)]
        outs = refs[len(flat) : len(flat) + 3]
        spread, buf, sems = refs[len(flat) + 3 :]
        step = pl.program_id(0)
        rho = lax.axis_index("rate")
        slots = []
        for i in range(heads_here):
            slot = jnp.int32(0)
            for s in range(HEADS):
                slot = jnp.where(sm_ref[s] == rho * heads_here + i, s, slot)
            slots.append(slot)
        shifts = [slot // group_size for slot in slots]

        @pl.when(step == 0)
        def _():
            for i in range(heads_here):
                for level in range(1, LEVELS):
                    end = 3 * levels[level].rows
                    buf[i, end : end + block, :] = jnp.zeros((block, LANES), BF16)

            def each(act):
                for i in range(heads_here):
                    lane_i = slots[i] % group_size
                    for g, members in enumerate(GROUPS):
                        at = 0
                        for level in members:
                            rows = 3 * levels[level].rows
                            for x in range(rates):
                                hit = jnp.logical_and(shifts[i] == level, lane_i == rho ^ x)

                                @pl.when(hit)
                                def _(i=i, g=g, x=x, at=at, rows=rows):
                                    act(
                                        pltpu.make_async_copy(
                                            sources[g * rates + x].at[pl.ds(at, rows)],
                                            buf.at[i, pl.ds(0, rows)],
                                            sems.at[i],
                                        )
                                    )

                            at += rows

            each(lambda copy: copy.start())
            row_id = lax.broadcasted_iota(jnp.int32, (tall, half), 0)
            col_id = lax.broadcasted_iota(jnp.int32, (tall, half), 1)
            for part in range(2):
                for i in range(heads_here):
                    rate = 1 << shifts[i]
                    off = (slots[i] % group_size) & (rate - 1)
                    first = jnp.where(shifts[i] == 0, 0, part * half)
                    token = col_id * rate + (off - first)
                    hit = row_id == token * heads_here + i
                    spread[part, :, i * half : (i + 1) * half] = hit.astype(BF16)
            each(lambda copy: copy.wait())

        for part in range(2):
            columns = []
            for which in range(3):
                rows = []
                for i in range(heads_here):
                    at = which * (local_tokens >> shifts[i]) + step * (block >> shifts[i])
                    at += jnp.where(shifts[i] == 0, part * half, 0)
                    rows.append(buf[i, pl.ds(pl.multiple_of(at, TAG_ROWS), half), :])
                columns.append(jnp.concatenate(rows, axis=0))
            two = plain_dot(spread[part], jnp.concatenate(columns[:2], axis=1))
            where = pl.ds(part * tall, tall)
            outs[0][where, :] = two[:, :LANES].astype(BF16)
            outs[1][where, :] = two[:, LANES:].astype(BF16)
            outs[2][where, :] = plain_dot(spread[part], columns[2]).astype(BF16)

    shape = jax.ShapeDtypeStruct((local_tokens * heads_here, LANES), BF16)
    spec = pl.BlockSpec((block * heads_here, LANES), lambda i: (i, 0))
    results = pl.pallas_call(
        kernel,
        grid=(steps,),
        out_shape=[shape] * 3,
        in_specs=[pl.BlockSpec(memory_space=pltpu.SMEM)]
        + [pl.BlockSpec(memory_space=pl.ANY)] * len(flat),
        out_specs=[spec] * 3,
        scratch_shapes=[
            pltpu.VMEM((2, tall, tall), BF16),
            pltpu.VMEM((heads_here, 3 * local_tokens + block, LANES), BF16),
            pltpu.SemaphoreType.DMA((heads_here,)),
        ],
        name="place",
    )(sm, *flat)
    return tuple(r.reshape(local_tokens, heads_here, LANES) for r in results)


def body(queries, key_rows, values, attn_out, out_grad, log_totals, assignment):
    local_tokens = queries.shape[0]
    scaling = queries.shape[2] ** (-0.5)
    rate_count = lax.axis_size("rate")
    seq_count = lax.axis_size("seq")
    group_size = HEADS // LEVELS
    levels = [Level(c, local_tokens, local_tokens * seq_count) for c in range(LEVELS)]
    paired = [
        a.reshape(local_tokens, HEADS // 2, 2, LANES)
        for a in (key_rows, values, queries, out_grad, attn_out)
    ]
    logs = log_totals.T
    kept, received = {}, {}
    for groups in (GROUPS[:1], GROUPS[1:]):
        some, sends = extract(levels, groups, group_size, assignment, paired, logs)
        kept.update(some)
        for members in groups:
            received[members] = {}
            for k in range(1, 2 ** group_bits(levels, members)):
                got = swapped(sends[members, k.bit_length() - 1], "seq", k)
                received[members][k] = got
    gathered = []
    for members in GROUPS:
        bits = list(range(group_bits(levels, members)))
        after = [kept[GROUPS[-1][-1]][1]] if members == GROUPS[0] else []
        split = 2 if len(bits) > 2 else len(bits)
        mine = None
        for part in (bits[:split], bits[split:]):
            if part:
                mine = compute(
                    levels,
                    members,
                    part,
                    kept,
                    received[members],
                    mine,
                    after,
                    part[-1] == bits[-1],
                    scaling,
                )
        far = swapped(mine, "rate", 2)
        gathered.append([mine, swapped(mine, "rate", 1), far, swapped(far, "rate", 1)])
    return place(levels, group_size, HEADS // rate_count, local_tokens, assignment, gathered)


def solution(mesh):
    placed = (P("seq", None, None),) * 5 + (P("seq", None), P())
    return jax.shard_map(
        body,
        mesh=mesh,
        in_specs=placed,
        out_specs=(P("seq", "rate", None),) * 3,
        check_vma=False,
    )
```

time: 530 us -> 116 us (0.22); the launches traced: 537 us -> 116 us
  waiting for transfers between devices: 304 us -> 40.2 us
  local copies, waits for them, and re-layouts: 86.8 us -> 3.97 us
  starting transfers between devices: 80.9 us -> 27.5 us
  Pallas kernels: 0 us -> 43.1 us
  other arithmetic: 22.1 us -> 0 us
  between operations: 22.3 us -> 0.91 us
  matrix products: 18.9 us -> 0 us
    reduce_scatter x3 -> x0, waiting for transfers between devices: 135 us -> none  [body(): lax.psum_scatter(shortened(lowered), 'rate', scatter_dimension=1, tiled=T...]
    ppermute x80 -> x20, waiting for transfers between devices: 168 us -> 40.2 us  [swapped(): return lax.ppermute(array, axis, [(i, i ^ by) for i in range(devices)])]
    ppermute x80 -> x20, starting transfers between devices: 80.8 us -> 27.5 us  [swapped(): return lax.ppermute(array, axis, [(i, i ^ by) for i in range(devices)])]
    pallas_call x0 -> x7, Pallas kernels: none -> 43.1 us  [the longest x4 24.4 us: compute(): pl.pallas_call(kernel, out_shape=jax.ShapeDtypeStruct((total_rows, LANES)...]
    dynamic_slice x19 -> x0, local copies, waits for them, and re-layouts: 28.3 us -> none  [the longest x3 20.1 us: pick_rows(): lax.dynamic_index_in_dim(source_array, head_index, 1, keepdims=False)]
    unnamed x79 -> x36, local copies, waits for them, and re-layouts: 30.1 us -> 3.97 us
    dot_general x20 -> x0, matrix products: 18.9 us -> none  [the longest x4 4.99 us: block_terms(): jnp.einsum('hqk,hqd->hkd', probs.astype(jnp.bfloat16), grad_blk, preferre...]
    while x34 -> x0, local copies, waits for them, and re-layouts: 12.5 us -> none
  transfers between devices with their start and end apart: 83 -> 20, of which waited for: 40 -> 9; matrix products, arithmetic and copies ran while one was open for 20% -> 0% of each run, Pallas kernels for 0% -> 18%
where the time goes in v1:
time: 116 us
  Pallas kernels  43.1 us (37%)
  waiting for transfers between devices  40.2 us (35%)
  starting transfers between devices  27.5 us (24%)
  local copies, waits for them, and re-layouts  3.97 us (3%)
    ppermute x20, waiting for transfers between devices, swapped(): return lax.ppermute(array, axis, [(i, i ^ by) for i in range(devices)])  40.2 us
    ppermute x20, starting transfers between devices, swapped(): return lax.ppermute(array, axis, [(i, i ^ by) for i in range(devices)])  27.5 us
    pallas_call x4, Pallas kernels, compute(): pl.pallas_call(kernel, out_shape=jax.ShapeDtypeStruct((total_rows, LANES)...  24.4 us
    pallas_call x2, Pallas kernels, extract(): pl.pallas_call(kernel, out_shape=shapes, in_specs=[pl.BlockSpec(memory_sp...  11.9 us
    pallas_call x1, Pallas kernels, place(): pl.pallas_call(kernel, grid=(steps,), out_shape=[shape] * 3, in_specs=[pl...  6.81 us
    unnamed x36, local copies, waits for them, and re-layouts  3.97 us
  transfers between devices with their start and end apart: 20, of which 9 were waited for; matrix products, arithmetic and copies ran while one was open for 0% of the time, Pallas kernels for 18%

profile of v1, /device:TPU:0, one launch (start us, length us, event | category | flops | bytes accessed | tf_op | source)
XLA Modules:
  0.0 115.7 jit_solution(11126679146802613440)
XLA Ops:
  0.6 6.1 %shard_map.94 = (bf16[4096,128]{1,0:T(8,128)(2,1)}, bf16[128,128]{1,0:T(8,128)(2,1)}, f32[1024,128]{1,0:T(8,128)}, bf16[2176,128]{1,0:T(8,128)(2,1)}) custom-call(s32[16]{0:T(128)} %sm_ref.1, bf16[1024,8,2,128]{3,2,1,0:T(2,128)(2,1)} %bitcast.9, bf16[1024,8,2,128]{3,2,1,0:T(2,128)(2,1)} %bitcast.11, bf16[1024,8,2,128]{3,2,1,0:T(2,128)(2,1)} %bitcast.13, ...), custom_call_target="tpu_custom_call" | custom-call | tf_op jit(solution)/shard_map/pallas_call | solution.py:157
  6.7 3.0 %collective-permute-start = (bf16[2176,128]{1,0:T(8,128)(2,1)}, bf16[2176,128]{1,0:T(8,128)(2,1)S(1)}, u32[]{:S(2)}, u32[]{:S(2)}) collective-permute-start(bf16[2176,128]{1,0:T(8,128)(2,1)} %get-tuple-element.27), channel_id=1, source_target_pairs={{0,1},{1,0},{2,3},{3,2},{4,5},{5,4},{6,7},{7,6},{8,9},{9,8},{10,11... | collective-permute-start | bytes 1671176 | tf_op jit(solution)/shard_map/ppermute | solution.py:26
  9.8 5.8 %shard_map.95 = (bf16[2048,128]{1,0:T(8,128)(2,1)}, bf16[1024,128]{1,0:T(8,128)(2,1)}, bf16[512,128]{1,0:T(8,128)(2,1)}, bf16[64,128]{1,0:T(8,128)(2,1)}, bf16[3...) custom-call(s32[16]{0:T(128)} %sm_ref.1, ...), custom_call_target="tpu_custom_call" | custom-call | tf_op jit(solution)/shard_map/pallas_call | solution.py:157
  15.6 7.0 %collective-permute-done.refs_3_ = bf16[2176,128]{1,0:T(8,128)(2,1)S(1)} collective-permute-done((bf16[2176,128]{1,0:T(8,128)(2,1)}, bf16[2176,128]{1,0:T(8,128)(2,1)S(1)}, u32[]{:S(2)}, u32[]{:S(2)}) %collective-permute-start) | collective-permute-done | bytes 557088 | tf_op jit(solution)/shard_map/ppermute | solution.py:26
  22.6 0.8 copy-done.3
  23.4 9.2 %shard_map.96.refs_0_ = bf16[3072,128]{1,0:T(8,128)(2,1)} custom-call(bf16[4096,128]{1,0:T(8,128)(2,1)} %get-tuple-element.24.refs_0_, bf16[128,128]{1,0:T(8,128)(2,1)} %get-tuple-element.25.refs_1_, f32[1024,128]{1,0:T(8,128)} %get-tuple-element.26.refs_2_, bf16[2176,128]{1,0:T(8,128)(2,1)} %copy-done.3, bf16[16,128]{1,0:T(8,128)(2,1)} %get-tuple-element.28.refs_4_.refs_3_), custom_call_target="tpu_custom_call" | custom-call | tf_op jit(solution)/shard_map/pallas_call | solution.py:361
  32.6 1.8 %collective-permute-start.2 = (bf16[3072,128]{1,0:T(8,128)(2,1)}, bf16[3072,128]{1,0:T(8,128)(2,1)S(1)}, u32[]{:S(2)}, u32[]{:S(2)}) collective-permute-start(bf16[3072,128]{1,0:T(8,128)(2,1)} %shard_map.96.refs_0_), channel_id=1, source_target_pairs={{0,16},{8,24},{16,0},{24,8},{1,17},{9,25},{17,1},{25,9},{2,18},{10... | collective-permute-start | bytes 2359304 | tf_op jit(solution)/shard_map/ppermute | solution.py:26
  34.4 1.4 %collective-permute-start.14 = (bf16[816,128]{1,0:T(8,128)(2,1)}, bf16[816,128]{1,0:T(8,128)(2,1)S(1)}, u32[]{:S(2)}, u32[]{:S(2)}) collective-permute-start(bf16[816,128]{1,0:T(8,128)(2,1)} %get-tuple-element.40), channel_id=1, source_target_pairs={{0,1},{1,0},{2,3},{3,2},{4,5},{5,4},{6,7},{7,6},{8,9},{9,8},{10,11... | collective-permute-start | bytes 626696 | tf_op jit(solution)/shard_map/ppermute | solution.py:26
  35.9 1.6 %collective-permute-start.16 = (bf16[816,128]{1,0:T(8,128)(2,1)}, bf16[816,128]{1,0:T(8,128)(2,1)S(1)}, u32[]{:S(2)}, u32[]{:S(2)}) collective-permute-start(bf16[816,128]{1,0:T(8,128)(2,1)} %get-tuple-element.41), channel_id=1, source_target_pairs={{0,3},{1,2},{2,1},{3,0},{4,7},{5,6},{6,5},{7,4},{8,11},{9,10},{10,... | collective-permute-start | bytes 626696 | tf_op jit(solution)/shard_map/ppermute | solution.py:26
  37.4 1.4 %collective-permute-start.4 = (bf16[1088,128]{1,0:T(8,128)(2,1)}, bf16[1088,128]{1,0:T(8,128)(2,1)S(1)}, u32[]{:S(2)}, u32[]{:S(2)}) collective-permute-start(bf16[1088,128]{1,0:T(8,128)(2,1)} %get-tuple-element.32), channel_id=1, source_target_pairs={{0,1},{1,0},{2,3},{3,2},{4,5},{5,4},{6,7},{7,6},{8,9},{9,8},{10,11... | collective-permute-start | bytes 835592 | tf_op jit(solution)/shard_map/ppermute | solution.py:26
  38.9 0.4 collective-permute-start.15
  39.3 8.1 %collective-permute-done.14.refs_6_ = bf16[816,128]{1,0:T(8,128)(2,1)S(1)} collective-permute-done((bf16[816,128]{1,0:T(8,128)(2,1)}, bf16[816,128]{1,0:T(8,128)(2,1)S(1)}, u32[]{:S(2)}, u32[]{:S(2)}) %collective-permute-start.14) | collective-permute-done | bytes 208928 | tf_op jit(solution)/shard_map/ppermute | solution.py:26
  47.4 1.4 %collective-permute-start.6 = (bf16[1088,128]{1,0:T(8,128)(2,1)}, bf16[1088,128]{1,0:T(8,128)(2,1)S(1)}, u32[]{:S(2)}, u32[]{:S(2)}) collective-permute-start(bf16[1088,128]{1,0:T(8,128)(2,1)} %get-tuple-element.33), channel_id=1, source_target_pairs={{0,3},{1,2},{2,1},{3,0},{4,7},{5,6},{6,5},{7,4},{8,11},{9,10},{10,... | collective-permute-start | bytes 835592 | tf_op jit(solution)/shard_map/ppermute | solution.py:26
  48.8 0.0 collective-permute-done.16.refs_8_
  48.8 1.4 %collective-permute-start.5 = (bf16[1088,128]{1,0:T(8,128)(2,1)}, bf16[1088,128]{1,0:T(8,128)(2,1)S(1)}, u32[]{:S(2)}, u32[]{:S(2)}) collective-permute-start(bf16[1088,128]{1,0:T(8,128)(2,1)} %get-tuple-element.33), channel_id=1, source_target_pairs={{0,2},{1,3},{2,0},{3,1},{4,6},{5,7},{6,4},{7,5},{8,10},{9,11},{10,... | collective-permute-start | bytes 835592 | tf_op jit(solution)/shard_map/ppermute | solution.py:26
  50.2 4.8 %collective-permute-start.13 = (bf16[816,128]{1,0:T(8,128)(2,1)}, bf16[816,128]{1,0:T(8,128)(2,1)S(1)}, u32[]{:S(2)}, u32[]{:S(2)}) collective-permute-start(bf16[816,128]{1,0:T(8,128)(2,1)} %get-tuple-element.39), channel_id=1, source_target_pairs={{0,7},{1,6},{2,5},{3,4},{4,3},{5,2},{6,1},{7,0},{8,15},{9,14},{10,... | collective-permute-start | bytes 626696 | tf_op jit(solution)/shard_map/ppermute | solution.py:26
  55.1 2.7 %collective-permute-done.4.refs_3_ = bf16[1088,128]{1,0:T(8,128)(2,1)S(1)} collective-permute-done((bf16[1088,128]{1,0:T(8,128)(2,1)}, bf16[1088,128]{1,0:T(8,128)(2,1)S(1)}, u32[]{:S(2)}, u32[]{:S(2)}) %collective-permute-start.4) | collective-permute-done | bytes 278560 | tf_op jit(solution)/shard_map/ppermute | solution.py:26
  57.8 4.9 %collective-permute-start.12 = (bf16[816,128]{1,0:T(8,128)(2,1)}, bf16[816,128]{1,0:T(8,128)(2,1)S(1)}, u32[]{:S(2)}, u32[]{:S(2)}) collective-permute-start(bf16[816,128]{1,0:T(8,128)(2,1)} %get-tuple-element.39), channel_id=1, source_target_pairs={{0,6},{1,7},{2,4},{3,5},{4,2},{5,3},{6,0},{7,1},{8,14},{9,15},{10,... | collective-permute-start | bytes 626696 | tf_op jit(solution)/shard_map/ppermute | solution.py:26
  62.6 0.0 collective-permute-done.6.refs_5_
  62.7 2.5 %collective-permute-start.11 = (bf16[816,128]{1,0:T(8,128)(2,1)}, bf16[816,128]{1,0:T(8,128)(2,1)}, u32[]{:S(2)}, u32[]{:S(2)}) collective-permute-start(bf16[816,128]{1,0:T(8,128)(2,1)} %get-tuple-element.39), channel_id=1, source_target_pairs={{0,5},{1,4},{2,7},{3,6},{4,1},{5,0},{6,3},{7,2},{8,13},{9,12},{10,... | collective-permute-start | bytes 626696 | tf_op jit(solution)/shard_map/ppermute | solution.py:26
  65.2 1.2 %collective-permute-start.10 = (bf16[816,128]{1,0:T(8,128)(2,1)}, bf16[816,128]{1,0:T(8,128)(2,1)}, u32[]{:S(2)}, u32[]{:S(2)}) collective-permute-start(bf16[816,128]{1,0:T(8,128)(2,1)} %get-tuple-element.39), channel_id=1, source_target_pairs={{0,4},{1,5},{2,6},{3,7},{4,0},{5,1},{6,2},{7,3},{8,12},{9,13},{10,... | collective-permute-start | bytes 626696 | tf_op jit(solution)/shard_map/ppermute | solution.py:26
  66.4 6.3 %shard_map.97.refs_4_ = bf16[1536,128]{1,0:T(8,128)(2,1)} custom-call(bf16[2048,128]{1,0:T(8,128)(2,1)} %get-tuple-element.29.refs_0_, bf16[64,128]{1,0:T(8,128)(2,1)} %get-tuple-element.30.refs_1_, f32[512,128]{1,0:T(8,128)} %get-tuple-element.31.refs_2_, bf16[1088,128]{1,0:T(8,128)(2,1)} %copy-done.10, bf16[1088,128]{1,0:T(8,128)(2,1)} %copy-done.12, ...), custom_call_target="tpu_custom_call" | custom-call | tf_op jit(solution)/shard_map/pallas_call | solution.py:361
  72.7 0.0 collective-permute-done.13.refs_9_
  72.7 0.5 collective-permute-start.8
  73.3 0.7 collective-permute-done.12.refs_8_
  74.0 0.7 copy-done.17
  74.7 0.0 collective-permute-done.2.refs_2_
  74.7 0.0 collective-permute-start.3
  74.7 4.6 %shard_map.98.refs_10_ = f32[1152,128]{1,0:T(8,128)} custom-call(bf16[1024,128]{1,0:T(8,128)(2,1)} %get-tuple-element.34.refs_0_, bf16[512,128]{1,0:T(8,128)(2,1)} %get-tuple-element.35.refs_1_, bf16[32,128]{1,0:T(8,128)(2,1)} %get-tuple-element.36.refs_2_, bf16[16,128]{1,0:T(8,128)(2,1)} %get-tuple-element.28.refs_4_.refs_3_, ...), custom_call_target="tpu_custom_call" | custom-call | tf_op jit(solution)/shard_map/pallas_call | solution.py:361
  79.4 8.7 %collective-permute-done.11.refs_7_ = bf16[816,128]{1,0:T(8,128)(2,1)} collective-permute-done((bf16[816,128]{1,0:T(8,128)(2,1)}, bf16[816,128]{1,0:T(8,128)(2,1)}, u32[]{:S(2)}, u32[]{:S(2)}) %collective-permute-start.11) | collective-permute-done | bytes 208928 | tf_op jit(solution)/shard_map/ppermute | solution.py:26
  88.0 3.4 %collective-permute-done.10.refs_6_ = bf16[816,128]{1,0:T(8,128)(2,1)} collective-permute-done((bf16[816,128]{1,0:T(8,128)(2,1)}, bf16[816,128]{1,0:T(8,128)(2,1)}, u32[]{:S(2)}, u32[]{:S(2)}) %collective-permute-start.10) | collective-permute-done | bytes 208928 | tf_op jit(solution)/shard_map/ppermute | solution.py:26
  91.5 4.1 %shard_map.99.refs_8_ = bf16[1152,128]{1,0:T(8,128)(2,1)} custom-call(bf16[1024,128]{1,0:T(8,128)(2,1)} %get-tuple-element.34.refs_0_, bf16[512,128]{1,0:T(8,128)(2,1)} %get-tuple-element.35.refs_1_, bf16[32,128]{1,0:T(8,128)(2,1)} %get-tuple-element.36.refs_2_, bf16[16,128]{1,0:T(8,128)(2,1)} %get-tuple-element.28.refs_4_.refs_3_, ...), custom_call_target="tpu_custom_call" | custom-call | tf_op jit(solution)/shard_map/pallas_call | solution.py:361
  95.6 0.4 collective-permute-start.18
  96.1 0.0 collective-permute-start.17
  96.1 7.3 %collective-permute-done.18.refs_10_ = bf16[1152,128]{1,0:T(8,128)(2,1)S(1)} collective-permute-done((bf16[1152,128]{1,0:T(8,128)(2,1)}, bf16[1152,128]{1,0:T(8,128)(2,1)S(1)}, u32[]{:S(2)}, u32[]{:S(2)}) %collective-permute-start.18) | collective-permute-done | bytes 294944 | tf_op jit(solution)/shard_map/ppermute | solution.py:26
  103.3 0.0 collective-permute-start.7
  103.4 0.5 collective-permute-start.9
  103.8 0.0 collective-permute-done.17.refs_9_
  103.9 0.1 collective-permute-start.19
  103.9 1.3 %collective-permute-done.7.refs_5_ = bf16[1536,128]{1,0:T(8,128)(2,1)S(1)} collective-permute-done((bf16[1536,128]{1,0:T(8,128)(2,1)}, bf16[1536,128]{1,0:T(8,128)(2,1)S(1)}, u32[]{:S(2)}, u32[]{:S(2)}) %collective-permute-start.7) | collective-permute-done | bytes 393248 | tf_op jit(solution)/shard_map/ppermute | solution.py:26
  105.3 1.0 collective-permute-done.19.refs_11_
  106.3 0.0 collective-permute-done.9.refs_7_
  106.3 0.0 collective-permute-done.1.refs_1_
  106.3 0.7 copy-done.9
  107.0 0.1 copy-done.6
  107.1 0.7 copy-done.1
  107.9 0.9 copy-done.2
  108.8 6.8 %place.1 = (bf16[4096,128]{1,0:T(8,128)(2,1)}, bf16[4096,128]{1,0:T(8,128)(2,1)}, bf16[4096,128]{1,0:T(8,128)(2,1)}) custom-call(s32[16]{0:T(128)} %sm_ref.1, bf16[3072,128]{1,0:T(8,128)(2,1)} %shard_map.96.refs_0_, bf16[3072,128]{1,0:T(8,128)(2,1)} %copy-done.1, bf16[3072,128]{1,0:T(8,128)(2,1)} %copy-done, bf16[3072,128]{1,0:T(8,128)(2,1)} %copy-done.2, ...), custom_call_target="tpu_custom_call" | custom-call | tf_op jit(solution)/shard_map/place/pallas_call | solution.py:450
  (35 shorter events, 0.1 us)
Async XLA Ops:
  6.7 15.9 %collective-permute-start = (bf16[2176,128]{1,0:T(8,128)(2,1)}, bf16[2176,128]{1,0:T(8,128)(2,1)S(1)}, u32[]{:S(2)}, u32[]{:S(2)}) collective-permute-start(bf16[2176,128]{1,0:T(8,128)(2,1)} %get-tuple-element.27), channel_id=1, source_target_pairs={{0,1},{1,0},{2,3},{3,2},{4,5},{5,4},{6,7},{7,6},{8,9},{9,8},{10,11... | collective-permute-start | bytes 1671176 | tf_op jit(solution)/shard_map/ppermute | solution.py:26
  22.6 0.8 copy-start.3
  32.6 42.1 %collective-permute-start.2 = (bf16[3072,128]{1,0:T(8,128)(2,1)}, bf16[3072,128]{1,0:T(8,128)(2,1)S(1)}, u32[]{:S(2)}, u32[]{:S(2)}) collective-permute-start(bf16[3072,128]{1,0:T(8,128)(2,1)} %shard_map.96.refs_0_), channel_id=1, source_target_pairs={{0,16},{8,24},{16,0},{24,8},{1,17},{9,25},{17,1},{25,9},{2,18},{10... | collective-permute-start | bytes 2359304 | tf_op jit(solution)/shard_map/ppermute | solution.py:26
  34.4 13.0 %collective-permute-start.14 = (bf16[816,128]{1,0:T(8,128)(2,1)}, bf16[816,128]{1,0:T(8,128)(2,1)S(1)}, u32[]{:S(2)}, u32[]{:S(2)}) collective-permute-start(bf16[816,128]{1,0:T(8,128)(2,1)} %get-tuple-element.40), channel_id=1, source_target_pairs={{0,1},{1,0},{2,3},{3,2},{4,5},{5,4},{6,7},{7,6},{8,9},{9,8},{10,11... | collective-permute-start | bytes 626696 | tf_op jit(solution)/shard_map/ppermute | solution.py:26
  35.9 12.9 %collective-permute-start.16 = (bf16[816,128]{1,0:T(8,128)(2,1)}, bf16[816,128]{1,0:T(8,128)(2,1)S(1)}, u32[]{:S(2)}, u32[]{:S(2)}) collective-permute-start(bf16[816,128]{1,0:T(8,128)(2,1)} %get-tuple-element.41), channel_id=1, source_target_pairs={{0,3},{1,2},{2,1},{3,0},{4,7},{5,6},{6,5},{7,4},{8,11},{9,10},{10,... | collective-permute-start | bytes 626696 | tf_op jit(solution)/shard_map/ppermute | solution.py:26
  37.4 20.3 %collective-permute-start.4 = (bf16[1088,128]{1,0:T(8,128)(2,1)}, bf16[1088,128]{1,0:T(8,128)(2,1)S(1)}, u32[]{:S(2)}, u32[]{:S(2)}) collective-permute-start(bf16[1088,128]{1,0:T(8,128)(2,1)} %get-tuple-element.32), channel_id=1, source_target_pairs={{0,1},{1,0},{2,3},{3,2},{4,5},{5,4},{6,7},{7,6},{8,9},{9,8},{10,11... | collective-permute-start | bytes 835592 | tf_op jit(solution)/shard_map/ppermute | solution.py:26
  38.9 11.4 %collective-permute-start.15 = (bf16[816,128]{1,0:T(8,128)(2,1)}, bf16[816,128]{1,0:T(8,128)(2,1)S(1)}, u32[]{:S(2)}, u32[]{:S(2)}) collective-permute-start(bf16[816,128]{1,0:T(8,128)(2,1)} %get-tuple-element.41), channel_id=1, source_target_pairs={{0,2},{1,3},{2,0},{3,1},{4,6},{5,7},{6,4},{7,5},{8,10},{9,11},{10,... | collective-permute-start | bytes 626696 | tf_op jit(solution)/shard_map/ppermute | solution.py:26
  47.4 27.3 %copy-start.13 = (bf16[816,128]{1,0:T(8,128)(2,1)}, bf16[816,128]{1,0:T(8,128)(2,1)S(1)}, u32[]{:S(2)}) copy-start(bf16[816,128]{1,0:T(8,128)(2,1)S(1)} %collective-permute-done.14.refs_6_) | copy-start | bytes 626692
  47.4 15.2 %collective-permute-start.6 = (bf16[1088,128]{1,0:T(8,128)(2,1)}, bf16[1088,128]{1,0:T(8,128)(2,1)S(1)}, u32[]{:S(2)}, u32[]{:S(2)}) collective-permute-start(bf16[1088,128]{1,0:T(8,128)(2,1)} %get-tuple-element.33), channel_id=1, source_target_pairs={{0,3},{1,2},{2,1},{3,0},{4,7},{5,6},{6,5},{7,4},{8,11},{9,10},{10,... | collective-permute-start | bytes 835592 | tf_op jit(solution)/shard_map/ppermute | solution.py:26
  48.8 25.9 %copy-start.14 = (bf16[816,128]{1,0:T(8,128)(2,1)}, bf16[816,128]{1,0:T(8,128)(2,1)S(1)}, u32[]{:S(2)}) copy-start(bf16[816,128]{1,0:T(8,128)(2,1)S(1)} %collective-permute-done.16.refs_8_) | copy-start | bytes 626692
  48.8 16.4 %collective-permute-start.5 = (bf16[1088,128]{1,0:T(8,128)(2,1)}, bf16[1088,128]{1,0:T(8,128)(2,1)S(1)}, u32[]{:S(2)}, u32[]{:S(2)}) collective-permute-start(bf16[1088,128]{1,0:T(8,128)(2,1)} %get-tuple-element.33), channel_id=1, source_target_pairs={{0,2},{1,3},{2,0},{3,1},{4,6},{5,7},{6,4},{7,5},{8,10},{9,11},{10,... | collective-permute-start | bytes 835592 | tf_op jit(solution)/shard_map/ppermute | solution.py:26
  50.2 24.5 %copy-start.15 = (bf16[816,128]{1,0:T(8,128)(2,1)}, bf16[816,128]{1,0:T(8,128)(2,1)S(1)}, u32[]{:S(2)}) copy-start(bf16[816,128]{1,0:T(8,128)(2,1)S(1)} %collective-permute-done.15.refs_7_) | copy-start | bytes 626692
  50.2 22.5 %collective-permute-start.13 = (bf16[816,128]{1,0:T(8,128)(2,1)}, bf16[816,128]{1,0:T(8,128)(2,1)S(1)}, u32[]{:S(2)}, u32[]{:S(2)}) collective-permute-start(bf16[816,128]{1,0:T(8,128)(2,1)} %get-tuple-element.39), channel_id=1, source_target_pairs={{0,7},{1,6},{2,5},{3,4},{4,3},{5,2},{6,1},{7,0},{8,15},{9,14},{10,... | collective-permute-start | bytes 626696 | tf_op jit(solution)/shard_map/ppermute | solution.py:26
  57.8 8.6 %copy-start.10 = (bf16[1088,128]{1,0:T(8,128)(2,1)}, bf16[1088,128]{1,0:T(8,128)(2,1)S(1)}, u32[]{:S(2)}) copy-start(bf16[1088,128]{1,0:T(8,128)(2,1)S(1)} %collective-permute-done.4.refs_3_) | copy-start | bytes 835588
  57.8 16.2 %collective-permute-start.12 = (bf16[816,128]{1,0:T(8,128)(2,1)}, bf16[816,128]{1,0:T(8,128)(2,1)S(1)}, u32[]{:S(2)}, u32[]{:S(2)}) collective-permute-start(bf16[816,128]{1,0:T(8,128)(2,1)} %get-tuple-element.39), channel_id=1, source_target_pairs={{0,6},{1,7},{2,4},{3,5},{4,2},{5,3},{6,0},{7,1},{8,14},{9,15},{10,... | collective-permute-start | bytes 626696 | tf_op jit(solution)/shard_map/ppermute | solution.py:26
  62.7 3.7 %copy-start.11 = (bf16[1088,128]{1,0:T(8,128)(2,1)}, bf16[1088,128]{1,0:T(8,128)(2,1)S(1)}, u32[]{:S(2)}) copy-start(bf16[1088,128]{1,0:T(8,128)(2,1)S(1)} %collective-permute-done.6.refs_5_) | copy-start | bytes 835588
  62.7 25.4 %collective-permute-start.11 = (bf16[816,128]{1,0:T(8,128)(2,1)}, bf16[816,128]{1,0:T(8,128)(2,1)}, u32[]{:S(2)}, u32[]{:S(2)}) collective-permute-start(bf16[816,128]{1,0:T(8,128)(2,1)} %get-tuple-element.39), channel_id=1, source_target_pairs={{0,5},{1,4},{2,7},{3,6},{4,1},{5,0},{6,3},{7,2},{8,13},{9,12},{10,... | collective-permute-start | bytes 626696 | tf_op jit(solution)/shard_map/ppermute | solution.py:26
  65.2 1.2 %copy-start.12 = (bf16[1088,128]{1,0:T(8,128)(2,1)}, bf16[1088,128]{1,0:T(8,128)(2,1)S(1)}, u32[]{:S(2)}) copy-start(bf16[1088,128]{1,0:T(8,128)(2,1)S(1)} %collective-permute-done.5.refs_4_) | copy-start | bytes 835588
  65.2 26.3 %collective-permute-start.10 = (bf16[816,128]{1,0:T(8,128)(2,1)}, bf16[816,128]{1,0:T(8,128)(2,1)}, u32[]{:S(2)}, u32[]{:S(2)}) collective-permute-start(bf16[816,128]{1,0:T(8,128)(2,1)} %get-tuple-element.39), channel_id=1, source_target_pairs={{0,4},{1,5},{2,6},{3,7},{4,0},{5,1},{6,2},{7,3},{8,12},{9,13},{10,... | collective-permute-start | bytes 626696 | tf_op jit(solution)/shard_map/ppermute | solution.py:26
  72.7 1.3 %copy-start.16 = (bf16[816,128]{1,0:T(8,128)(2,1)}, bf16[816,128]{1,0:T(8,128)(2,1)S(1)}, u32[]{:S(2)}) copy-start(bf16[816,128]{1,0:T(8,128)(2,1)S(1)} %collective-permute-done.13.refs_9_) | copy-start | bytes 626692
  72.7 30.6 %collective-permute-start.8 = (bf16[1536,128]{1,0:T(8,128)(2,1)}, bf16[1536,128]{1,0:T(8,128)(2,1)S(1)}, u32[]{:S(2)}, u32[]{:S(2)}) collective-permute-start(bf16[1536,128]{1,0:T(8,128)(2,1)} %shard_map.97.refs_4_), channel_id=1, source_target_pairs={{0,16},{8,24},{16,0},{24,8},{1,17},{9,25},{17,1},{25,9},{2,18},{10... | collective-permute-start | bytes 1179656 | tf_op jit(solution)/shard_map/ppermute | solution.py:26
  74.0 0.7 copy-start.17
  74.0 32.2 %collective-permute-start.1 = (bf16[3072,128]{1,0:T(8,128)(2,1)}, bf16[3072,128]{1,0:T(8,128)(2,1)S(1)}, u32[]{:S(2)}, u32[]{:S(2)}) collective-permute-start(bf16[3072,128]{1,0:T(8,128)(2,1)} %shard_map.96.refs_0_), channel_id=1, source_target_pairs={{0,8},{8,0},{16,24},{24,16},{1,9},{9,1},{17,25},{25,17},{2,10},{10... | collective-permute-start | bytes 2359304 | tf_op jit(solution)/shard_map/ppermute | solution.py:26
  74.7 32.3 %copy-start = (bf16[3072,128]{1,0:T(8,128)(2,1)}, bf16[3072,128]{1,0:T(8,128)(2,1)S(1)}, u32[]{:S(2)}) copy-start(bf16[3072,128]{1,0:T(8,128)(2,1)S(1)} %collective-permute-done.2.refs_2_) | copy-start | bytes 2359300
  74.7 32.3 %collective-permute-start.3 = (bf16[3072,128]{1,0:T(8,128)(2,1)S(1)}, bf16[3072,128]{1,0:T(8,128)(2,1)S(1)}, u32[]{:S(2)}, u32[]{:S(2)}) collective-permute-start(bf16[3072,128]{1,0:T(8,128)(2,1)S(1)} %collective-permute-done.2.refs_2_), channel_id=1, source_target_pairs={{0,8},{8,0},{16,24},{24,16},{1,9},{9,1},{17,25},{25,17},{2,10},{10... | collective-permute-start | bytes 2359304 | tf_op jit(solution)/shard_map/ppermute | solution.py:26
  95.6 7.7 %collective-permute-start.18 = (bf16[1152,128]{1,0:T(8,128)(2,1)}, bf16[1152,128]{1,0:T(8,128)(2,1)S(1)}, u32[]{:S(2)}, u32[]{:S(2)}) collective-permute-start(bf16[1152,128]{1,0:T(8,128)(2,1)} %shard_map.99.refs_8_), channel_id=1, source_target_pairs={{0,16},{8,24},{16,0},{24,8},{1,17},{9,25},{17,1},{25,9},{2,18},{10... | collective-permute-start | bytes 884744 | tf_op jit(solution)/shard_map/ppermute | solution.py:26
  96.1 7.8 %collective-permute-start.17 = (bf16[1152,128]{1,0:T(8,128)(2,1)}, bf16[1152,128]{1,0:T(8,128)(2,1)S(1)}, u32[]{:S(2)}, u32[]{:S(2)}) collective-permute-start(bf16[1152,128]{1,0:T(8,128)(2,1)} %shard_map.99.refs_8_), channel_id=1, source_target_pairs={{0,8},{8,0},{16,24},{24,16},{1,9},{9,1},{17,25},{25,17},{2,10},{10... | collective-permute-start | bytes 884744 | tf_op jit(solution)/shard_map/ppermute | solution.py:26
  103.3 2.9 %copy-start.7 = (bf16[1152,128]{1,0:T(8,128)(2,1)}, bf16[1152,128]{1,0:T(8,128)(2,1)S(1)}, u32[]{:S(2)}) copy-start(bf16[1152,128]{1,0:T(8,128)(2,1)S(1)} %collective-permute-done.18.refs_10_) | copy-start | bytes 884740
  103.3 1.9 %collective-permute-start.7 = (bf16[1536,128]{1,0:T(8,128)(2,1)}, bf16[1536,128]{1,0:T(8,128)(2,1)S(1)}, u32[]{:S(2)}, u32[]{:S(2)}) collective-permute-start(bf16[1536,128]{1,0:T(8,128)(2,1)} %shard_map.97.refs_4_), channel_id=1, source_target_pairs={{0,8},{8,0},{16,24},{24,16},{1,9},{9,1},{17,25},{25,17},{2,10},{10... | collective-permute-start | bytes 1179656 | tf_op jit(solution)/shard_map/ppermute | solution.py:26
  103.3 3.6 %copy-start.4 = (bf16[1536,128]{1,0:T(8,128)(2,1)}, bf16[1536,128]{1,0:T(8,128)(2,1)S(1)}, u32[]{:S(2)}) copy-start(bf16[1536,128]{1,0:T(8,128)(2,1)S(1)} %collective-permute-done.8.refs_6_) | copy-start | bytes 1179652
  103.4 2.9 %collective-permute-start.9 = (bf16[1536,128]{1,0:T(8,128)(2,1)S(1)}, bf16[1536,128]{1,0:T(8,128)(2,1)S(1)}, u32[]{:S(2)}, u32[]{:S(2)}) collective-permute-start(bf16[1536,128]{1,0:T(8,128)(2,1)S(1)} %collective-permute-done.8.refs_6_), channel_id=1, source_target_pairs={{0,8},{8,0},{16,24},{24,16},{1,9},{9,1},{17,25},{25,17},{2,10},{10... | collective-permute-start | bytes 1179656 | tf_op jit(solution)/shard_map/ppermute | solution.py:26
  103.9 2.4 %copy-start.8 = (bf16[1152,128]{1,0:T(8,128)(2,1)}, bf16[1152,128]{1,0:T(8,128)(2,1)S(1)}, u32[]{:S(2)}) copy-start(bf16[1152,128]{1,0:T(8,128)(2,1)S(1)} %collective-permute-done.17.refs_9_) | copy-start | bytes 884740
  103.9 2.4 %collective-permute-start.19 = (bf16[1152,128]{1,0:T(8,128)(2,1)S(1)}, bf16[1152,128]{1,0:T(8,128)(2,1)S(1)}, u32[]{:S(2)}, u32[]{:S(2)}) collective-permute-start(bf16[1152,128]{1,0:T(8,128)(2,1)S(1)} %collective-permute-done.18.refs_10_), channel_id=1, source_target_pairs={{0,8},{8,0},{16,24},{24,16},{1,9},{9,1},{17,25},{25,17},{2,10},{10... | collective-permute-start | bytes 884744 | tf_op jit(solution)/shard_map/ppermute | solution.py:26
  105.3 1.7 %copy-start.5 = (bf16[1536,128]{1,0:T(8,128)(2,1)}, bf16[1536,128]{1,0:T(8,128)(2,1)S(1)}, u32[]{:S(2)}) copy-start(bf16[1536,128]{1,0:T(8,128)(2,1)S(1)} %collective-permute-done.7.refs_5_) | copy-start | bytes 1179652
  106.3 0.7 copy-start.9
  106.3 0.9 copy-start.6
  107.0 0.9 copy-start.1
  107.9 0.9 copy-start.2

commit v2 on v1

--- a/solution.py
+++ b/solution.py
@@ -12,8 +12,11 @@
 SEG = 2048
 LEVELS = 4
 GROUPS = ((0,), (1,), (2, 3))
+SENDS = ((0,), (1, 2, 3))
+VMEM_LIMIT = 24 * 1024 * 1024
 LANES = 128
-TAG_ROWS = 16
+TAG_ROWS = 8
+PAIR = 16
 LOG2E = math.log2(math.e)
 
 
@@ -40,7 +43,7 @@
         self.rows = local_tokens // self.rate
         self.span = min(SEG, all_tokens // self.rate) * self.rate // local_tokens
         self.bits = self.span.bit_length() - 1
-        self.tags = self.rows // LANES * TAG_ROWS
+        self.tags = max(self.rows // LANES * TAG_ROWS, PAIR)
         self.pack_rows = 2 * self.rows + self.tags
 
 
@@ -71,7 +74,7 @@
             send_refs[group, bit] = refs[at]
             at += 1
     bufs = refs[at : at + n]
-    turned, sems = refs[at + n :]
+    turned, logs_buf, logs_sem, sems = refs[at + n :]
     rho, seq = lax.axis_index("rate"), lax.axis_index("seq")
     tokens = keys.shape[0]
     sources = (keys, values, queries, grads, outs)
@@ -85,8 +88,12 @@
             copy = pltpu.make_async_copy(picked, bufs[w].at[s], sems.at[w, s])
             copy.start()
             copies.append(copy)
+        if w == 0:
+            logs_copy = pltpu.make_async_copy(logs, logs_buf, logs_sem)
+            logs_copy.start()
+    logs_copy.wait()
     for u in range(tokens // LANES):
-        part = logs[:, u * LANES : (u + 1) * LANES]
+        part = logs_buf[:, u * LANES : (u + 1) * LANES]
         square = jnp.concatenate([part, jnp.zeros((LANES - HEADS, LANES), F32)], axis=0)
         turned[u * LANES : (u + 1) * LANES, :] = square.T
     row_id = lax.broadcasted_iota(jnp.int32, (LANES, 2 * LANES), 0)
@@ -101,6 +108,7 @@
         pick = (col_id == 2 * row_id + head % 2).astype(BF16)
         for s in range(len(sources)):
             copies[w * len(sources) + s].wait()
+        tops = []
         flat = [bufs[w].at[s].reshape(2 * lv.rows, LANES) for s in range(len(sources))]
         for u in range(lv.rows // LANES):
             got = [
@@ -118,8 +126,7 @@
             for at, col in enumerate(split3(total) + split3(delta) + (total, delta)):
                 square = jnp.where(lane == at, col, square)
             col_refs[w][u * LANES : (u + 1) * LANES, :] = square
-            tags = square.T[:TAG_ROWS].astype(BF16)
-            tag_refs[w][u * TAG_ROWS : (u + 1) * TAG_ROWS, :] = tags
+            tops.append(square.T[:TAG_ROWS])
             low = [g.astype(BF16) for g in got[:4]]
             for s in range(4):
                 own_refs[w][s * lv.rows + u * LANES : s * lv.rows + (u + 1) * LANES, :] = low[s]
@@ -130,8 +137,13 @@
                 for s in range(2):
                     first = base + s * lv.rows + u * LANES
                     send[first : first + LANES, :] = jnp.where(later, low[2 + s], low[s])
-                first = base + 2 * lv.rows + u * TAG_ROWS
-                send[first : first + TAG_ROWS, :] = tags
+        if len(tops) == 1:
+            tops.append(jnp.zeros((TAG_ROWS, LANES), F32))
+        tags = jnp.concatenate(tops, axis=0).astype(BF16)
+        tag_refs[w][...] = tags
+        for bit in range(lv.bits):
+            first = pack_layout(levels, group, bit)[0][level] + 2 * lv.rows
+            send_refs[group, bit][first : first + lv.tags, :] = tags
 
 
 def group_bits(levels, group):
@@ -158,21 +170,29 @@
         kernel,
         out_shape=shapes,
         in_specs=[pl.BlockSpec(memory_space=pltpu.SMEM)]
-        + [pl.BlockSpec(memory_space=pl.ANY)] * 5
-        + [pl.BlockSpec(memory_space=pltpu.VMEM)],
+        + [pl.BlockSpec(memory_space=pltpu.HBM)] * 6,
         scratch_shapes=[pltpu.VMEM((5, levels[m].rows, 2, LANES), BF16) for m in members]
-        + [pltpu.VMEM((tokens, LANES), F32), pltpu.SemaphoreType.DMA((n, 5))],
-    )(sm, *sources, logs)
+        + [
+            pltpu.VMEM((tokens, LANES), F32),
+            pltpu.VMEM(logs.shape, F32),
+            pltpu.SemaphoreType.DMA,
+            pltpu.SemaphoreType.DMA((n, 5)),
+        ],
+        compiler_params=pltpu.CompilerParams(vmem_limit_bytes=VMEM_LIMIT),
+    )(sm, *[pltpu.with_memory_space_constraint(a, pltpu.HBM) for a in (*sources, logs)])
     kept = {m: (results[w], results[n + w], results[2 * n + w]) for w, m in enumerate(members)}
     return kept, dict(zip(sent, results[3 * n :]))
 
 
-def tag_row(tags, first_row, count, which):
+def tag_row(tags, base, first_row, count, which):
     parts = []
+    tile = None
     for u in range(count // LANES):
-        at = pl.multiple_of(first_row // LANES * TAG_ROWS + u * TAG_ROWS, TAG_ROWS)
-        tile = tags[pl.ds(at, TAG_ROWS), :].astype(F32)
-        parts.append(tile[which : which + 1] + tile[which + 1 : which + 2] + tile[which + 2 : which + 3])
+        if u % 2 == 0:
+            at = pl.multiple_of(base + first_row // LANES * TAG_ROWS + u * TAG_ROWS, PAIR)
+            tile = tags[pl.ds(at, PAIR), :].astype(F32)
+        at = u % 2 * TAG_ROWS + which
+        parts.append(tile[at : at + 1] + tile[at + 1 : at + 2] + tile[at + 2 : at + 3])
     return parts[0] if len(parts) == 1 else jnp.concatenate(parts, axis=1)
 
 
@@ -202,13 +222,12 @@
 
     def pair(self, at, tile):
         def load(base):
-            return self.ref[pl.ds(pl.multiple_of(base + at, TAG_ROWS), tile), :]
+            return self.ref[pl.ds(pl.multiple_of(base + at, PAIR), tile), :]
 
         return load(self.first), load(self.second)
 
     def tags(self, at, tile):
-        base = self.tag_base // TAG_ROWS * LANES
-        return tag_row(self.tag_ref, base + at, tile, 0), tag_row(self.tag_ref, base + at, tile, 3)
+        return tuple(tag_row(self.tag_ref, self.tag_base, at, tile, which) for which in (0, 3))
 
 
 def run_tiles(count, tile, step):
@@ -234,7 +253,7 @@
 
     def put(self, which, at, value, add):
         first = self.at + which * self.rows + at
-        where = pl.ds(pl.multiple_of(first, TAG_ROWS), self.tile)
+        where = pl.ds(pl.multiple_of(first, PAIR), self.tile)
         if add:
             self.acc[where, :] += value
         else:
@@ -297,21 +316,41 @@
         run_tiles(self.count, self.tile, step)
 
 
-def compute(levels, members, bits, kept, received, before, after, last, scaling):
+STAGES = {
+    (0,): (("first", True, slice(0, -1), (0, 1)), ("last", False, slice(-1, None), (1, 3))),
+    (1,): (("own", True, slice(0, 0), None), ("last", False, slice(0, None), (0, 3))),
+    (2, 3): (
+        ("own", True, slice(0, 0), None),
+        ("first", False, slice(0, -1), (0, 1)),
+        ("last", False, slice(-1, None), (1, 3)),
+    ),
+}
+
+
+def compute(levels, members, group, stage, kept, received, before, scaling):
     n = len(members)
+    name, own_block, chosen, parts = stage
+    more = name != "last"
+    bits_of = {m: list(range(levels[m].bits))[chosen] for m in members}
+    bits = sorted({bit for m in members for bit in bits_of[m]})
     steps = [k for k in sorted(received) if k.bit_length() - 1 in bits]
-    total_rows = 3 * sum(levels[m].rows for m in members)
+    rows_sum = sum(levels[m].rows for m in members)
     given = [kept[m][part] for part in range(3) for m in members]
     given += [received[k] for k in steps]
     if before is not None:
         given.append(before)
     inputs = len(given)
+    low, high = parts or (0, 0)
+    shapes = []
+    if parts:
+        shapes.append(jax.ShapeDtypeStruct(((high - low) * rows_sum, LANES), BF16))
+    if more:
+        shapes.append(jax.ShapeDtypeStruct((3 * rows_sum, LANES), F32))
 
     def kernel(*refs):
         own_refs, tag_refs, col_refs = refs[:n], refs[n : 2 * n], refs[2 * n : 3 * n]
         got = dict(zip(steps, refs[3 * n :]))
-        out = refs[inputs + len(after)]
-        acc = refs[inputs + len(after) + 1] if last else out
+        out, acc = refs[inputs], refs[inputs + (1 if parts else 0)]
         seq = lax.axis_index("seq")
         if before is not None:
             acc[...] = refs[inputs - 1][...]
@@ -320,15 +359,15 @@
             lv = levels[level]
             work.append(LevelWork(lv, own_refs[w], tag_refs[w], col_refs[w], acc, at, scaling))
             at += 3 * lv.rows
-        if before is None:
+        if own_block:
             for each in work:
                 each.diagonal()
         for bit in bits:
             later = (seq >> bit) % 2 == 1
-            offsets = pack_layout(levels, members, bit)[0]
+            offsets = pack_layout(levels, group, bit)[0]
             todo = []
             for w, level in enumerate(members):
-                if level in offsets:
+                if bit in bits_of[level]:
                     rows, base = levels[level].rows, offsets[level]
                     todo.append(
                         (
@@ -350,74 +389,87 @@
                 for each, blocks in todo:
                     each.later_queries(blocks)
 
-        if last:
-            at = 0
-            for level in members:
-                rows = levels[level].rows
-                out[at : at + 2 * rows, :] = (acc[at : at + 2 * rows, :] * scaling).astype(BF16)
-                out[at + 2 * rows : at + 3 * rows, :] = acc[at + 2 * rows : at + 3 * rows, :].astype(BF16)
-                at += 3 * rows
+        at, put = 0, 0
+        for level in members:
+            lv = levels[level]
+            top = (seq >> (lv.bits - 1)) % 2 == 1
+            for place_at in range(low, high):
+                when_low, when_high = place_at, (place_at + 2) % 3
+                value = jnp.where(
+                    top,
+                    acc[at + when_high * lv.rows : at + (when_high + 1) * lv.rows, :],
+                    acc[at + when_low * lv.rows : at + (when_low + 1) * lv.rows, :],
+                )
+                factor = jnp.where(
+                    top, 1.0 if when_high == 2 else scaling, 1.0 if when_low == 2 else scaling
+                )
+                out[put : put + lv.rows, :] = (value * factor).astype(BF16)
+                put += lv.rows
+            at += 3 * lv.rows
 
     return pl.pallas_call(
         kernel,
-        out_shape=jax.ShapeDtypeStruct((total_rows, LANES), BF16 if last else F32),
-        in_specs=[pl.BlockSpec(memory_space=pltpu.VMEM)] * inputs
-        + [pl.BlockSpec(memory_space=pl.ANY)] * len(after),
-        scratch_shapes=[pltpu.VMEM((total_rows, LANES), F32)] if last else [],
-    )(*given, *after)
+        out_shape=shapes,
+        in_specs=[pl.BlockSpec(memory_space=pltpu.VMEM)] * inputs,
+        scratch_shapes=[] if more else [pltpu.VMEM((3 * rows_sum, LANES), F32)],
+        compiler_params=pltpu.CompilerParams(vmem_limit_bytes=VMEM_LIMIT),
+    )(*given)
 
 
 def place(levels, group_size, heads_here, local_tokens, sm, gathered):
-    rates = len(gathered[0])
-    flat = [array for group in gathered for array in group]
-    block, half = LANES, LANES // 2
+    rates = len(gathered[0][0][2])
+    flat = [array for pieces in gathered for piece in pieces for array in piece[2]]
+    block, half = 2 * LANES, LANES // 2
+    parts = block // half
     steps = local_tokens // block
     tall = heads_here * half
 
     def kernel(sm_ref, *refs):
         sources = refs[: len(flat)]
         outs = refs[len(flat) : len(flat) + 3]
-        spread, buf, sems = refs[len(flat) + 3 :]
+        spread, buf, table, sems = refs[len(flat) + 3 :]
         step = pl.program_id(0)
         rho = lax.axis_index("rate")
-        slots = []
-        for i in range(heads_here):
-            slot = jnp.int32(0)
-            for s in range(HEADS):
-                slot = jnp.where(sm_ref[s] == rho * heads_here + i, s, slot)
-            slots.append(slot)
-        shifts = [slot // group_size for slot in slots]
 
         @pl.when(step == 0)
         def _():
+            slots = []
+            for i in range(heads_here):
+                slot = jnp.int32(0)
+                for s in range(HEADS):
+                    slot = jnp.where(sm_ref[s] == rho * heads_here + i, s, slot)
+                slots.append(slot)
+                table[i] = slot // group_size
+            shifts = [slot // group_size for slot in slots]
             for i in range(heads_here):
                 for level in range(1, LEVELS):
                     end = 3 * levels[level].rows
-                    buf[i, end : end + block, :] = jnp.zeros((block, LANES), BF16)
-
-            def each(act):
-                for i in range(heads_here):
-                    lane_i = slots[i] % group_size
-                    for g, members in enumerate(GROUPS):
-                        at = 0
-                        for level in members:
-                            rows = 3 * levels[level].rows
-                            for x in range(rates):
-                                hit = jnp.logical_and(shifts[i] == level, lane_i == rho ^ x)
-
-                                @pl.when(hit)
-                                def _(i=i, g=g, x=x, at=at, rows=rows):
-                                    act(
-                                        pltpu.make_async_copy(
-                                            sources[g * rates + x].at[pl.ds(at, rows)],
-                                            buf.at[i, pl.ds(0, rows)],
-                                            sems.at[i],
-                                        )
-                                    )
-
-                            at += rows
-
-            each(lambda copy: copy.start())
+                    buf[i, end : end + half, :] = jnp.zeros((half, LANES), BF16)
+
+            for i in range(heads_here):
+                lane_i = slots[i] % group_size
+                first = 0
+                for g, members in enumerate(GROUPS):
+                    above = 0
+                    for level in members:
+                        rows = levels[level].rows
+                        for x in range(rates):
+                            hit = jnp.logical_and(shifts[i] == level, lane_i == rho ^ x)
+
+                            @pl.when(hit)
+                            def _(i=i, pieces=gathered[g], first=first, x=x, above=above, rows=rows):
+                                for p, (low, high, _) in enumerate(pieces):
+                                    source = sources[first + p * rates + x]
+                                    size = (high - low) * rows
+                                    pltpu.make_async_copy(
+                                        source.at[pl.ds(above * (high - low), size)],
+                                        buf.at[i, pl.ds(low * rows, size)],
+                                        sems.at[i],
+                                    ).start()
+
+                        above += rows
+                    first += rates * len(gathered[g])
+
             row_id = lax.broadcasted_iota(jnp.int32, (tall, half), 0)
             col_id = lax.broadcasted_iota(jnp.int32, (tall, half), 1)
             for part in range(2):
@@ -428,22 +480,41 @@
                     token = col_id * rate + (off - first)
                     hit = row_id == token * heads_here + i
                     spread[part, :, i * half : (i + 1) * half] = hit.astype(BF16)
-            each(lambda copy: copy.wait())
-
-        for part in range(2):
+            for i in range(heads_here):
+                for level in range(LEVELS):
+                    rows = 3 * levels[level].rows
+
+                    @pl.when(shifts[i] == level)
+                    def _(i=i, rows=rows):
+                        there = buf.at[i, pl.ds(0, rows)]
+                        pltpu.make_async_copy(there, there, sems.at[i]).wait()
+
+        shifts = [table[i] for i in range(heads_here)]
+        seq = lax.axis_index("seq")
+        tops = []
+        for i in range(heads_here):
+            top = jnp.int32(0)
+            for level in range(LEVELS):
+                bit = (seq >> (levels[level].bits - 1)) & 1
+                top = jnp.where(shifts[i] == level, bit, top)
+            tops.append(top)
+
+        for part in range(parts):
             columns = []
             for which in range(3):
                 rows = []
                 for i in range(heads_here):
-                    at = which * (local_tokens >> shifts[i]) + step * (block >> shifts[i])
-                    at += jnp.where(shifts[i] == 0, part * half, 0)
-                    rows.append(buf[i, pl.ds(pl.multiple_of(at, TAG_ROWS), half), :])
+                    turned = jnp.where(tops[i] == 1, (which + 1) % 3, which)
+                    at = turned * (local_tokens >> shifts[i]) + step * (block >> shifts[i])
+                    at += part // 2 * (2 * half >> shifts[i])
+                    at += jnp.where(shifts[i] == 0, part % 2 * half, 0)
+                    rows.append(buf[i, pl.ds(pl.multiple_of(at, PAIR), half), :])
                 columns.append(jnp.concatenate(rows, axis=0))
-            two = plain_dot(spread[part], jnp.concatenate(columns[:2], axis=1))
+            two = plain_dot(spread[part % 2], jnp.concatenate(columns[:2], axis=1))
             where = pl.ds(part * tall, tall)
             outs[0][where, :] = two[:, :LANES].astype(BF16)
             outs[1][where, :] = two[:, LANES:].astype(BF16)
-            outs[2][where, :] = plain_dot(spread[part], columns[2]).astype(BF16)
+            outs[2][where, :] = plain_dot(spread[part % 2], columns[2]).astype(BF16)
 
     shape = jax.ShapeDtypeStruct((local_tokens * heads_here, LANES), BF16)
     spec = pl.BlockSpec((block * heads_here, LANES), lambda i: (i, 0))
@@ -457,8 +528,10 @@
         scratch_shapes=[
             pltpu.VMEM((2, tall, tall), BF16),
             pltpu.VMEM((heads_here, 3 * local_tokens + block, LANES), BF16),
+            pltpu.SMEM((heads_here,), jnp.int32),
             pltpu.SemaphoreType.DMA((heads_here,)),
         ],
+        compiler_params=pltpu.CompilerParams(vmem_limit_bytes=VMEM_LIMIT),
         name="place",
     )(sm, *flat)
     return tuple(r.reshape(local_tokens, heads_here, LANES) for r in results)
@@ -476,36 +549,27 @@
         for a in (key_rows, values, queries, out_grad, attn_out)
     ]
     logs = log_totals.T
-    kept, received = {}, {}
-    for groups in (GROUPS[:1], GROUPS[1:]):
-        some, sends = extract(levels, groups, group_size, assignment, paired, logs)
+    received = {}
+    kept = {}
+    for group in SENDS:
+        some, sends = extract(levels, (group,), group_size, assignment, paired, logs)
         kept.update(some)
-        for members in groups:
-            received[members] = {}
-            for k in range(1, 2 ** group_bits(levels, members)):
-                got = swapped(sends[members, k.bit_length() - 1], "seq", k)
-                received[members][k] = got
+        received[group] = {}
+        for k in range(1, 2 ** group_bits(levels, group)):
+            received[group][k] = swapped(sends[group, k.bit_length() - 1], "seq", k)
     gathered = []
     for members in GROUPS:
-        bits = list(range(group_bits(levels, members)))
-        after = [kept[GROUPS[-1][-1]][1]] if members == GROUPS[0] else []
-        split = 2 if len(bits) > 2 else len(bits)
-        mine = None
-        for part in (bits[:split], bits[split:]):
-            if part:
-                mine = compute(
-                    levels,
-                    members,
-                    part,
-                    kept,
-                    received[members],
-                    mine,
-                    after,
-                    part[-1] == bits[-1],
-                    scaling,
-                )
-        far = swapped(mine, "rate", 2)
-        gathered.append([mine, swapped(mine, "rate", 1), far, swapped(far, "rate", 1)])
+        group = next(g for g in SENDS if members[0] in g)
+        pieces, before = [], None
+        for stage in STAGES[members]:
+            results = compute(levels, members, group, stage, kept, received[group], before, scaling)
+            before = results[-1]
+            if stage[3]:
+                mine = results[0]
+                far = swapped(mine, "rate", 2)
+                near = swapped(mine, "rate", 1)
+                pieces.append((*stage[3], [mine, near, far, swapped(far, "rate", 1)]))
+        gathered.append(pieces)
     return place(levels, group_size, HEADS // rate_count, local_tokens, assignment, gathered)
 
 

time: 116 us -> 93 us (0.80)
  Pallas kernels: 43.1 us -> 30.3 us
  waiting for transfers between devices: 40.2 us -> 35.3 us
  local copies, waits for them, and re-layouts: 3.97 us -> 0.66 us
  starting transfers between devices: 27.5 us -> 25.5 us
    pallas_call x4 -> x7, Pallas kernels: 24.4 us -> 15.2 us  [compute(): pl.pallas_call(kernel, out_shape=shapes, in_specs=[pl.BlockSpec(memory_sp...]
    ppermute x20 -> x23, waiting for transfers between devices: 40.2 us -> 35.3 us  [swapped(): return lax.ppermute(array, axis, [(i, i ^ by) for i in range(devices)])]
    unnamed x36 -> x4, local copies, waits for them, and re-layouts: 3.97 us -> 0.66 us
    pallas_call x2, Pallas kernels: 11.9 us -> 9.63 us  [extract(): pl.pallas_call(kernel, out_shape=shapes, in_specs=[pl.BlockSpec(memory_sp...]
    ppermute x20 -> x23, starting transfers between devices: 27.5 us -> 25.5 us  [swapped(): return lax.ppermute(array, axis, [(i, i ^ by) for i in range(devices)])]
    pallas_call x1, Pallas kernels: 6.81 us -> 5.46 us  [place(): pl.pallas_call(kernel, grid=(steps,), out_shape=[shape] * 3, in_specs=[pl...]
  transfers between devices with their start and end apart: 20 -> 23, of which waited for: 9 -> 9; matrix products, arithmetic and copies ran while one was open for 0% -> 0% of each run, Pallas kernels for 18% -> 22%
where the time goes in v2:
time: 93 us; the launch traced here: 92.8 us
  waiting for transfers between devices  35.3 us (38%)
  Pallas kernels  30.3 us (33%)
  starting transfers between devices  25.5 us (27%)
  between operations  0.94 us (1%)
    ppermute x23, waiting for transfers between devices, swapped(): return lax.ppermute(array, axis, [(i, i ^ by) for i in range(devices)])  35.3 us
    ppermute x23, starting transfers between devices, swapped(): return lax.ppermute(array, axis, [(i, i ^ by) for i in range(devices)])  25.5 us
    pallas_call x7, Pallas kernels, compute(): pl.pallas_call(kernel, out_shape=shapes, in_specs=[pl.BlockSpec(memory_sp...  15.2 us
    pallas_call x2, Pallas kernels, extract(): pl.pallas_call(kernel, out_shape=shapes, in_specs=[pl.BlockSpec(memory_sp...  9.63 us
    pallas_call x1, Pallas kernels, place(): pl.pallas_call(kernel, grid=(steps,), out_shape=[shape] * 3, in_specs=[pl...  5.46 us
  transfers between devices with their start and end apart: 23, of which 9 were waited for; matrix products, arithmetic and copies ran while one was open for 0% of the time, Pallas kernels for 22%

profile of v2, /device:TPU:0, one launch (start us, length us, event | category | flops | bytes accessed | tf_op | source)
XLA Modules:
  0.0 92.8 jit_solution(17208823583456776043)
XLA Ops:
  0.6 0.0 copy-start
  0.6 0.6 copy-done
  1.3 4.6 %shard_map.94 = (bf16[4096,128]{1,0:T(8,128)(2,1)S(1)}, bf16[64,128]{1,0:T(8,128)(2,1)S(1)}, f32[1024,128]{1,0:T(8,128)S(1)}, bf16[2112,128]{1,0:T(8,128)(2,1)S(1)}) custom-call(s32[16]{0:T(128)S(1)} %copy-done, bf16[1024,8,2,128]{3,2,1,0:T(2,128)(2,1)} %bitcast.9, bf16[1024,8,2,128]{3,2,1,0:T(2,128)(2,1)} %bitcast.11, bf16[1024,8,2,128]{3,2,1,0:T(2,128)(2,1)} %bitcast.13, ...), custom_call_target="tpu_custom_call" | custom-call | tf_op jit(solution)/shard_map/pallas_call | solution.py:169
  5.9 3.0 %collective-permute-start.3 = (bf16[2112,128]{1,0:T(8,128)(2,1)S(1)}, bf16[2112,128]{1,0:T(8,128)(2,1)S(1)}, u32[]{:S(2)}, u32[]{:S(2)}) collective-permute-start(bf16[2112,128]{1,0:T(8,128)(2,1)S(1)} %get-tuple-element.30), channel_id=1, source_target_pairs={{0,1},{1,0},{2,3},{3,2},{4,5},{5,4},{6,7},{7,6},{8,9},{9,8},{10,11... | collective-permute-start | bytes 1622024 | tf_op jit(solution)/shard_map/ppermute | solution.py:29
  8.9 5.0 %shard_map.97 = (bf16[2048,128]{1,0:T(8,128)(2,1)S(1)}, bf16[1024,128]{1,0:T(8,128)(2,1)S(1)}, bf16[512,128]{1,0:T(8,128)(2,1)S(1)}, bf16[32,128]{1,0:T(8,128)(2...) custom-call(s32[16]{0:T(128)S(1)} %copy-done, ...), custom_call_target="tpu_custom_call" | custom-call | tf_op jit(solution)/shard_map/pallas_call | solution.py:169
  14.0 3.6 %collective-permute-start.19 = (bf16[800,128]{1,0:T(8,128)(2,1)S(1)}, bf16[800,128]{1,0:T(8,128)(2,1)S(1)}, u32[]{:S(2)}, u32[]{:S(2)}) collective-permute-start(bf16[800,128]{1,0:T(8,128)(2,1)S(1)} %get-tuple-element.44), channel_id=1, source_target_pairs={{0,7},{1,6},{2,5},{3,4},{4,3},{5,2},{6,1},{7,0},{8,15},{9,14},{10,... | collective-permute-start | bytes 614408 | tf_op jit(solution)/shard_map/ppermute | solution.py:29
  17.6 1.5 %collective-permute-start.7 = (bf16[1856,128]{1,0:T(8,128)(2,1)S(1)}, bf16[1856,128]{1,0:T(8,128)(2,1)S(1)}, u32[]{:S(2)}, u32[]{:S(2)}) collective-permute-start(bf16[1856,128]{1,0:T(8,128)(2,1)S(1)} %get-tuple-element.35), channel_id=1, source_target_pairs={{0,1},{1,0},{2,3},{3,2},{4,5},{5,4},{6,7},{7,6},{8,9},{9,8},{10,11... | collective-permute-start | bytes 1425416 | tf_op jit(solution)/shard_map/ppermute | solution.py:29
  19.1 2.0 %collective-permute-start.8 = (bf16[1856,128]{1,0:T(8,128)(2,1)S(1)}, bf16[1856,128]{1,0:T(8,128)(2,1)S(1)}, u32[]{:S(2)}, u32[]{:S(2)}) collective-permute-start(bf16[1856,128]{1,0:T(8,128)(2,1)S(1)} %get-tuple-element.36), channel_id=1, source_target_pairs={{0,2},{1,3},{2,0},{3,1},{4,6},{5,7},{6,4},{7,5},{8,10},{9,11},{10,... | collective-permute-start | bytes 1425416 | tf_op jit(solution)/shard_map/ppermute | solution.py:29
  21.1 3.3 %shard_map.95 = (bf16[1024,128]{1,0:T(8,128)(2,1)S(1)}, f32[3072,128]{1,0:T(8,128)S(1)}) custom-call(bf16[4096,128]{1,0:T(8,128)(2,1)S(1)} %get-tuple-element.26.refs_0_, bf16[64,128]{1,0:T(8,128)(2,1)S(1)} %get-tuple-element.27.refs_1_, f32[1024,128]{1,0:T(8,128)S(1)} %get-tuple-element.28.refs_2_), custom_call_target="tpu_custom_call" | custom-call | tf_op jit(solution)/shard_map/pallas_call | solution.py:410
  24.4 0.2 collective-permute-done.19.refs_9_
  24.7 1.6 %collective-permute-start.1 = (bf16[1024,128]{1,0:T(8,128)(2,1)S(1)}, bf16[1024,128]{1,0:T(8,128)(2,1)S(1)}, u32[]{:S(2)}, u32[]{:S(2)}) collective-permute-start(bf16[1024,128]{1,0:T(8,128)(2,1)S(1)} %get-tuple-element.29.refs_0_), channel_id=1, source_target_pairs={{0,16},{8,24},{16,0},{24,8},{1,17},{9,25},{17,1},{25,9},{2,18},{10... | collective-permute-start | bytes 786440 | tf_op jit(solution)/shard_map/ppermute | solution.py:29
  26.2 10.4 %collective-permute-done.3.refs_3_ = bf16[2112,128]{1,0:T(8,128)(2,1)S(1)} collective-permute-done((bf16[2112,128]{1,0:T(8,128)(2,1)S(1)}, bf16[2112,128]{1,0:T(8,128)(2,1)S(1)}, u32[]{:S(2)}, u32[]{:S(2)}) %collective-permute-start.3) | collective-permute-done | bytes 540704 | tf_op jit(solution)/shard_map/ppermute | solution.py:29
  36.6 4.1 %collective-permute-start.18 = (bf16[800,128]{1,0:T(8,128)(2,1)S(1)}, bf16[800,128]{1,0:T(8,128)(2,1)S(1)}, u32[]{:S(2)}, u32[]{:S(2)}) collective-permute-start(bf16[800,128]{1,0:T(8,128)(2,1)S(1)} %get-tuple-element.44), channel_id=1, source_target_pairs={{0,6},{1,7},{2,4},{3,5},{4,2},{5,3},{6,0},{7,1},{8,14},{9,15},{10,... | collective-permute-start | bytes 614408 | tf_op jit(solution)/shard_map/ppermute | solution.py:29
  40.8 3.6 %shard_map.96.refs_4_ = bf16[2048,128]{1,0:T(8,128)(2,1)S(1)} custom-call(bf16[4096,128]{1,0:T(8,128)(2,1)S(1)} %get-tuple-element.26.refs_0_, bf16[64,128]{1,0:T(8,128)(2,1)S(1)} %get-tuple-element.27.refs_1_, f32[1024,128]{1,0:T(8,128)S(1)} %get-tuple-element.28.refs_2_, bf16[2112,128]{1,0:T(8,128)(2,1)S(1)} %collective-permute-done.3.refs_3_, ...), custom_call_target="tpu_custom_call" | custom-call | tf_op jit(solution)/shard_map/pallas_call | solution.py:410
  44.3 5.2 %collective-permute-done.18.refs_8_ = bf16[800,128]{1,0:T(8,128)(2,1)S(1)} collective-permute-done((bf16[800,128]{1,0:T(8,128)(2,1)S(1)}, bf16[800,128]{1,0:T(8,128)(2,1)S(1)}, u32[]{:S(2)}, u32[]{:S(2)}) %collective-permute-start.18) | collective-permute-done | bytes 204832 | tf_op jit(solution)/shard_map/ppermute | solution.py:29
  49.5 1.4 %collective-permute-start.5 = (bf16[2048,128]{1,0:T(8,128)(2,1)S(1)}, bf16[2048,128]{1,0:T(8,128)(2,1)S(1)}, u32[]{:S(2)}, u32[]{:S(2)}) collective-permute-start(bf16[2048,128]{1,0:T(8,128)(2,1)S(1)} %shard_map.96.refs_4_), channel_id=1, source_target_pairs={{0,16},{8,24},{16,0},{24,8},{1,17},{9,25},{17,1},{25,9},{2,18},{10... | collective-permute-start | bytes 1572872 | tf_op jit(solution)/shard_map/ppermute | solution.py:29
  51.0 0.0 collective-permute-done.1.refs_2_
  51.0 0.0 collective-permute-start.17
  51.0 0.0 collective-permute-done.7.refs_3_.refs_6_
  51.0 0.1 collective-permute-start
  51.0 0.0 collective-permute-done.9.refs_5_.refs_8_
  51.1 0.5 collective-permute-start.2
  51.6 3.7 %collective-permute-start.16 = (bf16[800,128]{1,0:T(8,128)(2,1)S(1)}, bf16[800,128]{1,0:T(8,128)(2,1)S(1)}, u32[]{:S(2)}, u32[]{:S(2)}) collective-permute-start(bf16[800,128]{1,0:T(8,128)(2,1)S(1)} %get-tuple-element.44), channel_id=1, source_target_pairs={{0,4},{1,5},{2,6},{3,7},{4,0},{5,1},{6,2},{7,3},{8,12},{9,13},{10,... | collective-permute-start | bytes 614408 | tf_op jit(solution)/shard_map/ppermute | solution.py:29
  55.2 1.1 %shard_map.98.refs_6_ = f32[1536,128]{1,0:T(8,128)S(1)} custom-call(bf16[2048,128]{1,0:T(8,128)(2,1)S(1)} %get-tuple-element.32.refs_0_, bf16[32,128]{1,0:T(8,128)(2,1)S(1)} %get-tuple-element.33.refs_1_, f32[512,128]{1,0:T(8,128)S(1)} %get-tuple-element.34.refs_2_), custom_call_target="tpu_custom_call" | custom-call | tf_op jit(solution)/shard_map/pallas_call | solution.py:410
  56.4 0.0 copy-start.1
  56.4 3.1 %shard_map.99.refs_8_ = bf16[1536,128]{1,0:T(8,128)(2,1)S(1)} custom-call(bf16[2048,128]{1,0:T(8,128)(2,1)S(1)} %get-tuple-element.32.refs_0_, bf16[32,128]{1,0:T(8,128)(2,1)S(1)} %get-tuple-element.33.refs_1_, f32[512,128]{1,0:T(8,128)S(1)} %get-tuple-element.34.refs_2_, bf16[1856,128]{1,0:T(8,128)(2,1)S(1)} %collective-permute-done.7.refs_3_.refs_6_, ...), custom_call_target="tpu_custom_call" | custom-call | tf_op jit(solution)/shard_map/pallas_call | solution.py:410
  59.5 7.8 %collective-permute-done.17.refs_7_ = bf16[800,128]{1,0:T(8,128)(2,1)S(1)} collective-permute-done((bf16[800,128]{1,0:T(8,128)(2,1)S(1)}, bf16[800,128]{1,0:T(8,128)(2,1)S(1)}, u32[]{:S(2)}, u32[]{:S(2)}) %collective-permute-start.17) | collective-permute-done | bytes 204832 | tf_op jit(solution)/shard_map/ppermute | solution.py:29
  67.3 0.6 collective-permute-start.11
  67.9 0.9 shard_map.100.refs_9_
  68.8 1.4 %shard_map.101 = (bf16[384,128]{1,0:T(8,128)(2,1)S(1)}, f32[1152,128]{1,0:T(8,128)S(1)}) custom-call(bf16[1024,128]{1,0:T(8,128)(2,1)S(1)} %get-tuple-element.37.refs_0_, bf16[512,128]{1,0:T(8,128)(2,1)S(1)} %get-tuple-element.38.refs_1_, bf16[16,128]{1,0:T(8,128)(2,1)S(1)} %get-tuple-element.39.refs_2_, bf16[16,128]{1,0:T(8,128)(2,1)S(1)} %get-tuple-element.40.refs_3_, ...), custom_call_target="tpu_custom_call" | custom-call | tf_op jit(solution)/shard_map/pallas_call | solution.py:410
  70.2 0.5 collective-permute-done.16.refs_6_
  70.7 1.0 %collective-permute-start.14 = (bf16[384,128]{1,0:T(8,128)(2,1)S(1)}, bf16[384,128]{1,0:T(8,128)(2,1)S(1)}, u32[]{:S(2)}, u32[]{:S(2)}) collective-permute-start(bf16[384,128]{1,0:T(8,128)(2,1)S(1)} %get-tuple-element.43.refs_12_), channel_id=1, source_target_pairs={{0,16},{8,24},{16,0},{24,8},{1,17},{9,25},{17,1},{25,9},{2,18},{10... | collective-permute-start | bytes 294920 | tf_op jit(solution)/shard_map/ppermute | solution.py:29
  71.7 0.0 collective-permute-done.refs_1_
  71.7 0.0 collective-permute-start.13
  71.7 1.8 %shard_map.102.refs_16_ = bf16[768,128]{1,0:T(8,128)(2,1)S(1)} custom-call(bf16[1024,128]{1,0:T(8,128)(2,1)S(1)} %get-tuple-element.37.refs_0_, bf16[512,128]{1,0:T(8,128)(2,1)S(1)} %get-tuple-element.38.refs_1_, bf16[16,128]{1,0:T(8,128)(2,1)S(1)} %get-tuple-element.39.refs_2_, bf16[16,128]{1,0:T(8,128)(2,1)S(1)} %get-tuple-element.40.refs_3_, ...), custom_call_target="tpu_custom_call" | custom-call | tf_op jit(solution)/shard_map/pallas_call | solution.py:410
  73.5 1.1 %collective-permute-start.21 = (bf16[768,128]{1,0:T(8,128)(2,1)S(1)}, bf16[768,128]{1,0:T(8,128)(2,1)S(1)}, u32[]{:S(2)}, u32[]{:S(2)}) collective-permute-start(bf16[768,128]{1,0:T(8,128)(2,1)S(1)} %shard_map.102.refs_16_), channel_id=1, source_target_pairs={{0,16},{8,24},{16,0},{24,8},{1,17},{9,25},{17,1},{25,9},{2,18},{10... | collective-permute-start | bytes 589832 | tf_op jit(solution)/shard_map/ppermute | solution.py:29
  74.6 6.8 %collective-permute-done.14.refs_14_ = bf16[384,128]{1,0:T(8,128)(2,1)S(1)} collective-permute-done((bf16[384,128]{1,0:T(8,128)(2,1)S(1)}, bf16[384,128]{1,0:T(8,128)(2,1)S(1)}, u32[]{:S(2)}, u32[]{:S(2)}) %collective-permute-start.14) | collective-permute-done | bytes 98336 | tf_op jit(solution)/shard_map/ppermute | solution.py:29
  81.4 0.0 collective-permute-start.4
  81.4 0.5 collective-permute-start.6
  81.9 0.1 collective-permute-start.15
  82.0 2.2 %collective-permute-done.15.refs_15_ = bf16[384,128]{1,0:T(8,128)(2,1)S(1)} collective-permute-done((bf16[384,128]{1,0:T(8,128)(2,1)S(1)}, bf16[384,128]{1,0:T(8,128)(2,1)S(1)}, u32[]{:S(2)}, u32[]{:S(2)}) %collective-permute-start.15) | collective-permute-done | bytes 98336 | tf_op jit(solution)/shard_map/ppermute | solution.py:29
  84.2 0.1 collective-permute-start.20
  84.4 0.4 collective-permute-start.10
  84.7 0.1 collective-permute-start.12
  84.9 0.8 collective-permute-done.20.refs_17_
  85.7 0.1 collective-permute-start.22
  85.8 1.3 %collective-permute-done.22.refs_19_ = bf16[768,128]{1,0:T(8,128)(2,1)S(1)} collective-permute-done((bf16[768,128]{1,0:T(8,128)(2,1)S(1)}, bf16[768,128]{1,0:T(8,128)(2,1)S(1)}, u32[]{:S(2)}, u32[]{:S(2)}) %collective-permute-start.22) | collective-permute-done | bytes 196640 | tf_op jit(solution)/shard_map/ppermute | solution.py:29
  87.1 5.5 %place.1 = (bf16[4096,128]{1,0:T(8,128)(2,1)}, bf16[4096,128]{1,0:T(8,128)(2,1)}, bf16[4096,128]{1,0:T(8,128)(2,1)}) custom-call(s32[16]{0:T(128)S(1)} %copy-done.1, bf16[1024,128]{1,0:T(8,128)(2,1)S(1)} %get-tuple-element.29.refs_0_, bf16[1024,128]{1,0:T(8,128)(2,1)S(1)} %collective-permute-done.refs_1_, ...), custom_call_target="tpu_custom_call" | custom-call | tf_op jit(solution)/shard_map/place/pallas_call | solution.py:521
  (12 shorter events, 0.0 us)
Async XLA Ops:
  0.6 0.7 copy-start
  5.9 30.7 %collective-permute-start.3 = (bf16[2112,128]{1,0:T(8,128)(2,1)S(1)}, bf16[2112,128]{1,0:T(8,128)(2,1)S(1)}, u32[]{:S(2)}, u32[]{:S(2)}) collective-permute-start(bf16[2112,128]{1,0:T(8,128)(2,1)S(1)} %get-tuple-element.30), channel_id=1, source_target_pairs={{0,1},{1,0},{2,3},{3,2},{4,5},{5,4},{6,7},{7,6},{8,9},{9,8},{10,11... | collective-permute-start | bytes 1622024 | tf_op jit(solution)/shard_map/ppermute | solution.py:29
  14.0 10.7 %collective-permute-start.19 = (bf16[800,128]{1,0:T(8,128)(2,1)S(1)}, bf16[800,128]{1,0:T(8,128)(2,1)S(1)}, u32[]{:S(2)}, u32[]{:S(2)}) collective-permute-start(bf16[800,128]{1,0:T(8,128)(2,1)S(1)} %get-tuple-element.44), channel_id=1, source_target_pairs={{0,7},{1,6},{2,5},{3,4},{4,3},{5,2},{6,1},{7,0},{8,15},{9,14},{10,... | collective-permute-start | bytes 614408 | tf_op jit(solution)/shard_map/ppermute | solution.py:29
  17.6 33.4 %collective-permute-start.7 = (bf16[1856,128]{1,0:T(8,128)(2,1)S(1)}, bf16[1856,128]{1,0:T(8,128)(2,1)S(1)}, u32[]{:S(2)}, u32[]{:S(2)}) collective-permute-start(bf16[1856,128]{1,0:T(8,128)(2,1)S(1)} %get-tuple-element.35), channel_id=1, source_target_pairs={{0,1},{1,0},{2,3},{3,2},{4,5},{5,4},{6,7},{7,6},{8,9},{9,8},{10,11... | collective-permute-start | bytes 1425416 | tf_op jit(solution)/shard_map/ppermute | solution.py:29
  19.1 32.0 %collective-permute-start.9 = (bf16[1856,128]{1,0:T(8,128)(2,1)S(1)}, bf16[1856,128]{1,0:T(8,128)(2,1)S(1)}, u32[]{:S(2)}, u32[]{:S(2)}) collective-permute-start(bf16[1856,128]{1,0:T(8,128)(2,1)S(1)} %get-tuple-element.36), channel_id=1, source_target_pairs={{0,3},{1,2},{2,1},{3,0},{4,7},{5,6},{6,5},{7,4},{8,11},{9,10},{10,... | collective-permute-start | bytes 1425416 | tf_op jit(solution)/shard_map/ppermute | solution.py:29
  19.1 32.5 %collective-permute-start.8 = (bf16[1856,128]{1,0:T(8,128)(2,1)S(1)}, bf16[1856,128]{1,0:T(8,128)(2,1)S(1)}, u32[]{:S(2)}, u32[]{:S(2)}) collective-permute-start(bf16[1856,128]{1,0:T(8,128)(2,1)S(1)} %get-tuple-element.36), channel_id=1, source_target_pairs={{0,2},{1,3},{2,0},{3,1},{4,6},{5,7},{6,4},{7,5},{8,10},{9,11},{10,... | collective-permute-start | bytes 1425416 | tf_op jit(solution)/shard_map/ppermute | solution.py:29
  24.7 26.3 %collective-permute-start.1 = (bf16[1024,128]{1,0:T(8,128)(2,1)S(1)}, bf16[1024,128]{1,0:T(8,128)(2,1)S(1)}, u32[]{:S(2)}, u32[]{:S(2)}) collective-permute-start(bf16[1024,128]{1,0:T(8,128)(2,1)S(1)} %get-tuple-element.29.refs_0_), channel_id=1, source_target_pairs={{0,16},{8,24},{16,0},{24,8},{1,17},{9,25},{17,1},{25,9},{2,18},{10... | collective-permute-start | bytes 786440 | tf_op jit(solution)/shard_map/ppermute | solution.py:29
  36.6 12.9 %collective-permute-start.18 = (bf16[800,128]{1,0:T(8,128)(2,1)S(1)}, bf16[800,128]{1,0:T(8,128)(2,1)S(1)}, u32[]{:S(2)}, u32[]{:S(2)}) collective-permute-start(bf16[800,128]{1,0:T(8,128)(2,1)S(1)} %get-tuple-element.44), channel_id=1, source_target_pairs={{0,6},{1,7},{2,4},{3,5},{4,2},{5,3},{6,0},{7,1},{8,14},{9,15},{10,... | collective-permute-start | bytes 614408 | tf_op jit(solution)/shard_map/ppermute | solution.py:29
  49.5 31.9 %collective-permute-start.5 = (bf16[2048,128]{1,0:T(8,128)(2,1)S(1)}, bf16[2048,128]{1,0:T(8,128)(2,1)S(1)}, u32[]{:S(2)}, u32[]{:S(2)}) collective-permute-start(bf16[2048,128]{1,0:T(8,128)(2,1)S(1)} %shard_map.96.refs_4_), channel_id=1, source_target_pairs={{0,16},{8,24},{16,0},{24,8},{1,17},{9,25},{17,1},{25,9},{2,18},{10... | collective-permute-start | bytes 1572872 | tf_op jit(solution)/shard_map/ppermute | solution.py:29
  51.0 16.4 %collective-permute-start.17 = (bf16[800,128]{1,0:T(8,128)(2,1)S(1)}, bf16[800,128]{1,0:T(8,128)(2,1)S(1)}, u32[]{:S(2)}, u32[]{:S(2)}) collective-permute-start(bf16[800,128]{1,0:T(8,128)(2,1)S(1)} %get-tuple-element.44), channel_id=1, source_target_pairs={{0,5},{1,4},{2,7},{3,6},{4,1},{5,0},{6,3},{7,2},{8,13},{9,12},{10,... | collective-permute-start | bytes 614408 | tf_op jit(solution)/shard_map/ppermute | solution.py:29
  51.0 20.8 %collective-permute-start = (bf16[1024,128]{1,0:T(8,128)(2,1)S(1)}, bf16[1024,128]{1,0:T(8,128)(2,1)S(1)}, u32[]{:S(2)}, u32[]{:S(2)}) collective-permute-start(bf16[1024,128]{1,0:T(8,128)(2,1)S(1)} %get-tuple-element.29.refs_0_), channel_id=1, source_target_pairs={{0,8},{8,0},{16,24},{24,16},{1,9},{9,1},{17,25},{25,17},{2,10},{10... | collective-permute-start | bytes 786440 | tf_op jit(solution)/shard_map/ppermute | solution.py:29
  51.1 22.5 %collective-permute-start.2 = (bf16[1024,128]{1,0:T(8,128)(2,1)S(1)}, bf16[1024,128]{1,0:T(8,128)(2,1)S(1)}, u32[]{:S(2)}, u32[]{:S(2)}) collective-permute-start(bf16[1024,128]{1,0:T(8,128)(2,1)S(1)} %collective-permute-done.1.refs_2_), channel_id=1, source_target_pairs={{0,8},{8,0},{16,24},{24,16},{1,9},{9,1},{17,25},{25,17},{2,10},{10... | collective-permute-start | bytes 786440 | tf_op jit(solution)/shard_map/ppermute | solution.py:29
  51.6 19.2 %collective-permute-start.16 = (bf16[800,128]{1,0:T(8,128)(2,1)S(1)}, bf16[800,128]{1,0:T(8,128)(2,1)S(1)}, u32[]{:S(2)}, u32[]{:S(2)}) collective-permute-start(bf16[800,128]{1,0:T(8,128)(2,1)S(1)} %get-tuple-element.44), channel_id=1, source_target_pairs={{0,4},{1,5},{2,6},{3,7},{4,0},{5,1},{6,2},{7,3},{8,12},{9,13},{10,... | collective-permute-start | bytes 614408 | tf_op jit(solution)/shard_map/ppermute | solution.py:29
  56.4 30.8 %copy-start.1 = (s32[16]{0:T(128)S(1)}, s32[16]{0:T(128)}, u32[]{:S(2)}) copy-start(s32[16]{0:T(128)} %sm_ref.1) | copy-start | bytes 196
  67.3 17.4 %collective-permute-start.11 = (bf16[1536,128]{1,0:T(8,128)(2,1)S(1)}, bf16[1536,128]{1,0:T(8,128)(2,1)S(1)}, u32[]{:S(2)}, u32[]{:S(2)}) collective-permute-start(bf16[1536,128]{1,0:T(8,128)(2,1)S(1)} %shard_map.99.refs_8_), channel_id=1, source_target_pairs={{0,16},{8,24},{16,0},{24,8},{1,17},{9,25},{17,1},{25,9},{2,18},{10... | collective-permute-start | bytes 1179656 | tf_op jit(solution)/shard_map/ppermute | solution.py:29
  70.7 10.7 %collective-permute-start.14 = (bf16[384,128]{1,0:T(8,128)(2,1)S(1)}, bf16[384,128]{1,0:T(8,128)(2,1)S(1)}, u32[]{:S(2)}, u32[]{:S(2)}) collective-permute-start(bf16[384,128]{1,0:T(8,128)(2,1)S(1)} %get-tuple-element.43.refs_12_), channel_id=1, source_target_pairs={{0,16},{8,24},{16,0},{24,8},{1,17},{9,25},{17,1},{25,9},{2,18},{10... | collective-permute-start | bytes 294920 | tf_op jit(solution)/shard_map/ppermute | solution.py:29
  71.7 10.2 %collective-permute-start.13 = (bf16[384,128]{1,0:T(8,128)(2,1)S(1)}, bf16[384,128]{1,0:T(8,128)(2,1)S(1)}, u32[]{:S(2)}, u32[]{:S(2)}) collective-permute-start(bf16[384,128]{1,0:T(8,128)(2,1)S(1)} %get-tuple-element.43.refs_12_), channel_id=1, source_target_pairs={{0,8},{8,0},{16,24},{24,16},{1,9},{9,1},{17,25},{25,17},{2,10},{10... | collective-permute-start | bytes 294920 | tf_op jit(solution)/shard_map/ppermute | solution.py:29
  73.5 10.8 %collective-permute-start.21 = (bf16[768,128]{1,0:T(8,128)(2,1)S(1)}, bf16[768,128]{1,0:T(8,128)(2,1)S(1)}, u32[]{:S(2)}, u32[]{:S(2)}) collective-permute-start(bf16[768,128]{1,0:T(8,128)(2,1)S(1)} %shard_map.102.refs_16_), channel_id=1, source_target_pairs={{0,16},{8,24},{16,0},{24,8},{1,17},{9,25},{17,1},{25,9},{2,18},{10... | collective-permute-start | bytes 589832 | tf_op jit(solution)/shard_map/ppermute | solution.py:29
  81.4 5.7 %collective-permute-start.4 = (bf16[2048,128]{1,0:T(8,128)(2,1)S(1)}, bf16[2048,128]{1,0:T(8,128)(2,1)S(1)}, u32[]{:S(2)}, u32[]{:S(2)}) collective-permute-start(bf16[2048,128]{1,0:T(8,128)(2,1)S(1)} %shard_map.96.refs_4_), channel_id=1, source_target_pairs={{0,8},{8,0},{16,24},{24,16},{1,9},{9,1},{17,25},{25,17},{2,10},{10... | collective-permute-start | bytes 1572872 | tf_op jit(solution)/shard_map/ppermute | solution.py:29
  81.4 5.7 %collective-permute-start.6 = (bf16[2048,128]{1,0:T(8,128)(2,1)S(1)}, bf16[2048,128]{1,0:T(8,128)(2,1)S(1)}, u32[]{:S(2)}, u32[]{:S(2)}) collective-permute-start(bf16[2048,128]{1,0:T(8,128)(2,1)S(1)} %collective-permute-done.5.refs_6_), channel_id=1, source_target_pairs={{0,8},{8,0},{16,24},{24,16},{1,9},{9,1},{17,25},{25,17},{2,10},{10... | collective-permute-start | bytes 1572872 | tf_op jit(solution)/shard_map/ppermute | solution.py:29
  81.9 2.3 %collective-permute-start.15 = (bf16[384,128]{1,0:T(8,128)(2,1)S(1)}, bf16[384,128]{1,0:T(8,128)(2,1)S(1)}, u32[]{:S(2)}, u32[]{:S(2)}) collective-permute-start(bf16[384,128]{1,0:T(8,128)(2,1)S(1)} %collective-permute-done.14.refs_14_), channel_id=1, source_target_pairs={{0,8},{8,0},{16,24},{24,16},{1,9},{9,1},{17,25},{25,17},{2,10},{10... | collective-permute-start | bytes 294920 | tf_op jit(solution)/shard_map/ppermute | solution.py:29
  84.2 1.4 %collective-permute-start.20 = (bf16[768,128]{1,0:T(8,128)(2,1)S(1)}, bf16[768,128]{1,0:T(8,128)(2,1)S(1)}, u32[]{:S(2)}, u32[]{:S(2)}) collective-permute-start(bf16[768,128]{1,0:T(8,128)(2,1)S(1)} %shard_map.102.refs_16_), channel_id=1, source_target_pairs={{0,8},{8,0},{16,24},{24,16},{1,9},{9,1},{17,25},{25,17},{2,10},{10... | collective-permute-start | bytes 589832 | tf_op jit(solution)/shard_map/ppermute | solution.py:29
  84.4 2.7 %collective-permute-start.10 = (bf16[1536,128]{1,0:T(8,128)(2,1)S(1)}, bf16[1536,128]{1,0:T(8,128)(2,1)S(1)}, u32[]{:S(2)}, u32[]{:S(2)}) collective-permute-start(bf16[1536,128]{1,0:T(8,128)(2,1)S(1)} %shard_map.99.refs_8_), channel_id=1, source_target_pairs={{0,8},{8,0},{16,24},{24,16},{1,9},{9,1},{17,25},{25,17},{2,10},{10... | collective-permute-start | bytes 1179656 | tf_op jit(solution)/shard_map/ppermute | solution.py:29
  84.7 2.4 %collective-permute-start.12 = (bf16[1536,128]{1,0:T(8,128)(2,1)S(1)}, bf16[1536,128]{1,0:T(8,128)(2,1)S(1)}, u32[]{:S(2)}, u32[]{:S(2)}) collective-permute-start(bf16[1536,128]{1,0:T(8,128)(2,1)S(1)} %collective-permute-done.11.refs_10_), channel_id=1, source_target_pairs={{0,8},{8,0},{16,24},{24,16},{1,9},{9,1},{17,25},{25,17},{2,10},{10... | collective-permute-start | bytes 1179656 | tf_op jit(solution)/shard_map/ppermute | solution.py:29
  85.7 1.4 %collective-permute-start.22 = (bf16[768,128]{1,0:T(8,128)(2,1)S(1)}, bf16[768,128]{1,0:T(8,128)(2,1)S(1)}, u32[]{:S(2)}, u32[]{:S(2)}) collective-permute-start(bf16[768,128]{1,0:T(8,128)(2,1)S(1)} %collective-permute-done.21.refs_18_), channel_id=1, source_target_pairs={{0,8},{8,0},{16,24},{24,16},{1,9},{9,1},{17,25},{25,17},{2,10},{10... | collective-permute-start | bytes 589832 | tf_op jit(solution)/shard_map/ppermute | solution.py:29

commit v3 on v2

--- a/solution.py
+++ b/solution.py
@@ -17,6 +17,7 @@
 LANES = 128
 TAG_ROWS = 8
 PAIR = 16
+COPY_ROWS = 1024
 LOG2E = math.log2(math.e)
 
 
@@ -61,6 +62,10 @@
     rest = col - hi
     mid = rest.astype(BF16).astype(F32)
     return hi, mid, rest - mid
+
+
+def copy_rows(lv):
+    return min(lv.rows, COPY_ROWS)
 
 
 def extract_kernel(levels, groups, group_size, sm, keys, values, queries, grads, outs, logs, *refs):
@@ -83,11 +88,17 @@
         rate, rows = levels[level].rate, levels[level].rows
         head = sm[level * group_size + rho]
         off = rho & (rate - 1)
-        for s, source in enumerate(sources):
-            picked = source.reshape(rows, rate, HEADS // 2, 2, LANES).at[:, off, head // 2]
-            copy = pltpu.make_async_copy(picked, bufs[w].at[s], sems.at[w, s])
-            copy.start()
-            copies.append(copy)
+        piece = copy_rows(levels[level])
+        for u in range(0, rows, piece):
+            for s, source in enumerate(sources):
+                picked = source.reshape(rows, rate, HEADS // 2, 2, LANES)
+                copy = pltpu.make_async_copy(
+                    picked.at[pl.ds(u, piece), off, head // 2],
+                    bufs[w].at[s, pl.ds(u, piece)],
+                    sems.at[len(copies)],
+                )
+                copy.start()
+                copies.append(copy)
         if w == 0:
             logs_copy = pltpu.make_async_copy(logs, logs_buf, logs_sem)
             logs_copy.start()
@@ -100,17 +111,20 @@
     col_id = lax.broadcasted_iota(jnp.int32, (LANES, 2 * LANES), 1)
     lane = lax.broadcasted_iota(jnp.int32, (LANES, LANES), 1)
     group_of = {m: group for group in groups for m in group}
+    waited = 0
     for w, level in enumerate(members):
         lv = levels[level]
         group = group_of[level]
         head = sm[level * group_size + rho]
         off = rho & (lv.rate - 1)
         pick = (col_id == 2 * row_id + head % 2).astype(BF16)
-        for s in range(len(sources)):
-            copies[w * len(sources) + s].wait()
         tops = []
         flat = [bufs[w].at[s].reshape(2 * lv.rows, LANES) for s in range(len(sources))]
         for u in range(lv.rows // LANES):
+            if u * LANES % copy_rows(lv) == 0:
+                for copy in copies[waited : waited + len(sources)]:
+                    copy.wait()
+                waited += len(sources)
             got = [
                 plain_dot(pick, flat[s][u * 2 * LANES : (u + 1) * 2 * LANES, :])
                 for s in range(len(sources))
@@ -176,7 +190,9 @@
             pltpu.VMEM((tokens, LANES), F32),
             pltpu.VMEM(logs.shape, F32),
             pltpu.SemaphoreType.DMA,
-            pltpu.SemaphoreType.DMA((n, 5)),
+            pltpu.SemaphoreType.DMA(
+                (5 * sum(levels[m].rows // copy_rows(levels[m]) for m in members),)
+            ),
         ],
         compiler_params=pltpu.CompilerParams(vmem_limit_bytes=VMEM_LIMIT),
     )(sm, *[pltpu.with_memory_space_constraint(a, pltpu.HBM) for a in (*sources, logs)])
@@ -317,23 +333,24 @@
 
 
 STAGES = {
-    (0,): (("first", True, slice(0, -1), (0, 1)), ("last", False, slice(-1, None), (1, 3))),
-    (1,): (("own", True, slice(0, 0), None), ("last", False, slice(0, None), (0, 3))),
+    (0,): (("first", True, slice(0, -1), (0, 1), (0, 1)), ("last", False, slice(-1, None), (0, 1), (1, 3))),
+    (1,): (("own", True, slice(0, 0), (), None), ("last", False, slice(0, None), (0, 1), (0, 3))),
     (2, 3): (
-        ("own", True, slice(0, 0), None),
-        ("first", False, slice(0, -1), (0, 1)),
-        ("last", False, slice(-1, None), (1, 3)),
+        ("own", True, slice(0, 0), (), None),
+        ("first", False, slice(0, -1), (0, 1), (0, 1)),
+        ("next", False, slice(-1, None), (0,), None),
+        ("last", False, slice(-1, None), (1,), (1, 3)),
     ),
 }
 
 
 def compute(levels, members, group, stage, kept, received, before, scaling):
     n = len(members)
-    name, own_block, chosen, parts = stage
+    name, own_block, chosen, odd, parts = stage
     more = name != "last"
     bits_of = {m: list(range(levels[m].bits))[chosen] for m in members}
     bits = sorted({bit for m in members for bit in bits_of[m]})
-    steps = [k for k in sorted(received) if k.bit_length() - 1 in bits]
+    steps = [k for k in sorted(received) if k.bit_length() - 1 in bits and k % 2 in odd]
     rows_sum = sum(levels[m].rows for m in members)
     given = [kept[m][part] for part in range(3) for m in members]
     given += [received[k] for k in steps]
@@ -375,6 +392,7 @@
                             [
                                 Block(got[k], base, base + rows, got[k], base + 2 * rows)
                                 for k in range(2**bit, 2 ** (bit + 1))
+                                if k in got
                             ],
                         )
                     )
@@ -419,7 +437,7 @@
 def place(levels, group_size, heads_here, local_tokens, sm, gathered):
     rates = len(gathered[0][0][2])
     flat = [array for pieces in gathered for piece in pieces for array in piece[2]]
-    block, half = 2 * LANES, LANES // 2
+    block, half = 4 * LANES, LANES // 2
     parts = block // half
     steps = local_tokens // block
     tall = heads_here * half
@@ -564,11 +582,11 @@
         for stage in STAGES[members]:
             results = compute(levels, members, group, stage, kept, received[group], before, scaling)
             before = results[-1]
-            if stage[3]:
+            if stage[4]:
                 mine = results[0]
                 far = swapped(mine, "rate", 2)
                 near = swapped(mine, "rate", 1)
-                pieces.append((*stage[3], [mine, near, far, swapped(far, "rate", 1)]))
+                pieces.append((*stage[4], [mine, near, far, swapped(far, "rate", 1)]))
         gathered.append(pieces)
     return place(levels, group_size, HEADS // rate_count, local_tokens, assignment, gathered)
 

time: 93 us -> 86.9 us (0.934)
  waiting for transfers between devices: 35.3 us -> 24.3 us
  starting transfers between devices: 25.5 us -> 30.2 us
    ppermute x23, waiting for transfers between devices: 35.3 us -> 24.3 us  [swapped(): return lax.ppermute(array, axis, [(i, i ^ by) for i in range(devices)])]
    ppermute x23, starting transfers between devices: 25.5 us -> 30.2 us  [swapped(): return lax.ppermute(array, axis, [(i, i ^ by) for i in range(devices)])]
    pallas_call x7 -> x8, Pallas kernels: 15.2 us -> 15.2 us  [compute(): pl.pallas_call(kernel, out_shape=shapes, in_specs=[pl.BlockSpec(memory_sp...]
  transfers between devices with their start and end apart: 23 -> 23, of which waited for: 9 -> 7; matrix products, arithmetic and copies ran while one was open for 0% -> 0% of each run, Pallas kernels for 22% -> 24%
where the time goes in v3:
time: 86.9 us; the launch traced here: 85.8 us
  starting transfers between devices  30.2 us (35%)
  Pallas kernels  29.7 us (34%)
  waiting for transfers between devices  24.3 us (28%)
  between operations  0.96 us (1%)
    ppermute x23, starting transfers between devices, swapped(): return lax.ppermute(array, axis, [(i, i ^ by) for i in range(devices)])  30.2 us
    ppermute x23, waiting for transfers between devices, swapped(): return lax.ppermute(array, axis, [(i, i ^ by) for i in range(devices)])  24.3 us
    pallas_call x8, Pallas kernels, compute(): pl.pallas_call(kernel, out_shape=shapes, in_specs=[pl.BlockSpec(memory_sp...  15.2 us
    pallas_call x2, Pallas kernels, extract(): pl.pallas_call(kernel, out_shape=shapes, in_specs=[pl.BlockSpec(memory_sp...  9.63 us
    pallas_call x1, Pallas kernels, place(): pl.pallas_call(kernel, grid=(steps,), out_shape=[shape] * 3, in_specs=[pl...  4.92 us
  transfers between devices with their start and end apart: 23, of which 7 were waited for; matrix products, arithmetic and copies ran while one was open for 0% of the time, Pallas kernels for 24%

profile of v3, /device:TPU:0, one launch (start us, length us, event | category | flops | bytes accessed | tf_op | source)
XLA Modules:
  0.0 85.8 jit_solution(1190084857237889389)
XLA Ops:
  0.6 0.6 copy-done
  1.3 4.6 %shard_map.94 = (bf16[4096,128]{1,0:T(8,128)(2,1)S(1)}, bf16[64,128]{1,0:T(8,128)(2,1)S(1)}, f32[1024,128]{1,0:T(8,128)S(1)}, bf16[2112,128]{1,0:T(8,128)(2,1)S(1)}) custom-call(s32[16]{0:T(128)S(1)} %copy-done, bf16[1024,8,2,128]{3,2,1,0:T(2,128)(2,1)} %bitcast.9, bf16[1024,8,2,128]{3,2,1,0:T(2,128)(2,1)} %bitcast.11, bf16[1024,8,2,128]{3,2,1,0:T(2,128)(2,1)} %bitcast.13, ...), custom_call_target="tpu_custom_call" | custom-call | tf_op jit(solution)/shard_map/pallas_call | solution.py:183
  5.9 3.0 %collective-permute-start.3 = (bf16[2112,128]{1,0:T(8,128)(2,1)S(1)}, bf16[2112,128]{1,0:T(8,128)(2,1)S(1)}, u32[]{:S(2)}, u32[]{:S(2)}) collective-permute-start(bf16[2112,128]{1,0:T(8,128)(2,1)S(1)} %get-tuple-element.30), channel_id=1, source_target_pairs={{0,1},{1,0},{2,3},{3,2},{4,5},{5,4},{6,7},{7,6},{8,9},{9,8},{10,11... | collective-permute-start | bytes 1622024 | tf_op jit(solution)/shard_map/ppermute | solution.py:30
  8.9 5.0 %shard_map.97 = (bf16[2048,128]{1,0:T(8,128)(2,1)S(1)}, bf16[1024,128]{1,0:T(8,128)(2,1)S(1)}, bf16[512,128]{1,0:T(8,128)(2,1)S(1)}, bf16[32,128]{1,0:T(8,128)(2...) custom-call(s32[16]{0:T(128)S(1)} %copy-done.1, ...), custom_call_target="tpu_custom_call" | custom-call | tf_op jit(solution)/shard_map/pallas_call | solution.py:183
  14.0 3.7 %collective-permute-start.19 = (bf16[800,128]{1,0:T(8,128)(2,1)S(1)}, bf16[800,128]{1,0:T(8,128)(2,1)S(1)}, u32[]{:S(2)}, u32[]{:S(2)}) collective-permute-start(bf16[800,128]{1,0:T(8,128)(2,1)S(1)} %get-tuple-element.44), channel_id=1, source_target_pairs={{0,6},{1,7},{2,4},{3,5},{4,2},{5,3},{6,0},{7,1},{8,14},{9,15},{10,... | collective-permute-start | bytes 614408 | tf_op jit(solution)/shard_map/ppermute | solution.py:30
  17.6 0.5 collective-permute-start.7
  18.2 0.5 collective-permute-start.9
  18.6 2.5 %collective-permute-start.8 = (bf16[1856,128]{1,0:T(8,128)(2,1)S(1)}, bf16[1856,128]{1,0:T(8,128)(2,1)S(1)}, u32[]{:S(2)}, u32[]{:S(2)}) collective-permute-start(bf16[1856,128]{1,0:T(8,128)(2,1)S(1)} %get-tuple-element.36), channel_id=1, source_target_pairs={{0,2},{1,3},{2,0},{3,1},{4,6},{5,7},{6,4},{7,5},{8,10},{9,11},{10,... | collective-permute-start | bytes 1425416 | tf_op jit(solution)/shard_map/ppermute | solution.py:30
  21.1 3.3 %shard_map.95 = (bf16[1024,128]{1,0:T(8,128)(2,1)S(1)}, f32[3072,128]{1,0:T(8,128)S(1)}) custom-call(bf16[4096,128]{1,0:T(8,128)(2,1)S(1)} %get-tuple-element.26.refs_0_, bf16[64,128]{1,0:T(8,128)(2,1)S(1)} %get-tuple-element.27.refs_1_, f32[1024,128]{1,0:T(8,128)S(1)} %get-tuple-element.28.refs_2_), custom_call_target="tpu_custom_call" | custom-call | tf_op jit(solution)/shard_map/pallas_call | solution.py:428
  24.5 1.6 %collective-permute-start.1 = (bf16[1024,128]{1,0:T(8,128)(2,1)S(1)}, bf16[1024,128]{1,0:T(8,128)(2,1)S(1)}, u32[]{:S(2)}, u32[]{:S(2)}) collective-permute-start(bf16[1024,128]{1,0:T(8,128)(2,1)S(1)} %get-tuple-element.29.refs_0_), channel_id=1, source_target_pairs={{0,16},{8,24},{16,0},{24,8},{1,17},{9,25},{17,1},{25,9},{2,18},{10... | collective-permute-start | bytes 786440 | tf_op jit(solution)/shard_map/ppermute | solution.py:30
  26.1 9.3 %collective-permute-start.18 = (bf16[800,128]{1,0:T(8,128)(2,1)S(1)}, bf16[800,128]{1,0:T(8,128)(2,1)S(1)}, u32[]{:S(2)}, u32[]{:S(2)}) collective-permute-start(bf16[800,128]{1,0:T(8,128)(2,1)S(1)} %get-tuple-element.44), channel_id=1, source_target_pairs={{0,4},{1,5},{2,6},{3,7},{4,0},{5,1},{6,2},{7,3},{8,12},{9,13},{10,... | collective-permute-start | bytes 614408 | tf_op jit(solution)/shard_map/ppermute | solution.py:30
  35.4 3.6 %shard_map.96.refs_4_ = bf16[2048,128]{1,0:T(8,128)(2,1)S(1)} custom-call(bf16[4096,128]{1,0:T(8,128)(2,1)S(1)} %get-tuple-element.26.refs_0_, bf16[64,128]{1,0:T(8,128)(2,1)S(1)} %get-tuple-element.27.refs_1_, f32[1024,128]{1,0:T(8,128)S(1)} %get-tuple-element.28.refs_2_, bf16[2112,128]{1,0:T(8,128)(2,1)S(1)} %collective-permute-done.3.refs_3_, ...), custom_call_target="tpu_custom_call" | custom-call | tf_op jit(solution)/shard_map/pallas_call | solution.py:428
  38.9 7.6 %collective-permute-done.18.refs_6_ = bf16[800,128]{1,0:T(8,128)(2,1)S(1)} collective-permute-done((bf16[800,128]{1,0:T(8,128)(2,1)S(1)}, bf16[800,128]{1,0:T(8,128)(2,1)S(1)}, u32[]{:S(2)}, u32[]{:S(2)}) %collective-permute-start.18) | collective-permute-done | bytes 204832 | tf_op jit(solution)/shard_map/ppermute | solution.py:30
  46.6 1.9 %collective-permute-start.5 = (bf16[2048,128]{1,0:T(8,128)(2,1)S(1)}, bf16[2048,128]{1,0:T(8,128)(2,1)S(1)}, u32[]{:S(2)}, u32[]{:S(2)}) collective-permute-start(bf16[2048,128]{1,0:T(8,128)(2,1)S(1)} %shard_map.96.refs_4_), channel_id=1, source_target_pairs={{0,16},{8,24},{16,0},{24,8},{1,17},{9,25},{17,1},{25,9},{2,18},{10... | collective-permute-start | bytes 1572872 | tf_op jit(solution)/shard_map/ppermute | solution.py:30
  48.4 0.0 collective-permute-done.1.refs_2_
  48.4 0.0 collective-permute-start.17
  48.4 0.0 collective-permute-done.7.refs_3_.refs_6_
  48.5 0.1 collective-permute-start
  48.5 0.0 collective-permute-done.9.refs_5_.refs_8_
  48.5 0.5 collective-permute-start.2
  49.0 3.2 %collective-permute-start.16 = (bf16[800,128]{1,0:T(8,128)(2,1)S(1)}, bf16[800,128]{1,0:T(8,128)(2,1)S(1)}, u32[]{:S(2)}, u32[]{:S(2)}) collective-permute-start(bf16[800,128]{1,0:T(8,128)(2,1)S(1)} %get-tuple-element.44), channel_id=1, source_target_pairs={{0,5},{1,4},{2,7},{3,6},{4,1},{5,0},{6,3},{7,2},{8,13},{9,12},{10,... | collective-permute-start | bytes 614408 | tf_op jit(solution)/shard_map/ppermute | solution.py:30
  52.3 1.1 %shard_map.98.refs_6_ = f32[1536,128]{1,0:T(8,128)S(1)} custom-call(bf16[2048,128]{1,0:T(8,128)(2,1)S(1)} %get-tuple-element.32.refs_0_, bf16[32,128]{1,0:T(8,128)(2,1)S(1)} %get-tuple-element.33.refs_1_, f32[512,128]{1,0:T(8,128)S(1)} %get-tuple-element.34.refs_2_), custom_call_target="tpu_custom_call" | custom-call | tf_op jit(solution)/shard_map/pallas_call | solution.py:428
  53.4 3.1 %shard_map.99.refs_8_ = bf16[1536,128]{1,0:T(8,128)(2,1)S(1)} custom-call(bf16[2048,128]{1,0:T(8,128)(2,1)S(1)} %get-tuple-element.32.refs_0_, bf16[32,128]{1,0:T(8,128)(2,1)S(1)} %get-tuple-element.33.refs_1_, f32[512,128]{1,0:T(8,128)S(1)} %get-tuple-element.34.refs_2_, bf16[1856,128]{1,0:T(8,128)(2,1)S(1)} %collective-permute-done.7.refs_3_.refs_6_, ...), custom_call_target="tpu_custom_call" | custom-call | tf_op jit(solution)/shard_map/pallas_call | solution.py:428
  56.6 1.0 %collective-permute-done.17.refs_7_ = bf16[800,128]{1,0:T(8,128)(2,1)S(1)} collective-permute-done((bf16[800,128]{1,0:T(8,128)(2,1)S(1)}, bf16[800,128]{1,0:T(8,128)(2,1)S(1)}, u32[]{:S(2)}, u32[]{:S(2)}) %collective-permute-start.17) | collective-permute-done | bytes 204832 | tf_op jit(solution)/shard_map/ppermute | solution.py:30
  57.5 0.0 collective-permute-start.11
  57.5 0.9 %shard_map.100.refs_9_ = f32[1152,128]{1,0:T(8,128)S(1)} custom-call(bf16[1024,128]{1,0:T(8,128)(2,1)S(1)} %get-tuple-element.37.refs_0_, bf16[512,128]{1,0:T(8,128)(2,1)S(1)} %get-tuple-element.38.refs_1_, bf16[16,128]{1,0:T(8,128)(2,1)S(1)} %get-tuple-element.39.refs_2_, bf16[16,128]{1,0:T(8,128)(2,1)S(1)} %get-tuple-element.40.refs_3_, ...), custom_call_target="tpu_custom_call" | custom-call | tf_op jit(solution)/shard_map/pallas_call | solution.py:428
  58.4 1.4 %shard_map.101 = (bf16[384,128]{1,0:T(8,128)(2,1)S(1)}, f32[1152,128]{1,0:T(8,128)S(1)}) custom-call(bf16[1024,128]{1,0:T(8,128)(2,1)S(1)} %get-tuple-element.37.refs_0_, bf16[512,128]{1,0:T(8,128)(2,1)S(1)} %get-tuple-element.38.refs_1_, bf16[16,128]{1,0:T(8,128)(2,1)S(1)} %get-tuple-element.39.refs_2_, bf16[16,128]{1,0:T(8,128)(2,1)S(1)} %get-tuple-element.40.refs_3_, ...), custom_call_target="tpu_custom_call" | custom-call | tf_op jit(solution)/shard_map/pallas_call | solution.py:428
  59.8 8.6 %collective-permute-done.16.refs_6_ = bf16[800,128]{1,0:T(8,128)(2,1)S(1)} collective-permute-done((bf16[800,128]{1,0:T(8,128)(2,1)S(1)}, bf16[800,128]{1,0:T(8,128)(2,1)S(1)}, u32[]{:S(2)}, u32[]{:S(2)}) %collective-permute-start.16) | collective-permute-done | bytes 204832 | tf_op jit(solution)/shard_map/ppermute | solution.py:30
  68.4 0.5 collective-permute-start.14
  68.9 0.8 shard_map.102.refs_8_
  69.8 0.0 collective-permute-done.refs_1_
  69.8 0.1 collective-permute-start.13
  69.9 0.9 %shard_map.103.refs_16_ = bf16[768,128]{1,0:T(8,128)(2,1)S(1)} custom-call(bf16[1024,128]{1,0:T(8,128)(2,1)S(1)} %get-tuple-element.37.refs_0_, bf16[512,128]{1,0:T(8,128)(2,1)S(1)} %get-tuple-element.38.refs_1_, bf16[16,128]{1,0:T(8,128)(2,1)S(1)} %get-tuple-element.39.refs_2_, bf16[16,128]{1,0:T(8,128)(2,1)S(1)} %get-tuple-element.40.refs_3_, ...), custom_call_target="tpu_custom_call" | custom-call | tf_op jit(solution)/shard_map/pallas_call | solution.py:428
  70.8 0.0 collective-permute-done.2.refs_3_
  70.8 1.5 %collective-permute-start.21 = (bf16[768,128]{1,0:T(8,128)(2,1)S(1)}, bf16[768,128]{1,0:T(8,128)(2,1)S(1)}, u32[]{:S(2)}, u32[]{:S(2)}) collective-permute-start(bf16[768,128]{1,0:T(8,128)(2,1)S(1)} %shard_map.103.refs_16_), channel_id=1, source_target_pairs={{0,16},{8,24},{16,0},{24,8},{1,17},{9,25},{17,1},{25,9},{2,18},{10... | collective-permute-start | bytes 589832 | tf_op jit(solution)/shard_map/ppermute | solution.py:30
  72.3 0.7 collective-permute-done.14.refs_14_
  73.0 0.0 collective-permute-start.4
  73.0 0.0 collective-permute-done.5.refs_6_
  73.0 0.5 collective-permute-start.6
  73.5 0.0 collective-permute-done.13.refs_13_
  73.5 0.1 collective-permute-start.15
  73.6 2.2 %collective-permute-done.15.refs_15_ = bf16[384,128]{1,0:T(8,128)(2,1)S(1)} collective-permute-done((bf16[384,128]{1,0:T(8,128)(2,1)S(1)}, bf16[384,128]{1,0:T(8,128)(2,1)S(1)}, u32[]{:S(2)}, u32[]{:S(2)}) %collective-permute-start.15) | collective-permute-done | bytes 98336 | tf_op jit(solution)/shard_map/ppermute | solution.py:30
  75.8 0.1 collective-permute-start.20
  75.9 2.2 %collective-permute-done.21.refs_18_ = bf16[768,128]{1,0:T(8,128)(2,1)S(1)} collective-permute-done((bf16[768,128]{1,0:T(8,128)(2,1)S(1)}, bf16[768,128]{1,0:T(8,128)(2,1)S(1)}, u32[]{:S(2)}, u32[]{:S(2)}) %collective-permute-start.21) | collective-permute-done | bytes 196640 | tf_op jit(solution)/shard_map/ppermute | solution.py:30
  78.1 0.5 collective-permute-start.12
  78.7 0.1 collective-permute-start.22
  78.7 2.0 %collective-permute-done.22.refs_19_ = bf16[768,128]{1,0:T(8,128)(2,1)S(1)} collective-permute-done((bf16[768,128]{1,0:T(8,128)(2,1)S(1)}, bf16[768,128]{1,0:T(8,128)(2,1)S(1)}, u32[]{:S(2)}, u32[]{:S(2)}) %collective-permute-start.22) | collective-permute-done | bytes 196640 | tf_op jit(solution)/shard_map/ppermute | solution.py:30
  80.7 4.9 %place.1 = (bf16[4096,128]{1,0:T(8,128)(2,1)}, bf16[4096,128]{1,0:T(8,128)(2,1)}, bf16[4096,128]{1,0:T(8,128)(2,1)}) custom-call(s32[16]{0:T(128)S(1)} %copy-done.1, bf16[1024,128]{1,0:T(8,128)(2,1)S(1)} %get-tuple-element.29.refs_0_, bf16[1024,128]{1,0:T(8,128)(2,1)S(1)} %collective-permute-done.refs_1_, ...), custom_call_target="tpu_custom_call" | custom-call | tf_op jit(solution)/shard_map/place/pallas_call | solution.py:539
  (13 shorter events, 0.0 us)
Async XLA Ops:
  0.6 0.7 copy-start
  1.3 7.6 %copy-start.1 = (s32[16]{0:T(128)S(1)}, s32[16]{0:T(128)}, u32[]{:S(2)}) copy-start(s32[16]{0:T(128)} %sm_ref.1) | copy-start | bytes 196
  5.9 20.2 %collective-permute-start.3 = (bf16[2112,128]{1,0:T(8,128)(2,1)S(1)}, bf16[2112,128]{1,0:T(8,128)(2,1)S(1)}, u32[]{:S(2)}, u32[]{:S(2)}) collective-permute-start(bf16[2112,128]{1,0:T(8,128)(2,1)S(1)} %get-tuple-element.30), channel_id=1, source_target_pairs={{0,1},{1,0},{2,3},{3,2},{4,5},{5,4},{6,7},{7,6},{8,9},{9,8},{10,11... | collective-permute-start | bytes 1622024 | tf_op jit(solution)/shard_map/ppermute | solution.py:30
  14.0 10.5 %collective-permute-start.19 = (bf16[800,128]{1,0:T(8,128)(2,1)S(1)}, bf16[800,128]{1,0:T(8,128)(2,1)S(1)}, u32[]{:S(2)}, u32[]{:S(2)}) collective-permute-start(bf16[800,128]{1,0:T(8,128)(2,1)S(1)} %get-tuple-element.44), channel_id=1, source_target_pairs={{0,6},{1,7},{2,4},{3,5},{4,2},{5,3},{6,0},{7,1},{8,14},{9,15},{10,... | collective-permute-start | bytes 614408 | tf_op jit(solution)/shard_map/ppermute | solution.py:30
  17.6 30.8 %collective-permute-start.7 = (bf16[1856,128]{1,0:T(8,128)(2,1)S(1)}, bf16[1856,128]{1,0:T(8,128)(2,1)S(1)}, u32[]{:S(2)}, u32[]{:S(2)}) collective-permute-start(bf16[1856,128]{1,0:T(8,128)(2,1)S(1)} %get-tuple-element.35), channel_id=1, source_target_pairs={{0,1},{1,0},{2,3},{3,2},{4,5},{5,4},{6,7},{7,6},{8,9},{9,8},{10,11... | collective-permute-start | bytes 1425416 | tf_op jit(solution)/shard_map/ppermute | solution.py:30
  18.2 30.4 %collective-permute-start.9 = (bf16[1856,128]{1,0:T(8,128)(2,1)S(1)}, bf16[1856,128]{1,0:T(8,128)(2,1)S(1)}, u32[]{:S(2)}, u32[]{:S(2)}) collective-permute-start(bf16[1856,128]{1,0:T(8,128)(2,1)S(1)} %get-tuple-element.36), channel_id=1, source_target_pairs={{0,3},{1,2},{2,1},{3,0},{4,7},{5,6},{6,5},{7,4},{8,11},{9,10},{10,... | collective-permute-start | bytes 1425416 | tf_op jit(solution)/shard_map/ppermute | solution.py:30
  18.6 30.4 %collective-permute-start.8 = (bf16[1856,128]{1,0:T(8,128)(2,1)S(1)}, bf16[1856,128]{1,0:T(8,128)(2,1)S(1)}, u32[]{:S(2)}, u32[]{:S(2)}) collective-permute-start(bf16[1856,128]{1,0:T(8,128)(2,1)S(1)} %get-tuple-element.36), channel_id=1, source_target_pairs={{0,2},{1,3},{2,0},{3,1},{4,6},{5,7},{6,4},{7,5},{8,10},{9,11},{10,... | collective-permute-start | bytes 1425416 | tf_op jit(solution)/shard_map/ppermute | solution.py:30
  24.5 24.0 %collective-permute-start.1 = (bf16[1024,128]{1,0:T(8,128)(2,1)S(1)}, bf16[1024,128]{1,0:T(8,128)(2,1)S(1)}, u32[]{:S(2)}, u32[]{:S(2)}) collective-permute-start(bf16[1024,128]{1,0:T(8,128)(2,1)S(1)} %get-tuple-element.29.refs_0_), channel_id=1, source_target_pairs={{0,16},{8,24},{16,0},{24,8},{1,17},{9,25},{17,1},{25,9},{2,18},{10... | collective-permute-start | bytes 786440 | tf_op jit(solution)/shard_map/ppermute | solution.py:30
  26.1 20.5 %collective-permute-start.18 = (bf16[800,128]{1,0:T(8,128)(2,1)S(1)}, bf16[800,128]{1,0:T(8,128)(2,1)S(1)}, u32[]{:S(2)}, u32[]{:S(2)}) collective-permute-start(bf16[800,128]{1,0:T(8,128)(2,1)S(1)} %get-tuple-element.44), channel_id=1, source_target_pairs={{0,4},{1,5},{2,6},{3,7},{4,0},{5,1},{6,2},{7,3},{8,12},{9,13},{10,... | collective-permute-start | bytes 614408 | tf_op jit(solution)/shard_map/ppermute | solution.py:30
  46.6 26.5 %collective-permute-start.5 = (bf16[2048,128]{1,0:T(8,128)(2,1)S(1)}, bf16[2048,128]{1,0:T(8,128)(2,1)S(1)}, u32[]{:S(2)}, u32[]{:S(2)}) collective-permute-start(bf16[2048,128]{1,0:T(8,128)(2,1)S(1)} %shard_map.96.refs_4_), channel_id=1, source_target_pairs={{0,16},{8,24},{16,0},{24,8},{1,17},{9,25},{17,1},{25,9},{2,18},{10... | collective-permute-start | bytes 1572872 | tf_op jit(solution)/shard_map/ppermute | solution.py:30
  48.4 9.1 %collective-permute-start.17 = (bf16[800,128]{1,0:T(8,128)(2,1)S(1)}, bf16[800,128]{1,0:T(8,128)(2,1)S(1)}, u32[]{:S(2)}, u32[]{:S(2)}) collective-permute-start(bf16[800,128]{1,0:T(8,128)(2,1)S(1)} %get-tuple-element.44), channel_id=1, source_target_pairs={{0,7},{1,6},{2,5},{3,4},{4,3},{5,2},{6,1},{7,0},{8,15},{9,14},{10,... | collective-permute-start | bytes 614408 | tf_op jit(solution)/shard_map/ppermute | solution.py:30
  48.5 21.3 %collective-permute-start = (bf16[1024,128]{1,0:T(8,128)(2,1)S(1)}, bf16[1024,128]{1,0:T(8,128)(2,1)S(1)}, u32[]{:S(2)}, u32[]{:S(2)}) collective-permute-start(bf16[1024,128]{1,0:T(8,128)(2,1)S(1)} %get-tuple-element.29.refs_0_), channel_id=1, source_target_pairs={{0,8},{8,0},{16,24},{24,16},{1,9},{9,1},{17,25},{25,17},{2,10},{10... | collective-permute-start | bytes 786440 | tf_op jit(solution)/shard_map/ppermute | solution.py:30
  48.5 22.2 %collective-permute-start.2 = (bf16[1024,128]{1,0:T(8,128)(2,1)S(1)}, bf16[1024,128]{1,0:T(8,128)(2,1)S(1)}, u32[]{:S(2)}, u32[]{:S(2)}) collective-permute-start(bf16[1024,128]{1,0:T(8,128)(2,1)S(1)} %collective-permute-done.1.refs_2_), channel_id=1, source_target_pairs={{0,8},{8,0},{16,24},{24,16},{1,9},{9,1},{17,25},{25,17},{2,10},{10... | collective-permute-start | bytes 786440 | tf_op jit(solution)/shard_map/ppermute | solution.py:30
  49.0 19.4 %collective-permute-start.16 = (bf16[800,128]{1,0:T(8,128)(2,1)S(1)}, bf16[800,128]{1,0:T(8,128)(2,1)S(1)}, u32[]{:S(2)}, u32[]{:S(2)}) collective-permute-start(bf16[800,128]{1,0:T(8,128)(2,1)S(1)} %get-tuple-element.44), channel_id=1, source_target_pairs={{0,5},{1,4},{2,7},{3,6},{4,1},{5,0},{6,3},{7,2},{8,13},{9,12},{10,... | collective-permute-start | bytes 614408 | tf_op jit(solution)/shard_map/ppermute | solution.py:30
  57.5 20.6 %collective-permute-start.11 = (bf16[1536,128]{1,0:T(8,128)(2,1)S(1)}, bf16[1536,128]{1,0:T(8,128)(2,1)S(1)}, u32[]{:S(2)}, u32[]{:S(2)}) collective-permute-start(bf16[1536,128]{1,0:T(8,128)(2,1)S(1)} %shard_map.99.refs_8_), channel_id=1, source_target_pairs={{0,16},{8,24},{16,0},{24,8},{1,17},{9,25},{17,1},{25,9},{2,18},{10... | collective-permute-start | bytes 1179656 | tf_op jit(solution)/shard_map/ppermute | solution.py:30
  68.4 4.6 %collective-permute-start.14 = (bf16[384,128]{1,0:T(8,128)(2,1)S(1)}, bf16[384,128]{1,0:T(8,128)(2,1)S(1)}, u32[]{:S(2)}, u32[]{:S(2)}) collective-permute-start(bf16[384,128]{1,0:T(8,128)(2,1)S(1)} %get-tuple-element.43.refs_12_), channel_id=1, source_target_pairs={{0,16},{8,24},{16,0},{24,8},{1,17},{9,25},{17,1},{25,9},{2,18},{10... | collective-permute-start | bytes 294920 | tf_op jit(solution)/shard_map/ppermute | solution.py:30
  69.8 3.7 %collective-permute-start.13 = (bf16[384,128]{1,0:T(8,128)(2,1)S(1)}, bf16[384,128]{1,0:T(8,128)(2,1)S(1)}, u32[]{:S(2)}, u32[]{:S(2)}) collective-permute-start(bf16[384,128]{1,0:T(8,128)(2,1)S(1)} %get-tuple-element.43.refs_12_), channel_id=1, source_target_pairs={{0,8},{8,0},{16,24},{24,16},{1,9},{9,1},{17,25},{25,17},{2,10},{10... | collective-permute-start | bytes 294920 | tf_op jit(solution)/shard_map/ppermute | solution.py:30
  70.8 7.4 %collective-permute-start.21 = (bf16[768,128]{1,0:T(8,128)(2,1)S(1)}, bf16[768,128]{1,0:T(8,128)(2,1)S(1)}, u32[]{:S(2)}, u32[]{:S(2)}) collective-permute-start(bf16[768,128]{1,0:T(8,128)(2,1)S(1)} %shard_map.103.refs_16_), channel_id=1, source_target_pairs={{0,16},{8,24},{16,0},{24,8},{1,17},{9,25},{17,1},{25,9},{2,18},{10... | collective-permute-start | bytes 589832 | tf_op jit(solution)/shard_map/ppermute | solution.py:30
  73.0 7.7 %collective-permute-start.4 = (bf16[2048,128]{1,0:T(8,128)(2,1)S(1)}, bf16[2048,128]{1,0:T(8,128)(2,1)S(1)}, u32[]{:S(2)}, u32[]{:S(2)}) collective-permute-start(bf16[2048,128]{1,0:T(8,128)(2,1)S(1)} %shard_map.96.refs_4_), channel_id=1, source_target_pairs={{0,8},{8,0},{16,24},{24,16},{1,9},{9,1},{17,25},{25,17},{2,10},{10... | collective-permute-start | bytes 1572872 | tf_op jit(solution)/shard_map/ppermute | solution.py:30
  73.0 7.7 %collective-permute-start.6 = (bf16[2048,128]{1,0:T(8,128)(2,1)S(1)}, bf16[2048,128]{1,0:T(8,128)(2,1)S(1)}, u32[]{:S(2)}, u32[]{:S(2)}) collective-permute-start(bf16[2048,128]{1,0:T(8,128)(2,1)S(1)} %collective-permute-done.5.refs_6_), channel_id=1, source_target_pairs={{0,8},{8,0},{16,24},{24,16},{1,9},{9,1},{17,25},{25,17},{2,10},{10... | collective-permute-start | bytes 1572872 | tf_op jit(solution)/shard_map/ppermute | solution.py:30
  73.5 2.3 %collective-permute-start.15 = (bf16[384,128]{1,0:T(8,128)(2,1)S(1)}, bf16[384,128]{1,0:T(8,128)(2,1)S(1)}, u32[]{:S(2)}, u32[]{:S(2)}) collective-permute-start(bf16[384,128]{1,0:T(8,128)(2,1)S(1)} %collective-permute-done.14.refs_14_), channel_id=1, source_target_pairs={{0,8},{8,0},{16,24},{24,16},{1,9},{9,1},{17,25},{25,17},{2,10},{10... | collective-permute-start | bytes 294920 | tf_op jit(solution)/shard_map/ppermute | solution.py:30
  75.8 2.8 %collective-permute-start.20 = (bf16[768,128]{1,0:T(8,128)(2,1)S(1)}, bf16[768,128]{1,0:T(8,128)(2,1)S(1)}, u32[]{:S(2)}, u32[]{:S(2)}) collective-permute-start(bf16[768,128]{1,0:T(8,128)(2,1)S(1)} %shard_map.103.refs_16_), channel_id=1, source_target_pairs={{0,8},{8,0},{16,24},{24,16},{1,9},{9,1},{17,25},{25,17},{2,10},{10... | collective-permute-start | bytes 589832 | tf_op jit(solution)/shard_map/ppermute | solution.py:30
  78.1 2.6 %collective-permute-start.10 = (bf16[1536,128]{1,0:T(8,128)(2,1)S(1)}, bf16[1536,128]{1,0:T(8,128)(2,1)S(1)}, u32[]{:S(2)}, u32[]{:S(2)}) collective-permute-start(bf16[1536,128]{1,0:T(8,128)(2,1)S(1)} %shard_map.99.refs_8_), channel_id=1, source_target_pairs={{0,8},{8,0},{16,24},{24,16},{1,9},{9,1},{17,25},{25,17},{2,10},{10... | collective-permute-start | bytes 1179656 | tf_op jit(solution)/shard_map/ppermute | solution.py:30
  78.1 2.6 %collective-permute-start.12 = (bf16[1536,128]{1,0:T(8,128)(2,1)S(1)}, bf16[1536,128]{1,0:T(8,128)(2,1)S(1)}, u32[]{:S(2)}, u32[]{:S(2)}) collective-permute-start(bf16[1536,128]{1,0:T(8,128)(2,1)S(1)} %collective-permute-done.11.refs_10_), channel_id=1, source_target_pairs={{0,8},{8,0},{16,24},{24,16},{1,9},{9,1},{17,25},{25,17},{2,10},{10... | collective-permute-start | bytes 1179656 | tf_op jit(solution)/shard_map/ppermute | solution.py:30
  78.7 2.0 %collective-permute-start.22 = (bf16[768,128]{1,0:T(8,128)(2,1)S(1)}, bf16[768,128]{1,0:T(8,128)(2,1)S(1)}, u32[]{:S(2)}, u32[]{:S(2)}) collective-permute-start(bf16[768,128]{1,0:T(8,128)(2,1)S(1)} %collective-permute-done.21.refs_18_), channel_id=1, source_target_pairs={{0,8},{8,0},{16,24},{24,16},{1,9},{9,1},{17,25},{25,17},{2,10},{10... | collective-permute-start | bytes 589832 | tf_op jit(solution)/shard_map/ppermute | solution.py:30
